TPU v7x, 32 devices: a whole 2x2x4 slice. The times are simulated.
32 devices in a mesh: replica: 4 (over x, y), ep: 8 (over z, core).
Axes of the slice: x: 2, y: 2, z: 4, core: 2. Of those that a mesh axis runs over, the one named last changes fastest.
Arguments:
- x: bfloat16 [128, 128, 2048], P(('replica', 'ep')), parts along dimension 0
- wq: bfloat16 [2048, 4096], P('ep')
- wk: bfloat16 [2048, 4096], P('ep')
- wv: bfloat16 [2048, 4096], P('ep')
- wo: bfloat16 [4096, 2048], P('ep')
- wr: float32 [2048, 128], replicated
- w1: bfloat16 [128, 2048, 768], P('ep')
- w3: bfloat16 [128, 2048, 768], P('ep')
- w2: bfloat16 [128, 768, 2048], P('ep')
- idx: int32 [128, 128, 8], P(('replica', 'ep')), parts along dimension 0
Outputs:
- output: bfloat16 [128, 128, 2048], P(('replica', 'ep')), parts along dimension 0
There are 4 independent parts. A program takes and returns all parts, laid end to end along the dimension named above; an argument that names none is the same for every part.
All inputs are finite; a program needn't handle non-finite values.
Results may differ from a plain program's by a relative error of at most 0.01184.
Values are sent between devices in bfloat16 or wider.
A program may use at most 1 GiB of HBM per device.

v0:
```python
import math
import jax
import jax.numpy as jnp
from jax import lax
from jax.sharding import PartitionSpec as P

HEAD = 128
BLOCK = 128
EPS = 1e-6
THETA = 10000.0


def rmsnorm(v):
    v = v.astype(jnp.float32)
    return v * lax.rsqrt(jnp.mean(v * v, axis=-1, keepdims=True) + EPS)


def rope(z):
    n = z.shape[-3]
    half = HEAD // 2
    freq = THETA ** (-jnp.arange(half, dtype=jnp.float32) / half)
    ang = jnp.arange(n, dtype=jnp.float32)[:, None] * freq
    c = jnp.cos(ang)[:, None, :]
    s = jnp.sin(ang)[:, None, :]
    z1, z2 = z[..., :half], z[..., half:]
    return jnp.concatenate([z1 * c - z2 * s, z2 * c + z1 * s], axis=-1)


def attention(x, s, wq, wk, wv, wo):
    t, d = x.shape
    nh = wq.shape[1] // HEAD
    a = rmsnorm(x).astype(jnp.bfloat16)

    def proj(w):
        return jnp.dot(a, w, preferred_element_type=jnp.float32).reshape(t // s, s, nh, HEAD)

    q = rope(proj(wq)).astype(jnp.bfloat16)
    k = rope(proj(wk)).astype(jnp.bfloat16)
    v = proj(wv).astype(jnp.bfloat16)
    sc = jnp.einsum('bqhe,bkhe->bhqk', q, k, preferred_element_type=jnp.float32) / math.sqrt(HEAD)
    sc = jnp.where(jnp.tril(jnp.ones((s, s), bool)), sc, -jnp.inf)
    p = jax.nn.softmax(sc, axis=-1).astype(jnp.bfloat16)
    o = jnp.einsum('bhqk,bkhe->bqhe', p, v, preferred_element_type=jnp.float32).astype(jnp.bfloat16)
    ao = jnp.dot(o.reshape(t, nh * HEAD), wo, preferred_element_type=jnp.float32)
    return (x.astype(jnp.float32) + ao).astype(jnp.bfloat16)


def router(h, wr, ids):
    r = rmsnorm(h)
    logits = jnp.dot(r, wr, precision=lax.Precision.HIGHEST, preferred_element_type=jnp.float32)
    g = jax.nn.softmax(jnp.take_along_axis(logits, ids, axis=1), axis=-1)
    return r.astype(jnp.bfloat16), g


def block_plan(eid, ne, cap):
    m = eid.shape[0]
    nb = (cap + ne * (BLOCK - 1)) // BLOCK + 1
    counts = jnp.bincount(eid, length=ne + 1)[:ne]
    nblk = (counts + BLOCK - 1) // BLOCK
    bend = jnp.cumsum(nblk)
    first = jnp.cumsum(counts) - counts
    order = jnp.argsort(eid)
    se = eid[order]
    sc = jnp.minimum(se, ne - 1)
    slot = jnp.where(se < ne, (bend[sc] - nblk[sc]) * BLOCK + jnp.arange(m) - first[sc], nb * BLOCK)
    cand = jnp.full((nb * BLOCK,), m, jnp.int32).at[slot].set(order.astype(jnp.int32), mode='drop')
    blk_e = jnp.minimum(jnp.searchsorted(bend, jnp.arange(nb), side='right'), ne - 1)
    return cand.reshape(nb, BLOCK), blk_e, bend[-1]


def expert_sum(rows, eid, gates, k, w1, w3, w2, cap):
    n, d = rows.shape
    ne = w1.shape[0]
    m = n * k
    cand, blk_e, nused = block_plan(eid, ne, cap)
    ok = cand < m
    row = jnp.where(ok, cand // k, 0)
    gate = jnp.where(ok, gates[jnp.minimum(cand, m - 1)], 0.0)

    def body(acc, xs):
        b, rb, gb, e = xs

        def work(acc):
            xb = rows[rb]
            a1 = jnp.dot(xb, w1[e], preferred_element_type=jnp.float32)
            a3 = jnp.dot(xb, w3[e], preferred_element_type=jnp.float32)
            act = (jax.nn.silu(a1) * a3).astype(jnp.bfloat16)
            o = jnp.dot(act, w2[e], preferred_element_type=jnp.float32).astype(jnp.bfloat16)
            return acc.at[rb].add(gb[:, None] * o.astype(jnp.float32))

        return lax.cond(b < nused, work, lambda acc: acc, acc), None

    acc, _ = lax.scan(body, jnp.zeros((n, d), jnp.float32), (jnp.arange(cand.shape[0]), row, gate, blk_e))
    return acc


def solution(mesh):
    nd = mesh.shape['ep']
    tok = P(('replica', 'ep'), None, None)
    rows_ep = P('ep', None)
    by_expert = P('ep', None, None)

    def a2a(v):
        return lax.all_to_all(v, 'ep', 0, 0, tiled=True)

    def local(x, wq, wk, wv, wo, wr, w1, w3, w2, idx):
        b, s, d = x.shape
        t, k, ne = b * s, idx.shape[-1], w1.shape[0]
        wq, wk, wv, wo = [lax.all_gather(w, 'ep', axis=0, tiled=True) for w in (wq, wk, wv, wo)]
        h = attention(x.reshape(t, d), s, wq, wk, wv, wo)
        ids = idx.reshape(t, k)
        u, g = router(h, wr, ids)
        dev = jnp.arange(nd)
        hit = jnp.any(ids[None] // ne == dev[:, None, None], axis=-1)
        pos = jnp.where(hit, jnp.cumsum(hit, axis=1) - 1, t)
        src = jnp.full((nd, t), t, jnp.int32).at[dev[:, None], pos].set(
            jnp.broadcast_to(jnp.arange(t, dtype=jnp.int32), (nd, t)), mode='drop')
        ok = src < t
        src = jnp.minimum(src, t - 1)
        mine = (ids[src] // ne == dev[:, None, None]) & ok[..., None]
        recv_x = a2a(jnp.where(ok[..., None], u[src], jnp.zeros((), jnp.bfloat16)))
        recv_e = a2a(jnp.where(mine, ids[src] % ne, ne))
        recv_g = a2a(jnp.where(mine, g[src], 0.0))
        n = nd * t
        part = expert_sum(recv_x.reshape(n, d), recv_e.reshape(-1), recv_g.reshape(-1), k,
                          w1, w3, w2, n * min(k, ne))
        back = a2a(part.astype(jnp.bfloat16).reshape(nd, t, d))
        moe = jnp.zeros((t, d), jnp.float32).at[src].add(
            jnp.where(ok[..., None], back.astype(jnp.float32), 0.0))
        return (h.astype(jnp.float32) + moe).astype(jnp.bfloat16).reshape(b, s, d)

    return jax.shard_map(local, mesh=mesh,
                         in_specs=(tok, rows_ep, rows_ep, rows_ep, rows_ep, P(None, None),
                                   by_expert, by_expert, by_expert, tok),
                         out_specs=tok, check_vma=False)
```

profile of v0, /device:TPU:0, one launch (start us, length us, event | category | flops | bytes accessed | tf_op | source)
XLA Modules:
  0.0 8272.0 jit_solution(1861112938916429760)
XLA Ops:
  60.0 226.6 %scatter_custom_fusion.1 = s32[17]{0:T(128)S(1)} fusion(s32[32768]{0:T(1024)S(1)} %reshape.615, s32[32768]{0:T(1024)S(1)} %broadcast.580, s32[]{:T(128)} %copy.145), kind=kCustom, calls=%fused_computation.194 | custom fusion | flops 32768 | bytes 72 | tf_op jit(solution)/shard_map/scatter-add | solution.py:58
  346.7 121.1 %all-gather.5.cloned.1.call-done = bf16[2048,4096]{1,0:T(8,128)(2,1)} async-done(((bf16[256,4096]{1,0:T(8,128)(2,1)}), bf16[2048,4096]{1,0:T(8,128)(2,1)}) %all-gather.5.cloned.1.call-update) | async-done | bytes 16777232 | tf_op jit(solution)/shard_map/all_gather | solution.py:109
  554.6 64.4 all-gather.11.cloned.1.call-done
  639.1 25.8 gather_fusion.6
  722.3 180.5 %gather_fusion.2 = s32[32768]{0:T(1024)S(1)} fusion(s32[32768]{0:T(1024)S(1)} %copy-done.3, s32[32768]{0:T(1024)S(1)} %copy-done.12), kind=kCustom, calls=%fused_computation.2 | custom fusion | bytes 393216 | tf_op jit(solution)/shard_map/gather | solution.py:63
  940.2 120.4 %scatter_custom_fusion.2 = s32[34816]{0:T(1024)S(1)} fusion(s32[32768]{0:T(1024)S(1)} %bitcast.267, s32[32768]{0:T(1024)} %copy-done.17, s32[]{:T(128)} %constant.197.clone.1), kind=kCustom, calls=%fused_computation.137 | custom fusion | bytes 139776 | tf_op jit(solution)/shard_map/scatter | solution.py:66
  1060.7 53.8 while.38
  1116.2 191.8 %gather_fusion.4 = f32[34816]{0:T(1024)S(1)} fusion(f32[32768]{0:T(1024)S(1)} %reshape.445, s32[34816]{0:T(1024)S(1)} %fusion.82), kind=kCustom, calls=%fused_computation.4 | custom fusion | bytes 417792 | tf_op jit(solution)/shard_map/gather | solution.py:78
  1319.3 1807.6 %while.37 = (s32[]{:T(128)}, f32[4096,2048]{1,0:T(8,128)}, s32[272]{0:T(512)S(1)}, s32[]{:T(128)}, s32[272,128]{1,0:T(8,128)S(1)}, /*index=5*/f32[272,128]{1,0:T...) while((s32[]{:T(128)}, f32[4096,2048]{1,0:T(8,128)}, ...), condition=%wide.region_21.22_spmd, body=%wide.region_17.21_spmd.sunk | while | flops 1209599360 | bytes 16524569 | solution.py:93
  1321.1 42.3 conditional.2
  1339.7 23.7 scatter_fusion
  1365.2 42.3 conditional.2
  1383.8 23.7 scatter_fusion
  1409.3 42.3 conditional.2
  1427.8 23.7 scatter_fusion
  1453.3 42.3 conditional.2
  1471.9 23.7 scatter_fusion
  1497.4 42.3 conditional.2
  1541.5 42.3 conditional.2
  1585.5 42.3 conditional.2
  1604.1 23.7 scatter_fusion
  1629.6 42.3 conditional.2
  1673.7 42.3 conditional.2
  1692.2 23.7 scatter_fusion
  1717.7 42.3 conditional.2
  1736.3 23.7 scatter_fusion
  1761.8 42.3 conditional.2
  1780.4 23.7 scatter_fusion
  1805.9 42.3 conditional.2
  1824.4 23.7 scatter_fusion
  1849.9 42.3 conditional.2
  1868.5 23.7 scatter_fusion
  1894.0 42.3 conditional.2
  1912.6 23.7 scatter_fusion
  1938.1 42.3 conditional.2
  1956.6 23.7 scatter_fusion
  1982.1 42.3 conditional.2
  2000.7 23.7 scatter_fusion
  2026.2 42.3 conditional.2
  2070.3 42.3 conditional.2
  2114.3 42.3 conditional.2
  2158.4 42.3 conditional.2
  2202.5 42.3 conditional.2
  2221.0 23.7 scatter_fusion
  2246.5 42.3 conditional.2
  2265.1 23.7 scatter_fusion
  2290.6 42.3 conditional.2
  2309.2 23.7 scatter_fusion
  2334.7 42.3 conditional.2
  2353.2 23.7 scatter_fusion
  2378.7 42.3 conditional.2
  2397.3 23.7 scatter_fusion
  2422.8 42.3 conditional.2
  2441.4 23.7 scatter_fusion
  2466.9 42.3 conditional.2
  2485.4 23.7 scatter_fusion
  2510.9 42.3 conditional.2
  2529.5 23.7 scatter_fusion
  2555.0 42.3 conditional.2
  2599.1 42.3 conditional.2
  2617.7 23.7 scatter_fusion
  2643.1 42.3 conditional.2
  3139.0 5055.1 %all_to_all.20 = bf16[8,512,2048]{2,1,0:T(8,128)(2,1)S(1)} all-to-all(bf16[8,512,2048]{2,1,0:T(8,128)(2,1)S(1)} %bitcast.247), channel_id=1, replica_groups=mesh['replica'=4,'ep'=8] {'ep'}, dimensions={0} | all-to-all | bytes 33554432 | tf_op jit(solution)/shard_map/all_to_all | solution.py:104
  8205.2 56.3 scatter_fusion.1
  (925 shorter events, 1298.2 us)
Async XLA Ops:
  6.5 629.0 %copy-start = (f32[2048,128]{1,0:T(8,128)S(1)}, f32[2048,128]{1,0:T(8,128)}, u32[]{:S(2)}) copy-start(f32[2048,128]{1,0:T(8,128)} %param.21) | copy-start | bytes 3145732
  6.5 4.4 copy-start.25
  6.5 4.5 copy-start.24
  6.5 2.8 copy-start.10
  6.5 294.7 %all-gather.9.cloned.1.call-start = ((), (), s32[]{:S(2)}) async-start(), calls=%async_computation.6 | async-start | bytes 18874368 | tf_op jit(solution)/shard_map/all_gather | solution.py:109
  7.3 317.0 %all-gather.7.cloned.1.call-start = ((), (), s32[]{:S(2)}) async-start(), calls=%async_computation.5 | async-start | bytes 18874368 | tf_op jit(solution)/shard_map/all_gather | solution.py:109
  8.0 459.8 %all-gather.5.cloned.1.call-start = ((), (), s32[]{:S(2)}) async-start(), calls=%async_computation.4 | async-start | bytes 18874368 | tf_op jit(solution)/shard_map/all_gather | solution.py:109
  8.8 610.3 %all-gather.11.cloned.1.call-start = ((), (), s32[]{:S(2)}) async-start(), calls=%async_computation.7 | async-start | bytes 18874368 | tf_op jit(solution)/shard_map/all_gather | solution.py:109
  26.7 0.6 copy-start.15
  26.8 11.9 copy-start.18
  27.3 10.8 copy-start.13
  38.7 9.4 copy-start.8
  39.5 18.8 all-to-all-start
  286.6 0.5 copy-start.26
  289.3 34.9 copy-start.2
  300.5 23.8 copy-start.17
  467.8 22.3 copy-start.6
  490.1 12.6 copy-start.5
  525.1 3.5 copy-start.4
  525.1 3.5 copy-start.7
  639.1 26.2 copy-start.14
  665.3 21.1 copy-start.11
  686.7 11.4 copy-start.9
  686.7 11.4 copy-start.19
  698.8 17.4 all-to-all-start.1
  716.2 5.9 copy-start.23
  716.2 5.9 copy-start.27
  716.2 6.1 copy-start.12
  716.3 6.0 copy-start.3
  716.3 591.8 %all-to-all-start.2 = ((bf16[8,512,2048]{2,1,0:T(8,128)(2,1)}), bf16[8,512,2048]{2,1,0:T(8,128)(2,1)}, u32[]{:S(2)}, u32[]{:S(2)}) async-start(bf16[8,512,2048]{2,1,0:T(8,128)(2,1)} %broadcast_select_fusion), calls=%async_computation.2 | async-start | bytes 33554432 | tf_op jit(solution)/shard_map/all_to_all | solution.py:104
  722.3 338.4 %copy-start.21 = (u32[272]{0:T(512)S(1)}, u32[272]{0:T(512)}, u32[]{:S(2)}) copy-start(u32[272]{0:T(512)} %custom-call.3) | copy-start | bytes 3268
  722.3 338.4 %copy-start.22 = (u32[272]{0:T(512)S(1)}, u32[272]{0:T(512)}, u32[]{:S(2)}) copy-start(u32[272]{0:T(512)} %custom-call.2) | copy-start | bytes 3268
  3139.0 5055.1 %copy-start.20 = (pred[8,512]{1,0:T(8,128)(4,1)S(1)}, pred[8,512]{1,0:T(8,128)(4,1)}, u32[]{:S(2)}) copy-start(pred[8,512]{1,0:T(8,128)(4,1)} %copy-done.18) | copy-start | bytes 12292
  8194.1 11.1 copy-start.16
  8205.2 60.1 copy-start.1
Sparse Core Ops, SparseCore 0:
  8.9 156.6 all-gather.8
  167.3 149.0 all-gather.6
  318.0 149.7 all-gather.4
  469.3 149.7 all-gather.10
where the time goes:
time: 8390 us; the launch traced here: 8270 us
  blocking collectives  5060 us (60%)
  other arithmetic  1170 us (14%)
  local copies, waits for them, and re-layouts  1150 us (14%)
  loops' own time  399 us (5%)
  matrix products  270 us (3%)
  waiting for transfers between devices  198 us (2%)
    all_to_all x1, blocking collectives, a2a(): return lax.all_to_all(v, 'ep', 0, 0, tiled=True)  5060 us
    scatter-add x31, other arithmetic, work(): return acc.at[rb].add(gb[:, None] * o.astype(jnp.float32))  735 us
    another operation x1, loops' own time, expert_sum(): lax.scan(body, jnp.zeros((n, d), jnp.float32), (jnp.arange(cand.shape[0])...  335 us
    gather x31, local copies, waits for them, and re-layouts, work(): xb = rows[rb]  290 us
    scatter-add x1, other arithmetic, block_plan(): counts = jnp.bincount(eid, length=ne + 1)[:ne]  227 us
    gather x1, local copies, waits for them, and re-layouts, expert_sum(): gate = jnp.where(ok, gates[jnp.minimum(cand, m - 1)], 0.0)  192 us
    all_gather x4, waiting for transfers between devices, local(): lax.all_gather(w, 'ep', axis=0, tiled=True)  185 us
    gather x1, local copies, waits for them, and re-layouts, block_plan(): se = eid[order]  181 us
  transfers between devices with their start and end apart: 7, of which 3 were waited for; matrix products, arithmetic and copies ran while one was open for 12% of the time, Pallas kernels for 0%

commit v1 on v0

v1 whole, which is shorter than its diff:
```python
import functools
import math
import jax
import jax.numpy as jnp
from jax import lax
from jax.experimental import pallas as pl
from jax.experimental.pallas import tpu as pltpu
from jax.sharding import PartitionSpec as P

HEAD = 128
EPS = 1e-6
THETA = 10000.0
BM = 128
PITCH = BM + 1
LANES = 128


def rmsnorm(v):
    v = v.astype(jnp.float32)
    return v * lax.rsqrt(jnp.mean(v * v, axis=-1, keepdims=True) + EPS)


def rope(z):
    n = z.shape[-3]
    half = HEAD // 2
    freq = THETA ** (-jnp.arange(half, dtype=jnp.float32) / half)
    ang = jnp.arange(n, dtype=jnp.float32)[:, None] * freq
    c = jnp.cos(ang)[:, None, :]
    s = jnp.sin(ang)[:, None, :]
    z1, z2 = z[..., :half], z[..., half:]
    return jnp.concatenate([z1 * c - z2 * s, z2 * c + z1 * s], axis=-1)


def attention(x, s, wq, wk, wv, wo):
    t, d = x.shape
    nh = wq.shape[1] // HEAD
    a = rmsnorm(x).astype(jnp.bfloat16)

    def proj(w):
        return jnp.dot(a, w, preferred_element_type=jnp.float32).reshape(t // s, s, nh, HEAD)

    q = rope(proj(wq)).astype(jnp.bfloat16)
    k = rope(proj(wk)).astype(jnp.bfloat16)
    v = proj(wv).astype(jnp.bfloat16)
    sc = jnp.einsum('bqhe,bkhe->bhqk', q, k, preferred_element_type=jnp.float32) / math.sqrt(HEAD)
    sc = jnp.where(jnp.tril(jnp.ones((s, s), bool)), sc, -jnp.inf)
    p = jax.nn.softmax(sc, axis=-1).astype(jnp.bfloat16)
    o = jnp.einsum('bhqk,bkhe->bqhe', p, v, preferred_element_type=jnp.float32).astype(jnp.bfloat16)
    ao = jnp.dot(o.reshape(t, nh * HEAD), wo, preferred_element_type=jnp.float32)
    return (x.astype(jnp.float32) + ao).astype(jnp.bfloat16)


def router(h, wr, ids):
    r = rmsnorm(h)
    logits = jnp.dot(r, wr, precision=lax.Precision.HIGHEST, preferred_element_type=jnp.float32)
    pick = ids[:, :, None] == jnp.arange(wr.shape[1], dtype=ids.dtype)
    g = jax.nn.softmax(jnp.sum(jnp.where(pick, logits[:, None, :], 0.0), axis=-1), axis=-1)
    return r.astype(jnp.bfloat16), g


def moe_kernel(nt, kk, nblk_ref, be_ref, bb_ref, bn_ref, key_ref, gate_ref, u_hbm, w1_hbm, w3_hbm, w2_hbm,
               out_hbm, ub, acc, w1, w3, w2, xs, zs, lhs, usem, wsem, osem):
    cols = ub.shape[1]
    gmask = nt * kk - 1
    shift = kk.bit_length() - 1
    nexp = w1_hbm.shape[0]
    nblk = nblk_ref[0]

    def weights(e, slot):
        return (pltpu.make_async_copy(w1_hbm.at[e], w1.at[slot], wsem.at[slot, 0]),
                pltpu.make_async_copy(w3_hbm.at[e], w3.at[slot], wsem.at[slot, 1]),
                pltpu.make_async_copy(w2_hbm.at[e], w2.at[slot], wsem.at[slot, 2]))

    load_u = pltpu.make_async_copy(u_hbm, ub.at[pl.ds(0, nt)], usem)
    load_u.start()
    for c in weights(0, 0):
        c.start()

    def zero(i, _):
        acc[pl.ds(i * 8, 8)] = jnp.zeros((8,) + acc.shape[1:], jnp.float32)
        return 0

    lax.fori_loop(0, acc.shape[0] // 8, zero, 0)
    load_u.wait()

    def gather(b):
        base = bb_ref[b]
        for i in range(BM):
            t = lax.shift_right_logical(key_ref[base + i] & gmask, shift)
            xs[pl.ds(i, cols, stride=PITCH), :] = ub[t].astype(jnp.float32)

    def scatter(base, n, rows):
        new = []
        for i in rows:
            gi = key_ref[base + i] & gmask
            t = jnp.where(i < n, lax.shift_right_logical(gi, shift), nt)
            new.append((t, acc[t] + gate_ref[gi] * zs[pl.ds(i, cols, stride=PITCH), :]))
        for t, v in new:
            acc[t] = v

    gather(0)

    def body(b, e_prev):
        e = be_ref[b]
        slot = e % 2

        @pl.when(e != e_prev)
        def _():
            for c in weights(e, slot):
                c.wait()

            @pl.when(e + 1 < nexp)
            def _():
                for c in weights(e + 1, 1 - slot):
                    c.start()

        for k in range(cols):
            lhs[:, k * LANES:(k + 1) * LANES] = xs[k * PITCH:k * PITCH + BM, :].astype(jnp.bfloat16)
        gather(b + 1)
        bp = jnp.maximum(b - 1, 0)
        base, n = bb_ref[bp], jnp.where(b > 0, bn_ref[bp], 0)
        for i in range(0, BM, 8):
            scatter(base, n, range(i, i + 8))
        x = lhs[...]
        a1 = jnp.dot(x, w1[slot], preferred_element_type=jnp.float32)
        a3 = jnp.dot(x, w3[slot], preferred_element_type=jnp.float32)
        act = (jax.nn.silu(a1) * a3).astype(jnp.bfloat16)
        z = jnp.dot(act, w2[slot], preferred_element_type=jnp.float32).astype(jnp.bfloat16).astype(jnp.float32)
        for k in range(cols):
            zs[k * PITCH:k * PITCH + BM, :] = z[:, k * LANES:(k + 1) * LANES]
        return e

    lax.fori_loop(0, nblk, body, -1)
    base, n = bb_ref[nblk - 1], bn_ref[nblk - 1]
    for i in range(0, BM, 8):
        scatter(base, n, range(i, i + 8))

    def pack(i, _):
        for j in range(8):
            t = i * 8 + j
            ub[t] = acc[t].astype(jnp.bfloat16)
        return 0

    lax.fori_loop(0, nt // 8, pack, 0)
    store = pltpu.make_async_copy(ub.at[pl.ds(0, nt)], out_hbm, osem)
    store.start()
    store.wait()


def moe(nblk, be, bb, bn, keys, gates, u, w1, w3, w2):
    nt, cols, _ = u.shape
    kk = gates.shape[0] // nt
    ne, d, f = w1.shape
    smem = pl.BlockSpec(memory_space=pltpu.SMEM)
    hbm = pl.BlockSpec(memory_space=pl.ANY)
    rows = nt * kk
    return pl.pallas_call(
        functools.partial(moe_kernel, nt, kk),
        out_shape=jax.ShapeDtypeStruct((nt, cols, LANES), jnp.bfloat16),
        in_specs=[smem] * 6 + [hbm] * 4,
        out_specs=hbm,
        scratch_shapes=[
            pltpu.VMEM((nt + 8, cols, LANES), jnp.bfloat16),
            pltpu.VMEM((nt + 8, cols, LANES), jnp.float32),
            pltpu.VMEM((2, d, f), jnp.bfloat16),
            pltpu.VMEM((2, d, f), jnp.bfloat16),
            pltpu.VMEM((2, f, d), jnp.bfloat16),
            pltpu.VMEM((cols * PITCH, LANES), jnp.float32),
            pltpu.VMEM((cols * PITCH, LANES), jnp.float32),
            pltpu.VMEM((BM, d), jnp.bfloat16),
            pltpu.SemaphoreType.DMA,
            pltpu.SemaphoreType.DMA((2, 3)),
            pltpu.SemaphoreType.DMA,
        ],
        compiler_params=pltpu.CompilerParams(vmem_limit_bytes=60 * 1024 * 1024),
        cost_estimate=pl.CostEstimate(flops=6 * 5000 * d * f, bytes_accessed=ne * 3 * d * f * 2, transcendentals=0),
    )(nblk, be, bb, bn, keys, gates, u, w1, w3, w2)


def block_plan(ids, me, ne):
    nt, k = ids.shape
    le = ids - me * ne
    local = (le >= 0) & (le < ne)
    flat = jnp.arange(nt * k, dtype=jnp.int32).reshape(nt, k)
    keys = jnp.sort(jnp.where(local, le * (nt * k) + flat, ne * nt * k).reshape(-1))
    experts = jnp.arange(ne, dtype=jnp.int32)
    counts = jnp.sum((le.reshape(-1)[None, :] == experts[:, None]).astype(jnp.int32), axis=1)
    low = (experts[None, :] < experts[:, None])
    first = jnp.sum(jnp.where(low, counts[None, :], 0), axis=1)
    nb = jnp.maximum((counts + BM - 1) // BM, 1)
    bfirst = jnp.sum(jnp.where(low, nb[None, :], 0), axis=1)
    maxb = nt * k // BM + ne + 2
    b = jnp.arange(maxb, dtype=jnp.int32)
    inside = (b[:, None] >= bfirst[None, :]) & (b[:, None] < (bfirst + nb)[None, :])

    def of(v):
        return jnp.sum(jnp.where(inside, v[None, :], 0), axis=1)

    done = (b - of(bfirst)) * BM
    be, bb = of(experts), of(first) + done
    bn = jnp.clip(of(counts) - done, 0, BM)
    bb = jnp.where(jnp.any(inside, axis=1), bb, 0)
    keys = jnp.concatenate([keys, jnp.zeros((BM,), jnp.int32)])
    return jnp.sum(nb).reshape(1), be, bb, bn, keys


def solution(mesh):
    nd = mesh.shape['ep']
    nr = mesh.shape['replica']
    tok = P(('replica', 'ep'), None, None)
    rows_ep = P('ep', None)
    by_expert = P('ep', None, None)
    halves = 2

    def local(x, wq, wk, wv, wo, wr, w1, w3, w2, idx):
        b, s, d = x.shape
        t, k, ne = b * s, idx.shape[-1], w1.shape[0]
        me = lax.axis_index('ep')
        cols = d // LANES
        x = lax.all_to_all(x, 'replica', 0, 0, tiled=True)
        idx = lax.all_to_all(idx, 'replica', 0, 0, tiled=True)
        ids = idx.reshape(t, k)
        th = t // halves
        ids_all = lax.all_gather(ids.T, 'ep', axis=0, tiled=False)
        plans = []
        for c in range(halves):
            ids_c = ids_all[:, :, c * th:(c + 1) * th].transpose(0, 2, 1).reshape(nd * th, k)
            plans.append(block_plan(ids_c, me, ne))

        wq, wk, wv, wo = [lax.all_gather(w, 'ep', axis=0, tiled=True) for w in (wq, wk, wv, wo)]
        h = attention(x.reshape(t, d), s, wq, wk, wv, wo)
        u, g = router(h, wr, ids)
        u = u.reshape(t, cols, LANES)
        h = h.reshape(t, cols, LANES)
        g_all = lax.all_gather(g.reshape(halves, th * k), 'ep', axis=1, tiled=False)
        ys = []
        for c in range(halves):
            u_all = lax.all_gather(u[c * th:(c + 1) * th], 'ep', axis=0, tiled=True)
            part = moe(*plans[c], g_all[c].reshape(-1), u_all, w1, w3, w2)
            back = lax.all_to_all(part.reshape(nd, th, cols, LANES), 'ep', 0, 0, tiled=True)
            total = h[c * th:(c + 1) * th].astype(jnp.float32) + jnp.sum(back.astype(jnp.float32), axis=0)
            ys.append(total.astype(jnp.bfloat16))
        y = jnp.concatenate(ys, axis=0).reshape(b, s, d)
        return lax.all_to_all(y, 'replica', 0, 0, tiled=True)

    return jax.shard_map(local, mesh=mesh,
                         in_specs=(tok, rows_ep, rows_ep, rows_ep, rows_ep, P(None, None),
                                   by_expert, by_expert, by_expert, tok),
                         out_specs=tok, check_vma=False)
```

time: 8390 us -> 1270 us (0.15); the launches traced: 8270 us -> 1260 us
  blocking collectives: 5060 us -> 59.1 us
  other arithmetic: 1170 us -> 53.4 us
  local copies, waits for them, and re-layouts: 1150 us -> 97.7 us
  waiting for transfers between devices: 198 us -> 708 us
  loops' own time: 399 us -> 0 us
  matrix products: 270 us -> 62.5 us
  Pallas kernels: 0 us -> 197 us
    all_to_all x1, blocking collectives: 5060 us -> 28.9 us  [local(): return lax.all_to_all(y, 'replica', 0, 0, tiled=True)]
    scatter-add x33 -> x0, other arithmetic: 1020 us -> none  [the longest x31 735 us: work(): return acc.at[rb].add(gb[:, None] * o.astype(jnp.float32))]
    gather x53 -> x0, local copies, waits for them, and re-layouts: 739 us -> none  [the longest x31 290 us: work(): xb = rows[rb]]
    another operation x274 -> x0, loops' own time: 399 us -> none  [the longest x1 335 us: expert_sum(): lax.scan(body, jnp.zeros((n, d), jnp.float32), (jnp.arange(cand.shape[0])...]
    all_gather x4, waiting for transfers between devices: 185 us -> 449 us  [local(): lax.all_gather(w, 'ep', axis=0, tiled=True)]
    all_to_all x3 -> x4, waiting for transfers between devices: 9.78 us -> 257 us  [the longest x2 231 us: local(): lax.all_to_all(part.reshape(nd, th, cols, LANES), 'ep', 0, 0, tiled=True)]
    dot_general x62 -> x0, matrix products: 204 us -> none  [the longest x31 127 us: work(): jnp.dot(act, w2[e], preferred_element_type=jnp.float32).astype(jnp.bfloat16)]
    pallas_call x0 -> x2, Pallas kernels: none -> 197 us  [moe(): pl.pallas_call(functools.partial(moe_kernel, nt, kk), out_shape=jax.Shape...]
  transfers between devices with their start and end apart: 7 -> 10, of which waited for: 3 -> 8; matrix products, arithmetic and copies ran while one was open for 12% -> 15% of each run, Pallas kernels for 0% -> 16%
where the time goes in v1:
time: 1270 us; the launch traced here: 1260 us
  waiting for transfers between devices  708 us (56%)
  Pallas kernels  197 us (16%)
  local copies, waits for them, and re-layouts  97.7 us (8%)
  starting transfers between devices  65.3 us (5%)
  matrix products  62.5 us (5%)
  blocking collectives  59.1 us (5%)
  other arithmetic  53.4 us (4%)
  between operations  14.2 us (1%)
    all_gather x4, waiting for transfers between devices, local(): lax.all_gather(w, 'ep', axis=0, tiled=True)  449 us
    all_to_all x2, waiting for transfers between devices, local(): lax.all_to_all(part.reshape(nd, th, cols, LANES), 'ep', 0, 0, tiled=True)  231 us
    pallas_call x2, Pallas kernels, moe(): pl.pallas_call(functools.partial(moe_kernel, nt, kk), out_shape=jax.Shape...  197 us
    dot_general x3, local copies, waits for them, and re-layouts, proj(): jnp.dot(a, w, preferred_element_type=jnp.float32)  65.8 us
    all_to_all x2, starting transfers between devices, local(): lax.all_to_all(part.reshape(nd, th, cols, LANES), 'ep', 0, 0, tiled=True)  47.7 us
    all_to_all x1, blocking collectives, local(): return lax.all_to_all(y, 'replica', 0, 0, tiled=True)  28.9 us
  transfers between devices with their start and end apart: 10, of which 8 were waited for; matrix products, arithmetic and copies ran while one was open for 15% of the time, Pallas kernels for 16%

profile of v1, /device:TPU:0, one launch (start us, length us, event | category | flops | bytes accessed | tf_op | source)
XLA Modules:
  0.0 1257.7 jit_solution(15840197335383171874)
XLA Ops:
  6.5 0.7 all-gather.12.cloned.1.call-update
  7.3 0.7 all-gather.10.cloned.1.call-update
  8.1 0.7 all-gather.8.cloned.1.call-update
  8.8 0.5 all-gather.14.cloned.1.call-update
  9.3 5.2 all-to-all-start
  14.8 24.6 %all-to-all-done = bf16[4,128,2048]{2,1,0:T(8,128)(2,1)S(1)} async-done(((bf16[4,128,2048]{2,1,0:T(8,128)(2,1)}), bf16[4,128,2048]{2,1,0:T(8,128)(2,1)S(1)}, u32[]{:S(2)}, u32[]{:S(2)}) %all-to-all-start) | async-done | bytes 2097184 | tf_op jit(solution)/shard_map/all_to_all | solution.py:220
  39.9 122.9 %all-gather.12.cloned.1.call-done = bf16[2048,4096]{1,0:T(8,128)(2,1)} async-done(((bf16[256,4096]{1,0:T(8,128)(2,1)}), bf16[2048,4096]{1,0:T(8,128)(2,1)}) %all-gather.12.cloned.1.call-update) | async-done | bytes 16777232 | tf_op jit(solution)/shard_map/all_gather | solution.py:230
  162.8 21.9 %copy.38 = bf16[4096,2048]{1,0:T(8,128)(2,1)} copy(bf16[4096,2048]{0,1:T(8,128)(2,1)} %bitcast.72) | data formatting | bytes 33554432 | tf_op jit(solution)/shard_map/dot_general | solution.py:40
  184.7 129.0 %all-gather.10.cloned.1.call-done = bf16[2048,4096]{1,0:T(8,128)(2,1)} async-done(((bf16[256,4096]{1,0:T(8,128)(2,1)}), bf16[2048,4096]{1,0:T(8,128)(2,1)}) %all-gather.10.cloned.1.call-update) | async-done | bytes 16777232 | tf_op jit(solution)/shard_map/all_gather | solution.py:230
  313.7 22.0 %copy.37 = bf16[4096,2048]{1,0:T(8,128)(2,1)} copy(bf16[4096,2048]{0,1:T(8,128)(2,1)} %bitcast.73) | data formatting | bytes 33554432 | tf_op jit(solution)/shard_map/dot_general | solution.py:40
  335.7 128.9 %all-gather.8.cloned.1.call-done = bf16[2048,4096]{1,0:T(8,128)(2,1)} async-done(((bf16[256,4096]{1,0:T(8,128)(2,1)}), bf16[2048,4096]{1,0:T(8,128)(2,1)}) %all-gather.8.cloned.1.call-update) | async-done | bytes 16777232 | tf_op jit(solution)/shard_map/all_gather | solution.py:230
  464.6 21.9 %copy.36 = bf16[4096,2048]{1,0:T(8,128)(2,1)} copy(bf16[4096,2048]{0,1:T(8,128)(2,1)} %bitcast.74) | data formatting | bytes 33554432 | tf_op jit(solution)/shard_map/dot_general | solution.py:40
  486.5 12.7 %fusion.32 = f32[4,128,32,128]{1,3,2,0:T(8,128)S(1)} fusion(bf16[32,128,2048,1]{2,1,0,3:T(8,128)(2,1)} %bitcast.76, bf16[4,128,2048]{2,1,0:T(8,128)(2,1)S(1)} %all-to-all-done, f32[4,128]{1,0:T(4,128)S(1)} %add_rsqrt_fusion.1), kind=kOutput, calls=%fused_computation.56 | convolution fusion | flops 8593080320 | bytes 27265024 | tf_op jit(solution)/shard_map/dot_general | solution.py:40
  499.2 9.1 fusion.34
  508.3 4.6 subtract_convert_fusion
  512.9 4.5 fusion.9
  517.4 2.1 fusion.60
  519.6 1.4 copy-done.2
  521.0 18.0 %convert_bitcast_fusion = bf16[4,128,32,128]{1,3,2,0:T(8,128)(2,1)} fusion(f32[4,32,128]{2,1,0:T(8,128)S(1)} %fusion.60, bf16[32,128,2048,1]{2,1,0,3:T(8,128)(2,1)} %bitcast.75, f32[4,32,128,128]{2,3,1,0:T(8,128)} %copy-done.2, pred[128,128]{0,1:T(8,128)(4,1)S(1)} %iota_compare_fusion.3, bf16[4,128,2048]{2,1,0:T(8,128)(2,1)S(1)} %copy-done.5, ...), kind=kOutput, calls=%fused_computation.25 | convolution fusion | flops 9148841984 | bytes 31541248 | tf_op jit(solution)/shard_map/bhqk,bkhe->bqhe/dot_general | solution.py:48
  538.9 8.0 copy.43
  546.9 68.4 %all-gather.14.cloned.1.call-done = bf16[4096,2048]{1,0:T(8,128)(2,1)} async-done(((bf16[512,2048]{1,0:T(8,128)(2,1)}), bf16[4096,2048]{1,0:T(8,128)(2,1)}) %all-gather.14.cloned.1.call-update) | async-done | bytes 16777232 | tf_op jit(solution)/shard_map/all_gather | solution.py:230
  615.3 14.8 %fusion.4 = (f32[512]{0:T(512)S(1)}, bf16[512,2048]{1,0:T(8,128)(2,1)S(1)}) fusion(bf16[4096,2048]{1,0:T(8,128)(2,1)} %all-gather.14.cloned.1.call-done, bf16[64,8,32,128]{3,2,1,0:T(8,128)(2,1)} %bitcast.80, bf16[4,128,2048]{2,1,0:T(8,128)(2,1)} %copy-done.4), kind=kOutput, calls=%fused_computation.11 | convolution fusion | flops 8596226048 | bytes 25167872 | tf_op jit(solution)/shard_map/dot_general | solution.py:49
  630.6 1.2 slice_bitcast_fusion.1
  631.8 1.2 copy.54
  633.0 12.2 all-to-all-start.1
  645.3 1.1 multiply_add_fusion
  646.4 2.3 reshape.276
  648.7 1.3 all-to-all-done.1
  650.1 15.2 %all-gather = s32[64,512]{1,0:T(8,128)S(1)} all-gather(s32[8,512]{1,0:T(8,128)S(1)} %bitcast.85), channel_id=2, replica_groups=mesh['replica'=4,'ep'=8] {'ep'}, dimensions={0}, use_global_device_ids=true | all-gather | bytes 147456 | tf_op jit(solution)/shard_map/all_gather | solution.py:224
  665.2 1.3 copy.46
  666.6 1.6 sub.117
  668.2 1.3 copy.44
  669.5 1.7 sub.103
  671.7 1.2 fusion.55
  673.0 0.5 add.117
  673.5 1.5 add_select_fusion.1
  675.0 8.6 sort.21
  683.6 0.6 concatenate.19.key_ref
  684.4 0.7 fusion.54
  685.1 1.3 select_reduce_fusion.5
  686.4 0.6 subtract_clamp_fusion.1
  687.0 3.5 fusion.3
  690.5 7.5 select_reduce_fusion
  699.2 2.4 copy.56
  701.6 15.0 %all_gather.33 = f32[2,8,2048]{2,0,1:T(2,128)S(1)} all-gather(f32[2,1,2048]{2,0,1:T(2,128)S(1)} %exponential_divide_fusion), channel_id=1, replica_groups=mesh['replica'=4,'ep'=8] {'ep'}, dimensions={1}, use_global_device_ids=true | all-gather | bytes 147456 | tf_op jit(solution)/shard_map/all_gather | solution.py:235
  716.7 0.7 fusion.59
  717.4 78.6 %shard_map.100 = bf16[2048,16,128]{2,1,0:T(8,128)(2,1)} custom-call(s32[1]{0:T(128)} %bitcast.18.nblk_ref, s32[146]{0:T(256)} %get-tuple-element.14.be_ref, s32[146]{0:T(256)} %get-tuple-element.40.bb_ref, s32[146]{0:T(256)} %get-tuple-element.39.bn_ref, s32[16512]{0:T(1024)} %concatenate.19.key_ref, f32[16384]{0:T(1024)} %bitcast.87, ...), custom_call_target="tpu_custom_call" | custom-call | flops 47185920000 | bytes 150994944 | tf_op jit(solution)/shard_map/pallas_call | solution.py:157
  796.1 42.7 %all-to-all-start.2 = ((bf16[8,256,16,128]{3,2,1,0:T(8,128)(2,1)}), bf16[8,256,16,128]{3,2,1,0:T(8,128)(2,1)}, u32[]{:S(2)}, u32[]{:S(2)}) async-start(bf16[8,256,16,128]{3,2,1,0:T(8,128)(2,1)} %bitcast.78), calls=%async_computation.2 | async-start | bytes 16777216 | tf_op jit(solution)/shard_map/all_to_all | solution.py:240
  839.0 7.8 sort.28
  846.7 0.6 concatenate.20.key_ref
  847.5 0.6 select_reduce_fusion.1
  848.2 0.5 subtract_clamp_fusion
  848.7 118.5 %shard_map.101 = bf16[2048,16,128]{2,1,0:T(8,128)(2,1)} custom-call(s32[1]{0:T(128)} %bitcast.22.nblk_ref, s32[146]{0:T(256)} %get-tuple-element.18.be_ref, s32[146]{0:T(256)} %get-tuple-element.42.bb_ref, s32[146]{0:T(256)} %get-tuple-element.41.bn_ref, s32[16512]{0:T(1024)} %concatenate.20.key_ref, f32[16384]{0:T(1024)} %bitcast.86, ...), custom_call_target="tpu_custom_call" | custom-call | flops 47185920000 | bytes 150994944 | tf_op jit(solution)/shard_map/pallas_call | solution.py:157
  967.2 55.5 %all-to-all-done.2 = bf16[8,256,16,128]{3,2,1,0:T(8,128)(2,1)} async-done(((bf16[8,256,16,128]{3,2,1,0:T(8,128)(2,1)}), bf16[8,256,16,128]{3,2,1,0:T(8,128)(2,1)}, u32[]{:S(2)}, u32[]{:S(2)}) %all-to-all-start.2) | async-done | bytes 8388640 | tf_op jit(solution)/shard_map/all_to_all | solution.py:240
  1022.8 5.0 all-to-all-start.3
  1028.7 1.7 copy.55
  1030.4 4.7 convert_reduce_fusion.1
  1035.1 1.5 fusion.30
  1036.6 175.1 %all-to-all-done.3 = bf16[8,256,16,128]{3,2,1,0:T(8,128)(2,1)} async-done(((bf16[8,256,16,128]{3,2,1,0:T(8,128)(2,1)}), bf16[8,256,16,128]{3,2,1,0:T(8,128)(2,1)}, u32[]{:S(2)}, u32[]{:S(2)}) %all-to-all-start.3) | async-done | bytes 8388640 | tf_op jit(solution)/shard_map/all_to_all | solution.py:240
  1211.6 4.8 convert_reduce_fusion
  1216.9 0.8 copy-done.7
  1217.9 2.3 reshape.280
  1220.2 28.9 %all_to_all.25 = bf16[4,128,2048]{2,1,0:T(8,128)(2,1)S(1)} all-to-all(bf16[4,128,2048]{2,1,0:T(8,128)(2,1)} %reshape.280), channel_id=1, replica_groups=mesh['replica'=4,'ep'=8] {'replica'}, dimensions={0} | all-to-all | bytes 4194304 | tf_op jit(solution)/shard_map/all_to_all | solution.py:244
  1249.1 1.3 copy.66
  (61 shorter events, 5.2 us)
Async XLA Ops:
  6.5 680.5 %copy-start = (f32[2048,128]{1,0:T(8,128)S(1)}, f32[2048,128]{1,0:T(8,128)}, u32[]{:S(2)}) copy-start(f32[2048,128]{1,0:T(8,128)} %param.15) | copy-start | bytes 3145732
  6.5 156.2 %all-gather.12.cloned.1.call-start = ((), (), s32[]{:S(2)}) async-start(), calls=%async_computation.7 | async-start | bytes 18874368 | tf_op jit(solution)/shard_map/all_gather | solution.py:230
  7.3 306.4 %all-gather.10.cloned.1.call-start = ((), (), s32[]{:S(2)}) async-start(), calls=%async_computation.6 | async-start | bytes 18874368 | tf_op jit(solution)/shard_map/all_gather | solution.py:230
  8.0 456.6 %all-gather.8.cloned.1.call-start = ((), (), s32[]{:S(2)}) async-start(), calls=%async_computation.5 | async-start | bytes 18874368 | tf_op jit(solution)/shard_map/all_gather | solution.py:230
  8.7 606.6 %all-gather.14.cloned.1.call-start = ((), (), s32[]{:S(2)}) async-start(), calls=%async_computation.8 | async-start | bytes 18874368 | tf_op jit(solution)/shard_map/all_gather | solution.py:230
  9.3 30.1 %all-to-all-start = ((bf16[4,128,2048]{2,1,0:T(8,128)(2,1)}), bf16[4,128,2048]{2,1,0:T(8,128)(2,1)S(1)}, u32[]{:S(2)}, u32[]{:S(2)}) async-start(bf16[4,128,2048]{2,1,0:T(8,128)(2,1)} %param.10), calls=%async_computation | async-start | bytes 4194304 | tf_op jit(solution)/shard_map/all_to_all | solution.py:220
  14.5 702.9 %all-gather.16.cloned.1.call-start = ((), (), s32[]{:S(2)}) async-start(), calls=%async_computation.9 | async-start | bytes 9437184 | tf_op jit(solution)/shard_map/all_gather | solution.py:238
  39.4 459.8 %copy-start.4 = (bf16[4,128,2048]{2,1,0:T(8,128)(2,1)}, bf16[4,128,2048]{2,1,0:T(8,128)(2,1)S(1)}, u32[]{:S(2)}) copy-start(bf16[4,128,2048]{2,1,0:T(8,128)(2,1)S(1)} %all-to-all-done) | copy-start | bytes 6291460
  486.5 12.7 %copy-start.3 = (bf16[4096,2048]{1,0:T(8,128)(2,1)S(1)}, bf16[4096,2048]{1,0:T(8,128)(2,1)}, u32[]{:S(2)}) copy-start(bf16[4096,2048]{1,0:T(8,128)(2,1)} %copy.37) | copy-start | bytes 50331652
  517.4 3.5 copy-start.2
  517.4 3.5 copy-start.5
  633.0 16.9 %all-to-all-start.1 = ((s32[4,128,8]{1,2,0:T(8,128)}), s32[4,128,8]{1,2,0:T(8,128)S(1)}, u32[]{:S(2)}, u32[]{:S(2)}) async-start(s32[4,128,8]{1,2,0:T(8,128)} %param.19), calls=%async_computation.1 | async-start | bytes 32768 | tf_op jit(solution)/shard_map/all_to_all | solution.py:221
  645.3 203.4 %all-gather.18.cloned.1.call-start = ((), (), s32[]{:S(2)}) async-start(), calls=%async_computation.10 | async-start | bytes 9437184 | tf_op jit(solution)/shard_map/all_gather | solution.py:238
  796.0 42.8 %copy-start.9 = (s32[16]{0:T(128)S(1)}, s32[16]{0:T(128)}, u32[]{:S(2)}) copy-start(s32[16]{0:T(128)} %get-tuple-element.48) | copy-start | bytes 196
  796.1 42.9 %copy-start.8 = (s32[16384]{0:T(1024)S(1)}, s32[16384]{0:T(1024)}, u32[]{:S(2)}) copy-start(s32[16384]{0:T(1024)} %get-tuple-element.36) | copy-start | bytes 196612
  796.1 226.7 %all-to-all-start.2 = ((bf16[8,256,16,128]{3,2,1,0:T(8,128)(2,1)}), bf16[8,256,16,128]{3,2,1,0:T(8,128)(2,1)}, u32[]{:S(2)}, u32[]{:S(2)}) async-start(bf16[8,256,16,128]{3,2,1,0:T(8,128)(2,1)} %bitcast.78), calls=%async_computation.2 | async-start | bytes 16777216 | tf_op jit(solution)/shard_map/all_to_all | solution.py:240
  1022.8 188.8 %all-to-all-start.3 = ((bf16[8,256,16,128]{3,2,1,0:T(8,128)(2,1)}), bf16[8,256,16,128]{3,2,1,0:T(8,128)(2,1)}, u32[]{:S(2)}, u32[]{:S(2)}) async-start(bf16[8,256,16,128]{3,2,1,0:T(8,128)(2,1)} %bitcast.79), calls=%async_computation.3 | async-start | bytes 16777216 | tf_op jit(solution)/shard_map/all_to_all | solution.py:240
  1211.6 4.9 copy-start.6
  1216.5 1.2 copy-start.7
  1217.9 32.6 %copy-start.1 = (f32[2048,128]{1,0:T(8,128)S(1)}, f32[2048,128]{1,0:T(8,128)}, u32[]{:S(2)}) copy-start(f32[2048,128]{1,0:T(8,128)} %param.15) | copy-start | bytes 3145732
Sparse Core Ops, SparseCore 0:
  8.9 153.7 all-gather.11
  164.4 149.2 all-gather.9
  315.3 149.2 all-gather.7
  466.0 149.2 all-gather.13
  633.2 82.0 all-gather.15
  717.5 79.9 all-gather.17

commit v2 on v1

--- a/solution.py
+++ b/solution.py
@@ -20,34 +20,397 @@
     return v * lax.rsqrt(jnp.mean(v * v, axis=-1, keepdims=True) + EPS)
 
 
-def rope(z):
-    n = z.shape[-3]
+STEPS = 8
+MESH_ID = pl.DeviceIdType.MESH
+
+
+def attn_kernel(seq, x_ref, cos_ref, sin_ref, wq_ref, wk_ref, wv_ref, wo_ref, h_ref, gw, go,
+                a_ref, acc, wbuf, obuf, zr, xr, yr, dr, pr, zp, zm, xs, xd, ys, yd, ps, lsem):
+    r, e = lax.axis_index('replica'), lax.axis_index('ep')
+    nz, nq = 4, 4
+    z, c = e // 2, e % 2
+    me_p = e + 1 - 2 * c
+    r_y = r + 1 - 2 * (r % 2)
+    r_x = (r + 2) % 4
+    r_d = (r_y + 2) % 4
+    rows, wide = wq_ref.shape[0], wq_ref.shape[1] // STEPS
+    quarter = rows // nq
+    orows = go.shape[0] // STEPS
+    oquarter = orows // nq
+    tokens, d = x_ref.shape
+
+    barrier = pltpu.get_barrier_semaphore()
+
+    def greet(dev):
+        pl.semaphore_signal(barrier, inc=1, device_id=dev, device_id_type=MESH_ID)
+
+    greet((r_x, e))
+    greet((r_y, e))
+    greet((r, me_p))
+
+    @pl.when(z > 0)
+    def _():
+        greet((r, e - 2))
+
+    @pl.when(z < nz - 1)
+    def _():
+        greet((r, e + 2))
+
+    pl.semaphore_wait(barrier, 3 + (z + 2) // 3 + (nz + 1 - z) // 3)
+
+    def piece(s, src_e, q):
+        return gw.at[s, :, pl.ds(src_e * rows + q * quarter, quarter), :]
+
+    def opiece(s, q):
+        return go.at[pl.ds(s * orows + q * oquarter, oquarter), :]
+
+    def rcopy(src, dst, ssem, rsem, dev):
+        return pltpu.make_async_remote_copy(src_ref=src, dst_ref=dst, send_sem=ssem, recv_sem=rsem,
+                                            device_id=dev, device_id_type=MESH_ID)
+
+    def z_send(w, s, zs, up):
+        dev = (r, e + 2) if up else (r, e - 2)
+        sem = (zp if up else zm).at[w, s, zs]
+        ref = opiece(s, r) if w else piece(s, 2 * zs + c, r)
+        return rcopy(ref, ref, sem, zr.at[w, s, zs], dev)
+
+    def x_send(w, s, zs):
+        ref = opiece(s, r) if w else piece(s, 2 * zs + c, r)
+        return rcopy(ref, ref, xs.at[w, s, zs], xr.at[w, s, zs], (r_x, e))
+
+    def y_send(w, s, zs):
+        ref = opiece(s, r) if w else piece(s, 2 * zs + c, r)
+        return rcopy(ref, ref, ys.at[w, s, zs], yr.at[w, s, zs], (r_y, e))
+
+    def xd_send(w, s, zs):
+        ref = opiece(s, r_y) if w else piece(s, 2 * zs + c, r_y)
+        return rcopy(ref, ref, xd.at[w, s, zs], dr.at[w, s, zs], (r_x, e))
+
+    def yd_send(w, s, zs):
+        ref = opiece(s, r_x) if w else piece(s, 2 * zs + c, r_x)
+        return rcopy(ref, ref, yd.at[w, s, zs], dr.at[w, s, zs], (r_y, e))
+
+    def x_recv(w, s, zs):
+        ref = opiece(s, r_x) if w else piece(s, 2 * zs + c, r_x)
+        return rcopy(ref, ref, xs.at[w, s, zs], xr.at[w, s, zs], (r_x, e))
+
+    def y_recv(w, s, zs):
+        ref = opiece(s, r_y) if w else piece(s, 2 * zs + c, r_y)
+        return rcopy(ref, ref, ys.at[w, s, zs], yr.at[w, s, zs], (r_y, e))
+
+    def p_send(w, s, zs, j):
+        q = (r, r_x, r_y, r_d)[j]
+        ref = opiece(s, q) if w else piece(s, 2 * zs + c, q)
+        return rcopy(ref, ref, ps.at[w, s, zs, j], pr.at[w, s, zs, j], (r, me_p))
+
+    def p_recv(w, s, zs, j):
+        q = (r, r_x, r_y, r_d)[j]
+        ref = opiece(s, q) if w else piece(s, 2 * zs + 1 - c, q)
+        return rcopy(ref, ref, ps.at[w, s, zs, j], pr.at[w, s, zs, j], (r, me_p))
+
+    def own_parts(s):
+        col = pl.ds(s * wide, wide)
+        return [(wq_ref, 0, col), (wk_ref, 1, col), (wv_ref, 2, col)]
+
+    def originate(s):
+        lo = pl.ds(r * quarter, quarter)
+
+        def line(up):
+            dev = (r, e + 2) if up else (r, e - 2)
+            sem = (zp if up else zm)
+            for w_ref, m, col in own_parts(s):
+                rcopy(w_ref.at[lo, col], gw.at[s, m, pl.ds(e * rows + r * quarter, quarter), :],
+                      sem.at[0, s, z], zr.at[0, s, z], dev).start()
+
+            @pl.when(s == e)
+            def _():
+                rcopy(wo_ref.at[pl.ds(r * oquarter, oquarter), :], opiece(s, r), sem.at[1, s, z], zr.at[1, s, z],
+                      dev).start()
+
+        @pl.when(z > 0)
+        def _():
+            line(False)
+
+        @pl.when(z < nz - 1)
+        def _():
+            line(True)
+
+        for w_ref, m, col in own_parts(s):
+            rcopy(w_ref.at[:, col], gw.at[s, m, pl.ds(e * rows, rows), :], ps.at[0, s, z, 0], pr.at[0, s, z, 0],
+                  (r, me_p)).start()
+
+        @pl.when(s == e)
+        def _():
+            rcopy(wo_ref, go.at[pl.ds(s * orows, orows), :], ps.at[1, s, z, 0], pr.at[1, s, z, 0], (r, me_p)).start()
+
+    def for_both(s, zs, fn):
+        fn(0)
+
+        @pl.when(s == 2 * zs + c)
+        def _():
+            fn(1)
+
+    def x_first(s, zs):
+        return (s + zs + s // 2) % 2 == 0
+
+    def each_side(k, fn):
+        @pl.when(z - k - 1 >= 0)
+        def _():
+            fn(z - k - 1, True)
+
+        @pl.when(z + k + 1 < nz)
+        def _():
+            fn(z + k + 1, False)
+
+    def along_z(s, k):
+        def side(zs, up):
+            def one(w):
+                z_send(w, s, zs, up).wait_recv()
+                if up:
+                    @pl.when(z < nz - 1)
+                    def _():
+                        z_send(w, s, zs, True).start()
+                else:
+                    @pl.when(z > 0)
+                    def _():
+                        z_send(w, s, zs, False).start()
+                x_send(w, s, zs).start()
+                y_send(w, s, zs).start()
+                p_send(w, s, zs, 0).start()
+
+            for_both(s, zs, one)
+
+        each_side(k, side)
+
+    def across(s, k):
+        def side(zs, up):
+            def one(w):
+                x_recv(w, s, zs).wait_recv()
+
+                @pl.when(x_first(s, zs))
+                def _():
+                    yd_send(w, s, zs).start()
+
+                p_send(w, s, zs, 1).start()
+                y_recv(w, s, zs).wait_recv()
+
+                @pl.when(jnp.logical_not(x_first(s, zs)))
+                def _():
+                    xd_send(w, s, zs).start()
+
+                p_send(w, s, zs, 2).start()
+
+            for_both(s, zs, one)
+
+        each_side(k, side)
+
+    def diagonal(s, k):
+        def side(zs, up):
+            def one(w):
+                ref = opiece(s, r_d) if w else piece(s, 2 * zs + c, r_d)
+                rcopy(ref, ref, xd.at[w, s, zs], dr.at[w, s, zs], (r_x, e)).wait_recv()
+                p_send(w, s, zs, 3).start()
+
+            for_both(s, zs, one)
+
+        each_side(k, side)
+
+    def load(s, slot, f):
+        return pltpu.make_async_copy(gw.at[s, :, pl.ds(f * rows, rows), :], wbuf.at[slot, :, pl.ds(f * rows, rows), :],
+                                     lsem.at[slot, f])
+
+    def oload(s, slot, own):
+        src = wo_ref if own else go.at[pl.ds(s * orows, orows), :]
+        return pltpu.make_async_copy(src, obuf.at[slot], lsem.at[slot, 2 * nz])
+
+    def collect(s):
+        slot = s % 2
+
+        def side(zs, up):
+            def one(w):
+                for j in range(4):
+                    p_recv(w, s, zs, j).wait_recv()
+
+            one(0)
+
+            @pl.when(s == 2 * zs + 1 - c)
+            def _():
+                one(1)
+
+        for k in range(nz - 1):
+            each_side(k, side)
+        full = gw.at[s, :, pl.ds(me_p * rows, rows), :]
+        rcopy(full, full, ps.at[0, s, z, 0], pr.at[0, s, z, 0], (r, me_p)).wait_recv()
+
+        @pl.when(s == me_p)
+        def _():
+            ofull = go.at[pl.ds(s * orows, orows), :]
+            rcopy(ofull, ofull, ps.at[1, s, z, 0], pr.at[1, s, z, 0], (r, me_p)).wait_recv()
+
+        for f in range(2 * nz):
+            @pl.when(f == e)
+            def _():
+                for w_ref, m, col in own_parts(s):
+                    pltpu.make_async_copy(w_ref.at[:, col], wbuf.at[slot, m, pl.ds(f * rows, rows), :],
+                                          lsem.at[slot, f]).start()
+
+            @pl.when(f != e)
+            def _():
+                load(s, slot, f).start()
+
+        @pl.when(s == e)
+        def _():
+            oload(s, slot, True).start()
+
+        @pl.when(s != e)
+        def _():
+            oload(s, slot, False).start()
+
+    def wait_loads(s):
+        slot = s % 2
+        for f in range(2 * nz):
+            load(s, slot, f).wait()
+        oload(s, slot, False).wait()
+
+    pair = 2 * HEAD
+    npair = wide // pair
+
+    def compute(s, j):
+        slot = s % 2
+        a = a_ref[...]
+        cols = slice(j * pair, (j + 1) * pair)
+        cos, sin = cos_ref[...], sin_ref[...]
+
+        def rot(v):
+            return (v * cos + pltpu.roll(v, HEAD // 2, 1) * sin).astype(jnp.bfloat16)
+
+        q = jnp.dot(a, wbuf[slot, 0, :, cols], preferred_element_type=jnp.float32)
+        k = jnp.dot(a, wbuf[slot, 1, :, cols], preferred_element_type=jnp.float32)
+        v = jnp.dot(a, wbuf[slot, 2, :, cols], preferred_element_type=jnp.float32).astype(jnp.bfloat16)
+        tri = lax.broadcasted_iota(jnp.int32, (seq, seq), 0) >= lax.broadcasted_iota(jnp.int32, (seq, seq), 1)
+        heads = []
+        for hh in range(2):
+            hc = slice(hh * HEAD, (hh + 1) * HEAD)
+            qh, kh, vh = rot(q[:, hc]), rot(k[:, hc]), v[:, hc]
+            outs = []
+            for b in range(tokens // seq):
+                rs = slice(b * seq, (b + 1) * seq)
+                sc = lax.dot_general(qh[rs], kh[rs], (((1,), (1,)), ((), ())), preferred_element_type=jnp.float32)
+                sc = jnp.where(tri, sc * (1.0 / math.sqrt(HEAD)), -jnp.inf)
+                ex = jnp.exp(sc - jnp.max(sc, axis=-1, keepdims=True))
+                p = (ex / jnp.sum(ex, axis=-1, keepdims=True)).astype(jnp.bfloat16)
+                outs.append(jnp.dot(p, vh[rs], preferred_element_type=jnp.float32).astype(jnp.bfloat16))
+            heads.append(jnp.concatenate(outs, axis=0))
+        o = jnp.concatenate(heads, axis=1)
+        acc[...] += jnp.dot(o, obuf[slot, j * pair:(j + 1) * pair, :], preferred_element_type=jnp.float32)
+
+    originate(0)
+    x = x_ref[...].astype(jnp.float32)
+    a_ref[...] = (x * lax.rsqrt(jnp.mean(x * x, axis=-1, keepdims=True) + EPS)).astype(jnp.bfloat16)
+    acc[...] = x
+
+    def within(s, fn):
+        @pl.when((s >= 0) & (s < STEPS))
+        def _():
+            fn()
+
+    def turn(i, _):
+        within(i + 1, lambda: originate(i + 1))
+        within(i - 3, lambda: wait_loads(i - 3))
+        for k in range(nz - 1):
+            within(i, lambda: along_z(i, k))
+            within(i - 1, lambda: across(i - 1, k))
+            within(i - 2, lambda: diagonal(i - 2, k))
+            if k < npair:
+                within(i - 3, lambda: compute(i - 3, k))
+        within(i - 2, lambda: collect(i - 2))
+        return 0
+
+    lax.fori_loop(0, STEPS + 3, turn, 0)
+    h_ref[...] = acc[...].astype(jnp.bfloat16)
+
+    def drain(s, _):
+        def sent(w, zs, up):
+            if up:
+                @pl.when(z < nz - 1)
+                def _():
+                    z_send(w, s, zs, True).wait_send()
+            else:
+                @pl.when(z > 0)
+                def _():
+                    z_send(w, s, zs, False).wait_send()
+            x_send(w, s, zs).wait_send()
+            y_send(w, s, zs).wait_send()
+
+            @pl.when(x_first(s, zs))
+            def _():
+                yd_send(w, s, zs).wait_send()
+
+            @pl.when(jnp.logical_not(x_first(s, zs)))
+            def _():
+                xd_send(w, s, zs).wait_send()
+
+            for j in range(4):
+                p_send(w, s, zs, j).wait_send()
+
+        for k in range(nz - 1):
+            each_side(k, lambda zs, up: for_both(s, zs, lambda w: sent(w, zs, up)))
+
+        def own(w):
+            @pl.when(z > 0)
+            def _():
+                z_send(w, s, z, False).wait_send()
+
+            @pl.when(z < nz - 1)
+            def _():
+                z_send(w, s, z, True).wait_send()
+
+            full = go.at[pl.ds(s * orows, orows), :] if w else gw.at[s, :, pl.ds(e * rows, rows), :]
+            rcopy(full, full, ps.at[w, s, z, 0], pr.at[w, s, z, 0], (r, me_p)).wait_send()
+
+        for_both(s, z, own)
+        return 0
+
+    lax.fori_loop(0, STEPS, drain, 0)
+
+
+def attention(x, seq, wq, wk, wv, wo):
+    t, d = x.shape
+    rows, hd = wq.shape
+    nd = d // rows
+    n = seq
     half = HEAD // 2
     freq = THETA ** (-jnp.arange(half, dtype=jnp.float32) / half)
     ang = jnp.arange(n, dtype=jnp.float32)[:, None] * freq
-    c = jnp.cos(ang)[:, None, :]
-    s = jnp.sin(ang)[:, None, :]
-    z1, z2 = z[..., :half], z[..., half:]
-    return jnp.concatenate([z1 * c - z2 * s, z2 * c + z1 * s], axis=-1)
-
-
-def attention(x, s, wq, wk, wv, wo):
-    t, d = x.shape
-    nh = wq.shape[1] // HEAD
-    a = rmsnorm(x).astype(jnp.bfloat16)
-
-    def proj(w):
-        return jnp.dot(a, w, preferred_element_type=jnp.float32).reshape(t // s, s, nh, HEAD)
-
-    q = rope(proj(wq)).astype(jnp.bfloat16)
-    k = rope(proj(wk)).astype(jnp.bfloat16)
-    v = proj(wv).astype(jnp.bfloat16)
-    sc = jnp.einsum('bqhe,bkhe->bhqk', q, k, preferred_element_type=jnp.float32) / math.sqrt(HEAD)
-    sc = jnp.where(jnp.tril(jnp.ones((s, s), bool)), sc, -jnp.inf)
-    p = jax.nn.softmax(sc, axis=-1).astype(jnp.bfloat16)
-    o = jnp.einsum('bhqk,bkhe->bqhe', p, v, preferred_element_type=jnp.float32).astype(jnp.bfloat16)
-    ao = jnp.dot(o.reshape(t, nh * HEAD), wo, preferred_element_type=jnp.float32)
-    return (x.astype(jnp.float32) + ao).astype(jnp.bfloat16)
+    c, s = jnp.cos(ang), jnp.sin(ang)
+    cos = jnp.tile(jnp.concatenate([c, c], axis=1), (t // n, 1))
+    sin = jnp.tile(jnp.concatenate([-s, s], axis=1), (t // n, 1))
+    vmem = pl.BlockSpec(memory_space=pltpu.VMEM)
+    hbm = pl.BlockSpec(memory_space=pl.ANY)
+    wide = hd // STEPS
+    orows = hd // STEPS
+    dma = pltpu.SemaphoreType.DMA
+    h, _, _ = pl.pallas_call(
+        functools.partial(attn_kernel, seq),
+        out_shape=(jax.ShapeDtypeStruct((t, d), jnp.bfloat16),
+                   jax.ShapeDtypeStruct((STEPS, 3, d, wide), jnp.bfloat16),
+                   jax.ShapeDtypeStruct((hd, d), jnp.bfloat16)),
+        in_specs=[vmem] * 3 + [hbm] * 4,
+        out_specs=(vmem, hbm, hbm),
+        scratch_shapes=[
+            pltpu.VMEM((t, d), jnp.bfloat16),
+            pltpu.VMEM((t, d), jnp.float32),
+            pltpu.VMEM((2, 3, d, wide), jnp.bfloat16),
+            pltpu.VMEM((2, orows, d), jnp.bfloat16),
+            dma((2, STEPS, 4)), dma((2, STEPS, 4)), dma((2, STEPS, 4)), dma((2, STEPS, 4)), dma((2, STEPS, 4, 4)),
+            dma((2, STEPS, 4)), dma((2, STEPS, 4)), dma((2, STEPS, 4)), dma((2, STEPS, 4)), dma((2, STEPS, 4)),
+            dma((2, STEPS, 4)), dma((2, STEPS, 4, 4)),
+            dma((2, nd + 1)),
+        ],
+        compiler_params=pltpu.CompilerParams(collective_id=0, has_side_effects=True, vmem_limit_bytes=58 * 1024 * 1024),
+        cost_estimate=pl.CostEstimate(flops=10 * t * d * hd, bytes_accessed=4 * d * hd * 2, transcendentals=0),
+    )(x, cos, sin, wq, wk, wv, wo)
+    return h
 
 
 def router(h, wr, ids):
@@ -227,7 +590,6 @@
             ids_c = ids_all[:, :, c * th:(c + 1) * th].transpose(0, 2, 1).reshape(nd * th, k)
             plans.append(block_plan(ids_c, me, ne))
 
-        wq, wk, wv, wo = [lax.all_gather(w, 'ep', axis=0, tiled=True) for w in (wq, wk, wv, wo)]
         h = attention(x.reshape(t, d), s, wq, wk, wv, wo)
         u, g = router(h, wr, ids)
         u = u.reshape(t, cols, LANES)

time: 1270 us -> 955 us (0.75)
  waiting for transfers between devices: 708 us -> 265 us
  Pallas kernels: 197 us -> 472 us
  local copies, waits for them, and re-layouts: 97.7 us -> 23.1 us
  matrix products: 62.5 us -> 3.49 us
    all_gather x4 -> x0, waiting for transfers between devices: 449 us -> none  [local(): lax.all_gather(w, 'ep', axis=0, tiled=True)]
    pallas_call x0 -> x1, Pallas kernels: none -> 275 us  [attention(): pl.pallas_call(functools.partial(attn_kernel, seq), out_shape=(jax.ShapeD...]
    dot_general x3 -> x0, local copies, waits for them, and re-layouts: 65.8 us -> none  [proj(): jnp.dot(a, w, preferred_element_type=jnp.float32)]
    dot_general x5 -> x0, matrix products: 59 us -> none  [the longest x2 21.7 us: proj(): jnp.dot(a, w, preferred_element_type=jnp.float32)]
  transfers between devices with their start and end apart: 10 -> 6, of which waited for: 8 -> 5; matrix products, arithmetic and copies ran while one was open for 15% -> 6% of each run, Pallas kernels for 16% -> 21%
where the time goes in v2:
time: 955 us; the launch traced here: 946 us
  Pallas kernels  472 us (49%)
  waiting for transfers between devices  265 us (28%)
  blocking collectives  63.8 us (7%)
  starting transfers between devices  57.5 us (6%)
  other arithmetic  47.5 us (5%)
  local copies, waits for them, and re-layouts  23.1 us (2%)
  between operations  14.1 us (1%)
    pallas_call x1, Pallas kernels, attention(): pl.pallas_call(functools.partial(attn_kernel, seq), out_shape=(jax.ShapeD...  275 us
    all_to_all x2, waiting for transfers between devices, local(): lax.all_to_all(part.reshape(nd, th, cols, LANES), 'ep', 0, 0, tiled=True)  232 us
    pallas_call x2, Pallas kernels, moe(): pl.pallas_call(functools.partial(moe_kernel, nt, kk), out_shape=jax.Shape...  197 us
    all_to_all x2, starting transfers between devices, local(): lax.all_to_all(part.reshape(nd, th, cols, LANES), 'ep', 0, 0, tiled=True)  48.9 us
    all_to_all x1, blocking collectives, local(): return lax.all_to_all(y, 'replica', 0, 0, tiled=True)  29.1 us
    all_to_all x1, waiting for transfers between devices, local(): x = lax.all_to_all(x, 'replica', 0, 0, tiled=True)  24.5 us
  transfers between devices with their start and end apart: 6, of which 5 were waited for; matrix products, arithmetic and copies ran while one was open for 6% of the time, Pallas kernels for 21%

profile of v2, /device:TPU:0, one launch (start us, length us, event | category | flops | bytes accessed | tf_op | source)
XLA Modules:
  0.0 946.3 jit_solution(3720439812799623613)
XLA Ops:
  6.5 5.3 all-to-all-start
  11.9 0.3 fusion.10
  12.3 24.5 %all-to-all-done = bf16[4,128,2048]{2,1,0:T(8,128)(2,1)S(1)} async-done(((bf16[4,128,2048]{2,1,0:T(8,128)(2,1)}), bf16[4,128,2048]{2,1,0:T(8,128)(2,1)S(1)}, u32[]{:S(2)}, u32[]{:S(2)}) %all-to-all-start) | async-done | bytes 2097184 | tf_op jit(solution)/shard_map/all_to_all | solution.py:583
  36.7 0.8 tile.8
  37.5 0.7 tile.20
  38.2 275.2 %shard_map.100 = (bf16[512,2048]{1,0:T(8,128)(2,1)}, bf16[8,3,2048,512]{3,2,1,0:T(8,128)(2,1)}, bf16[4096,2048]{1,0:T(8,128)(2,1)}) custom-call(bf16[512,2048]{1,0:T(8,128)(2,1)} %bitcast.40, f32[512,128]{1,0:T(8,128)} %bitcast.42, f32[512,128]{1,0:T(8,128)} %bitcast.43, bf16[256,4096]{1,0:T(8,128)(2,1)} %wq_ref.1, bf16[256,4096]{1,0:T(8,128)(2,1)} %wk_ref.1, ...), custom_call_target="tpu_custom_call" | custom-call | flops 42949672960 | bytes 67108864 | tf_op jit(solution)/shard_map/pallas_call | solution.py:393
  313.4 2.2 fusion.2
  315.6 0.4 fusion
  316.0 1.2 slice_bitcast_fusion.1
  317.3 1.2 copy.21
  318.5 3.3 all-to-all-start.1
  321.8 1.1 multiply_add_fusion
  322.9 2.2 reshape.204
  325.2 1.3 all-to-all-done.1
  326.5 0.1 copy.18
  326.6 18.8 %all-gather = s32[64,512]{1,0:T(8,128)S(1)} all-gather(s32[8,512]{1,0:T(8,128)S(1)} %bitcast.45), channel_id=2, replica_groups=mesh['replica'=4,'ep'=8] {'ep'}, dimensions={0}, use_global_device_ids=true | all-gather | bytes 147456 | tf_op jit(solution)/shard_map/all_gather | solution.py:587
  345.4 1.3 copy.19
  346.7 1.6 sub.99
  348.4 1.3 copy.17
  349.7 1.7 sub.85
  351.4 0.2 convert_reduce_fusion.2
  351.6 0.2 convert_reduce_fusion.3
  351.8 1.2 fusion.17
  353.1 0.5 add.99
  353.7 1.5 add_select_fusion.1
  355.2 8.6 sort.21
  363.8 0.6 concatenate.17.key_ref
  364.6 0.7 fusion.16
  365.3 1.3 select_reduce_fusion.5
  366.6 0.6 subtract_clamp_fusion.1
  367.2 3.5 fusion.1
  370.7 7.5 select_reduce_fusion
  378.2 0.2 reduce_sum.201
  378.3 0.1 reduce_max.9
  378.5 0.2 exponential_reduce_fusion
  378.8 0.1 div.66
  378.9 0.2 div.67
  379.1 0.1 sub.92
  379.2 0.2 sub.93
  379.4 2.4 copy.23
  381.8 15.9 %all_gather.17 = f32[2,8,2048]{2,0,1:T(2,128)S(1)} all-gather(f32[2,1,2048]{2,0,1:T(2,128)S(1)} %exponential_divide_fusion), channel_id=1, replica_groups=mesh['replica'=4,'ep'=8] {'ep'}, dimensions={1}, use_global_device_ids=true | all-gather | bytes 147456 | tf_op jit(solution)/shard_map/all_gather | solution.py:597
  397.7 0.7 fusion.21
  398.5 7.4 all-gather.4.cloned.1.call-done.u_hbm
  405.9 78.3 %shard_map.101 = bf16[2048,16,128]{2,1,0:T(8,128)(2,1)} custom-call(s32[1]{0:T(128)} %bitcast.7.nblk_ref, s32[146]{0:T(256)} %get-tuple-element.16.be_ref, s32[146]{0:T(256)} %get-tuple-element.36.bb_ref, s32[146]{0:T(256)} %get-tuple-element.35.bn_ref, s32[16512]{0:T(1024)} %concatenate.17.key_ref, f32[16384]{0:T(1024)} %bitcast.47, ...), custom_call_target="tpu_custom_call" | custom-call | flops 47185920000 | bytes 150994944 | tf_op jit(solution)/shard_map/pallas_call | solution.py:520
  484.2 43.9 %all-to-all-start.2 = ((bf16[8,256,16,128]{3,2,1,0:T(8,128)(2,1)}), bf16[8,256,16,128]{3,2,1,0:T(8,128)(2,1)}, u32[]{:S(2)}, u32[]{:S(2)}) async-start(bf16[8,256,16,128]{3,2,1,0:T(8,128)(2,1)} %bitcast.36), calls=%async_computation.2 | async-start | bytes 16777216 | tf_op jit(solution)/shard_map/all_to_all | solution.py:602
  528.3 7.8 sort.28
  536.0 0.6 concatenate.18.key_ref
  536.9 0.6 select_reduce_fusion.1
  537.5 0.5 subtract_clamp_fusion
  538.0 118.5 %shard_map.102 = bf16[2048,16,128]{2,1,0:T(8,128)(2,1)} custom-call(s32[1]{0:T(128)} %bitcast.11.nblk_ref, s32[146]{0:T(256)} %get-tuple-element.20.be_ref, s32[146]{0:T(256)} %get-tuple-element.38.bb_ref, s32[146]{0:T(256)} %get-tuple-element.37.bn_ref, s32[16512]{0:T(1024)} %concatenate.18.key_ref, f32[16384]{0:T(1024)} %bitcast.46, ...), custom_call_target="tpu_custom_call" | custom-call | flops 47185920000 | bytes 150994944 | tf_op jit(solution)/shard_map/pallas_call | solution.py:520
  656.5 55.5 %all-to-all-done.2 = bf16[8,256,16,128]{3,2,1,0:T(8,128)(2,1)} async-done(((bf16[8,256,16,128]{3,2,1,0:T(8,128)(2,1)}), bf16[8,256,16,128]{3,2,1,0:T(8,128)(2,1)}, u32[]{:S(2)}, u32[]{:S(2)}) %all-to-all-start.2) | async-done | bytes 8388640 | tf_op jit(solution)/shard_map/all_to_all | solution.py:602
  712.1 5.0 all-to-all-start.3
  717.1 0.5 convert_bitcast_fusion.1
  717.6 0.4 copy.20
  718.0 1.7 copy.22
  719.7 4.8 convert_reduce_fusion.1
  724.4 0.4 fusion.4
  724.8 176.1 %all-to-all-done.3 = bf16[8,256,16,128]{3,2,1,0:T(8,128)(2,1)} async-done(((bf16[8,256,16,128]{3,2,1,0:T(8,128)(2,1)}), bf16[8,256,16,128]{3,2,1,0:T(8,128)(2,1)}, u32[]{:S(2)}, u32[]{:S(2)}) %all-to-all-start.3) | async-done | bytes 8388640 | tf_op jit(solution)/shard_map/all_to_all | solution.py:602
  900.9 4.8 convert_reduce_fusion
  905.8 0.4 fusion.3
  906.2 0.2 pad_maximum_fusion
  906.4 2.3 reshape.208
  908.7 29.1 %all_to_all.25 = bf16[4,128,2048]{2,1,0:T(8,128)(2,1)S(1)} all-to-all(bf16[4,128,2048]{2,1,0:T(8,128)(2,1)} %reshape.208), channel_id=1, replica_groups=mesh['replica'=4,'ep'=8] {'replica'}, dimensions={0} | all-to-all | bytes 4194304 | tf_op jit(solution)/shard_map/all_to_all | solution.py:606
  937.7 1.3 copy.25
  (34 shorter events, 0.9 us)
Async XLA Ops:
  6.5 360.6 %copy-start = (f32[2048,128]{1,0:T(8,128)S(1)}, f32[2048,128]{1,0:T(8,128)}, u32[]{:S(2)}) copy-start(f32[2048,128]{1,0:T(8,128)} %param.15) | copy-start | bytes 3145732
  6.5 30.2 %all-to-all-start = ((bf16[4,128,2048]{2,1,0:T(8,128)(2,1)}), bf16[4,128,2048]{2,1,0:T(8,128)(2,1)S(1)}, u32[]{:S(2)}, u32[]{:S(2)}) async-start(bf16[4,128,2048]{2,1,0:T(8,128)(2,1)} %param.10), calls=%async_computation | async-start | bytes 4194304 | tf_op jit(solution)/shard_map/all_to_all | solution.py:583
  11.9 394.0 %all-gather.4.cloned.1.call-start = ((), (), s32[]{:S(2)}) async-start(), calls=%async_computation.5 | async-start | bytes 9437184 | tf_op jit(solution)/shard_map/all_gather | solution.py:600
  36.7 1.5 copy-start.4
  313.4 2.2 copy-start.2
  318.5 8.0 all-to-all-start.1
  321.8 216.2 %all-gather.6.cloned.1.call-start = ((), (), s32[]{:S(2)}) async-start(), calls=%async_computation.6 | async-start | bytes 9437184 | tf_op jit(solution)/shard_map/all_gather | solution.py:600
  484.2 43.9 %copy-start.6 = (s32[16]{0:T(128)S(1)}, s32[16]{0:T(128)}, u32[]{:S(2)}) copy-start(s32[16]{0:T(128)} %get-tuple-element.43) | copy-start | bytes 196
  484.2 44.1 %copy-start.5 = (s32[16384]{0:T(1024)S(1)}, s32[16384]{0:T(1024)}, u32[]{:S(2)}) copy-start(s32[16384]{0:T(1024)} %get-tuple-element.34) | copy-start | bytes 196612
  484.2 227.9 %all-to-all-start.2 = ((bf16[8,256,16,128]{3,2,1,0:T(8,128)(2,1)}), bf16[8,256,16,128]{3,2,1,0:T(8,128)(2,1)}, u32[]{:S(2)}, u32[]{:S(2)}) async-start(bf16[8,256,16,128]{3,2,1,0:T(8,128)(2,1)} %bitcast.36), calls=%async_computation.2 | async-start | bytes 16777216 | tf_op jit(solution)/shard_map/all_to_all | solution.py:602
  712.1 188.8 %all-to-all-start.3 = ((bf16[8,256,16,128]{3,2,1,0:T(8,128)(2,1)}), bf16[8,256,16,128]{3,2,1,0:T(8,128)(2,1)}, u32[]{:S(2)}, u32[]{:S(2)}) async-start(bf16[8,256,16,128]{3,2,1,0:T(8,128)(2,1)} %bitcast.37), calls=%async_computation.3 | async-start | bytes 16777216 | tf_op jit(solution)/shard_map/all_to_all | solution.py:602
  900.9 4.9 copy-start.3
  908.7 30.4 %copy-start.1 = (f32[2048,128]{1,0:T(8,128)S(1)}, f32[2048,128]{1,0:T(8,128)}, u32[]{:S(2)}) copy-start(f32[2048,128]{1,0:T(8,128)} %param.15) | copy-start | bytes 3145732
Sparse Core Ops, SparseCore 0:
  318.6 87.2 all-gather.3
  407.5 80.5 all-gather.5

commit v3 on v2

--- a/solution.py
+++ b/solution.py
@@ -15,17 +15,30 @@
 LANES = 128
 
 
+def loop(n, fn):
+    def step(i, carry):
+        fn(i)
+        return carry
+
+    lax.fori_loop(0, n, step, 0)
+
+
+def ep_at(z, c):
+    return 2 * z + c
+
+
 def rmsnorm(v):
     v = v.astype(jnp.float32)
     return v * lax.rsqrt(jnp.mean(v * v, axis=-1, keepdims=True) + EPS)
 
 
+CUT = 48
 STEPS = 8
 MESH_ID = pl.DeviceIdType.MESH
 
 
 def attn_kernel(seq, x_ref, cos_ref, sin_ref, wq_ref, wk_ref, wv_ref, wo_ref, h_ref, gw, go,
-                a_ref, acc, wbuf, obuf, zr, xr, yr, dr, pr, zp, zm, xs, xd, ys, yd, ps, lsem):
+                a_ref, acc, wbuf, obuf, zr, xr, yr, zp, zm, xs, xd, ys, yd, dr, pr, ps, lsem):
     r, e = lax.axis_index('replica'), lax.axis_index('ep')
     nz, nq = 4, 4
     z, c = e // 2, e % 2
@@ -37,7 +50,7 @@
     quarter = rows // nq
     orows = go.shape[0] // STEPS
     oquarter = orows // nq
-    tokens, d = x_ref.shape
+    tokens, _ = x_ref.shape
 
     barrier = pltpu.get_barrier_semaphore()
 
@@ -58,6 +71,11 @@
 
     pl.semaphore_wait(barrier, 3 + (z + 2) // 3 + (nz + 1 - z) // 3)
 
+    per = STEPS // (2 * nz)
+
+    def own_wo(s, lo, n):
+        return wo_ref.at[pl.ds((s % per) * orows + lo, n), :]
+
     def piece(s, src_e, q):
         return gw.at[s, :, pl.ds(src_e * rows + q * quarter, quarter), :]
 
@@ -71,41 +89,50 @@
     def z_send(w, s, zs, up):
         dev = (r, e + 2) if up else (r, e - 2)
         sem = (zp if up else zm).at[w, s, zs]
-        ref = opiece(s, r) if w else piece(s, 2 * zs + c, r)
+        ref = opiece(s, r) if w else piece(s, ep_at(zs, c), r)
         return rcopy(ref, ref, sem, zr.at[w, s, zs], dev)
 
     def x_send(w, s, zs):
-        ref = opiece(s, r) if w else piece(s, 2 * zs + c, r)
+        ref = opiece(s, r) if w else piece(s, ep_at(zs, c), r)
         return rcopy(ref, ref, xs.at[w, s, zs], xr.at[w, s, zs], (r_x, e))
 
     def y_send(w, s, zs):
-        ref = opiece(s, r) if w else piece(s, 2 * zs + c, r)
+        ref = opiece(s, r) if w else piece(s, ep_at(zs, c), r)
         return rcopy(ref, ref, ys.at[w, s, zs], yr.at[w, s, zs], (r_y, e))
 
+    def half(w, s, zs, q, i):
+        if w:
+            return go.at[pl.ds(s * orows + q * oquarter + i * (oquarter // 2), oquarter // 2), :]
+        return gw.at[s, :, pl.ds((ep_at(zs, c)) * rows + q * quarter + i * (quarter // 2), quarter // 2), :]
+
     def xd_send(w, s, zs):
-        ref = opiece(s, r_y) if w else piece(s, 2 * zs + c, r_y)
-        return rcopy(ref, ref, xd.at[w, s, zs], dr.at[w, s, zs], (r_x, e))
+        ref = half(w, s, zs, r_y, 1)
+        return rcopy(ref, ref, xd.at[w, s, zs], dr.at[1, w, s, zs], (r_x, e))
 
     def yd_send(w, s, zs):
-        ref = opiece(s, r_x) if w else piece(s, 2 * zs + c, r_x)
-        return rcopy(ref, ref, yd.at[w, s, zs], dr.at[w, s, zs], (r_y, e))
+        ref = half(w, s, zs, r_x, 0)
+        return rcopy(ref, ref, yd.at[w, s, zs], dr.at[0, w, s, zs], (r_y, e))
+
+    def d_recv(w, s, zs, i):
+        ref = half(w, s, zs, r_d, i)
+        return rcopy(ref, ref, xd.at[w, s, zs], dr.at[i, w, s, zs], (r_x, e))
 
     def x_recv(w, s, zs):
-        ref = opiece(s, r_x) if w else piece(s, 2 * zs + c, r_x)
+        ref = opiece(s, r_x) if w else piece(s, ep_at(zs, c), r_x)
         return rcopy(ref, ref, xs.at[w, s, zs], xr.at[w, s, zs], (r_x, e))
 
     def y_recv(w, s, zs):
-        ref = opiece(s, r_y) if w else piece(s, 2 * zs + c, r_y)
+        ref = opiece(s, r_y) if w else piece(s, ep_at(zs, c), r_y)
         return rcopy(ref, ref, ys.at[w, s, zs], yr.at[w, s, zs], (r_y, e))
 
     def p_send(w, s, zs, j):
         q = (r, r_x, r_y, r_d)[j]
-        ref = opiece(s, q) if w else piece(s, 2 * zs + c, q)
+        ref = opiece(s, q) if w else piece(s, ep_at(zs, c), q)
         return rcopy(ref, ref, ps.at[w, s, zs, j], pr.at[w, s, zs, j], (r, me_p))
 
     def p_recv(w, s, zs, j):
         q = (r, r_x, r_y, r_d)[j]
-        ref = opiece(s, q) if w else piece(s, 2 * zs + 1 - c, q)
+        ref = opiece(s, q) if w else piece(s, ep_at(zs, 1 - c), q)
         return rcopy(ref, ref, ps.at[w, s, zs, j], pr.at[w, s, zs, j], (r, me_p))
 
     def own_parts(s):
@@ -122,9 +149,9 @@
                 rcopy(w_ref.at[lo, col], gw.at[s, m, pl.ds(e * rows + r * quarter, quarter), :],
                       sem.at[0, s, z], zr.at[0, s, z], dev).start()
 
-            @pl.when(s == e)
+            @pl.when(s // per == e)
             def _():
-                rcopy(wo_ref.at[pl.ds(r * oquarter, oquarter), :], opiece(s, r), sem.at[1, s, z], zr.at[1, s, z],
+                rcopy(own_wo(s, r * oquarter, oquarter), opiece(s, r), sem.at[1, s, z], zr.at[1, s, z],
                       dev).start()
 
         @pl.when(z > 0)
@@ -139,19 +166,16 @@
             rcopy(w_ref.at[:, col], gw.at[s, m, pl.ds(e * rows, rows), :], ps.at[0, s, z, 0], pr.at[0, s, z, 0],
                   (r, me_p)).start()
 
-        @pl.when(s == e)
-        def _():
-            rcopy(wo_ref, go.at[pl.ds(s * orows, orows), :], ps.at[1, s, z, 0], pr.at[1, s, z, 0], (r, me_p)).start()
+        @pl.when(s // per == e)
+        def _():
+            rcopy(own_wo(s, 0, orows), go.at[pl.ds(s * orows, orows), :], ps.at[1, s, z, 0], pr.at[1, s, z, 0], (r, me_p)).start()
 
     def for_both(s, zs, fn):
         fn(0)
 
-        @pl.when(s == 2 * zs + c)
+        @pl.when(s // per == ep_at(zs, c))
         def _():
             fn(1)
-
-    def x_first(s, zs):
-        return (s + zs + s // 2) % 2 == 0
 
     def each_side(k, fn):
         @pl.when(z - k - 1 >= 0)
@@ -186,18 +210,10 @@
         def side(zs, up):
             def one(w):
                 x_recv(w, s, zs).wait_recv()
-
-                @pl.when(x_first(s, zs))
-                def _():
-                    yd_send(w, s, zs).start()
-
+                yd_send(w, s, zs).start()
                 p_send(w, s, zs, 1).start()
                 y_recv(w, s, zs).wait_recv()
-
-                @pl.when(jnp.logical_not(x_first(s, zs)))
-                def _():
-                    xd_send(w, s, zs).start()
-
+                xd_send(w, s, zs).start()
                 p_send(w, s, zs, 2).start()
 
             for_both(s, zs, one)
@@ -207,8 +223,8 @@
     def diagonal(s, k):
         def side(zs, up):
             def one(w):
-                ref = opiece(s, r_d) if w else piece(s, 2 * zs + c, r_d)
-                rcopy(ref, ref, xd.at[w, s, zs], dr.at[w, s, zs], (r_x, e)).wait_recv()
+                d_recv(w, s, zs, 0).wait_recv()
+                d_recv(w, s, zs, 1).wait_recv()
                 p_send(w, s, zs, 3).start()
 
             for_both(s, zs, one)
@@ -220,7 +236,7 @@
                                      lsem.at[slot, f])
 
     def oload(s, slot, own):
-        src = wo_ref if own else go.at[pl.ds(s * orows, orows), :]
+        src = own_wo(s, 0, orows) if own else go.at[pl.ds(s * orows, orows), :]
         return pltpu.make_async_copy(src, obuf.at[slot], lsem.at[slot, 2 * nz])
 
     def collect(s):
@@ -233,7 +249,7 @@
 
             one(0)
 
-            @pl.when(s == 2 * zs + 1 - c)
+            @pl.when(s // per == ep_at(zs, 1 - c))
             def _():
                 one(1)
 
@@ -242,7 +258,7 @@
         full = gw.at[s, :, pl.ds(me_p * rows, rows), :]
         rcopy(full, full, ps.at[0, s, z, 0], pr.at[0, s, z, 0], (r, me_p)).wait_recv()
 
-        @pl.when(s == me_p)
+        @pl.when(s // per == me_p)
         def _():
             ofull = go.at[pl.ds(s * orows, orows), :]
             rcopy(ofull, ofull, ps.at[1, s, z, 0], pr.at[1, s, z, 0], (r, me_p)).wait_recv()
@@ -258,11 +274,11 @@
             def _():
                 load(s, slot, f).start()
 
-        @pl.when(s == e)
+        @pl.when(s // per == e)
         def _():
             oload(s, slot, True).start()
 
-        @pl.when(s != e)
+        @pl.when(s // per != e)
         def _():
             oload(s, slot, False).start()
 
@@ -314,7 +330,7 @@
         def _():
             fn()
 
-    def turn(i, _):
+    def turn(i):
         within(i + 1, lambda: originate(i + 1))
         within(i - 3, lambda: wait_loads(i - 3))
         for k in range(nz - 1):
@@ -324,12 +340,11 @@
             if k < npair:
                 within(i - 3, lambda: compute(i - 3, k))
         within(i - 2, lambda: collect(i - 2))
-        return 0
-
-    lax.fori_loop(0, STEPS + 3, turn, 0)
+
+    loop(STEPS + 3, turn)
     h_ref[...] = acc[...].astype(jnp.bfloat16)
 
-    def drain(s, _):
+    def drain(s):
         def sent(w, zs, up):
             if up:
                 @pl.when(z < nz - 1)
@@ -341,14 +356,8 @@
                     z_send(w, s, zs, False).wait_send()
             x_send(w, s, zs).wait_send()
             y_send(w, s, zs).wait_send()
-
-            @pl.when(x_first(s, zs))
-            def _():
-                yd_send(w, s, zs).wait_send()
-
-            @pl.when(jnp.logical_not(x_first(s, zs)))
-            def _():
-                xd_send(w, s, zs).wait_send()
+            yd_send(w, s, zs).wait_send()
+            xd_send(w, s, zs).wait_send()
 
             for j in range(4):
                 p_send(w, s, zs, j).wait_send()
@@ -369,9 +378,8 @@
             rcopy(full, full, ps.at[w, s, z, 0], pr.at[w, s, z, 0], (r, me_p)).wait_send()
 
         for_both(s, z, own)
-        return 0
-
-    lax.fori_loop(0, STEPS, drain, 0)
+
+    loop(STEPS, drain)
 
 
 def attention(x, seq, wq, wk, wv, wo):
@@ -402,9 +410,7 @@
             pltpu.VMEM((t, d), jnp.float32),
             pltpu.VMEM((2, 3, d, wide), jnp.bfloat16),
             pltpu.VMEM((2, orows, d), jnp.bfloat16),
-            dma((2, STEPS, 4)), dma((2, STEPS, 4)), dma((2, STEPS, 4)), dma((2, STEPS, 4)), dma((2, STEPS, 4, 4)),
-            dma((2, STEPS, 4)), dma((2, STEPS, 4)), dma((2, STEPS, 4)), dma((2, STEPS, 4)), dma((2, STEPS, 4)),
-            dma((2, STEPS, 4)), dma((2, STEPS, 4, 4)),
+            *([dma((2, STEPS, 4))] * 9), dma((2, 2, STEPS, 4)), dma((2, STEPS, 4, 4)), dma((2, STEPS, 4, 4)),
             dma((2, nd + 1)),
         ],
         compiler_params=pltpu.CompilerParams(collective_id=0, has_side_effects=True, vmem_limit_bytes=58 * 1024 * 1024),
@@ -421,10 +427,14 @@
     return r.astype(jnp.bfloat16), g
 
 
+def span(n):
+    return 1 << (n - 1).bit_length()
+
+
 def moe_kernel(nt, kk, nblk_ref, be_ref, bb_ref, bn_ref, key_ref, gate_ref, u_hbm, w1_hbm, w3_hbm, w2_hbm,
                out_hbm, ub, acc, w1, w3, w2, xs, zs, lhs, usem, wsem, osem):
     cols = ub.shape[1]
-    gmask = nt * kk - 1
+    gmask = span(nt * kk) - 1
     shift = kk.bit_length() - 1
     nexp = w1_hbm.shape[0]
     nblk = nblk_ref[0]
@@ -434,17 +444,19 @@
                 pltpu.make_async_copy(w3_hbm.at[e], w3.at[slot], wsem.at[slot, 1]),
                 pltpu.make_async_copy(w2_hbm.at[e], w2.at[slot], wsem.at[slot, 2]))
 
-    load_u = pltpu.make_async_copy(u_hbm, ub.at[pl.ds(0, nt)], usem)
-    load_u.start()
+    nd = u_hbm.shape[0]
+    n = nt // nd
+    for dev in range(nd):
+        pltpu.make_async_copy(u_hbm.at[dev, pl.ds(0, n)], ub.at[pl.ds(dev * n, n)], usem).start()
+
     for c in weights(0, 0):
         c.start()
 
-    def zero(i, _):
+    def zero(i):
         acc[pl.ds(i * 8, 8)] = jnp.zeros((8,) + acc.shape[1:], jnp.float32)
-        return 0
-
-    lax.fori_loop(0, acc.shape[0] // 8, zero, 0)
-    load_u.wait()
+
+    loop(acc.shape[0] // 8, zero)
+    pltpu.make_async_copy(ub.at[pl.ds(0, nt)], ub.at[pl.ds(0, nt)], usem).wait()
 
     def gather(b):
         base = bb_ref[b]
@@ -469,13 +481,13 @@
 
         @pl.when(e != e_prev)
         def _():
-            for c in weights(e, slot):
-                c.wait()
-
             @pl.when(e + 1 < nexp)
             def _():
                 for c in weights(e + 1, 1 - slot):
                     c.start()
+
+            for c in weights(e, slot):
+                c.wait()
 
         for k in range(cols):
             lhs[:, k * LANES:(k + 1) * LANES] = xs[k * PITCH:k * PITCH + BM, :].astype(jnp.bfloat16)
@@ -498,25 +510,24 @@
     for i in range(0, BM, 8):
         scatter(base, n, range(i, i + 8))
 
-    def pack(i, _):
+    def pack(i):
         for j in range(8):
             t = i * 8 + j
             ub[t] = acc[t].astype(jnp.bfloat16)
-        return 0
-
-    lax.fori_loop(0, nt // 8, pack, 0)
+
+    loop(nt // 8, pack)
     store = pltpu.make_async_copy(ub.at[pl.ds(0, nt)], out_hbm, osem)
     store.start()
     store.wait()
 
 
-def moe(nblk, be, bb, bn, keys, gates, u, w1, w3, w2):
-    nt, cols, _ = u.shape
+def moe(nblk, be, bb, bn, keys, gates, u, n, w1, w3, w2):
+    nd, _, cols, _ = u.shape
+    nt = nd * n
     kk = gates.shape[0] // nt
     ne, d, f = w1.shape
     smem = pl.BlockSpec(memory_space=pltpu.SMEM)
     hbm = pl.BlockSpec(memory_space=pl.ANY)
-    rows = nt * kk
     return pl.pallas_call(
         functools.partial(moe_kernel, nt, kk),
         out_shape=jax.ShapeDtypeStruct((nt, cols, LANES), jnp.bfloat16),
@@ -540,12 +551,262 @@
     )(nblk, be, bb, bn, keys, gates, u, w1, w3, w2)
 
 
+def back_kernel(cut, piece, part, h_ref, ya, y_out, own, prt, raw, fin, fout, yst, raw_s, raw_r, prt_s, prt_r, f_s, f_r,
+                y_s, y_r, osem, lsem):
+    r, e = lax.axis_index('replica'), lax.axis_index('ep')
+    z, c = e // 2, e % 2
+    me_p = e + 1 - 2 * c
+    n = h_ref.shape[0]
+    np_ = n // piece
+    split = n // 4 // piece
+    mid = (z + 2) // 3 + (5 - z) // 3 - 1
+    is_mid, is_end = mid == 1, mid == 0
+    low = z // 2
+    z_mid = 1 + low
+    z_end = 3 * low
+    z_oth = 2 - low
+    h_a, h_b, h_c = 3 - 3 * low, 2 - low, 3 * low
+    replicas = [(r + i) % 4 for i in range(1, 4)]
+
+    def rows(p):
+        return pl.ds(p * piece, piece)
+
+    def rcopy(src, dst, ssem, rsem, dev):
+        return pltpu.make_async_remote_copy(src_ref=src, dst_ref=dst, send_sem=ssem, recv_sem=rsem, device_id=dev,
+                                            device_id_type=MESH_ID)
+
+    barrier = pltpu.get_barrier_semaphore()
+
+    def greet(dev):
+        pl.semaphore_signal(barrier, inc=1, device_id=dev, device_id_type=MESH_ID)
+
+    for q in replicas:
+        greet((q, e))
+    greet((r, me_p))
+
+    @pl.when(is_end)
+    def _():
+        greet((r, ep_at(z_mid, 0)))
+        greet((r, ep_at(z_mid, 1)))
+
+    @pl.when(is_mid)
+    def _():
+        greet((r, ep_at(z_end, 0)))
+        greet((r, ep_at(z_end, 1)))
+        greet((r, ep_at(z_oth, c)))
+
+    pl.semaphore_wait(barrier, 6 + mid)
+
+    def raw_send(i, c2, p):
+        dest = (3 - i) + low * (2 * i - 3)
+        return rcopy(part.at[ep_at(dest, c2), rows(p)], raw.at[i, c, rows(p)], raw_s.at[i, c2, p], raw_r.at[i, c, p],
+                     (r, ep_at(z_mid, c2)))
+
+    def raw_recv(i, src, p):
+        return rcopy(raw.at[i, src, rows(p)], raw.at[i, src, rows(p)], raw_s.at[i, src, p], raw_r.at[i, src, p],
+                     (r, ep_at(z_end, src)))
+
+    def prt_copy(hh, p):
+        return rcopy(part.at[ep_at(hh, 1 - c), rows(p)], prt.at[hh, rows(p)], prt_s.at[hh, p], prt_r.at[hh, p], (r, me_p))
+
+    def f_copy(i, slot, p, dev):
+        return rcopy(fout.at[i, rows(p)], fin.at[slot, rows(p)], f_s.at[i, p], f_r.at[slot, p], dev)
+
+    def loadown(hh):
+        return pltpu.make_async_copy(part.at[ep_at(hh, c)], own.at[hh], osem.at[hh])
+
+    def place(half):
+        return pl.ds(0, cut) if half < 0 else pl.ds(cut + half * piece, piece)
+
+    def y_copy(src, blk, half):
+        return rcopy(src, y_out.at[r, place(half)], y_s.at[blk, half + 1], y_r.at[r, half + 1], (blk, e))
+
+    def y_local(src, half):
+        return pltpu.make_async_copy(src, y_out.at[r, place(half)], lsem.at[half + 1])
+
+    def put(src, blk, half):
+        @pl.when(r == blk)
+        def _():
+            y_local(src, half).start()
+
+        @pl.when(r != blk)
+        def _():
+            y_copy(src, blk, half).start()
+
+    @pl.when(is_end)
+    def _():
+        loadown(z).start()
+        for i in range(3):
+            def send(p):
+                for c2 in range(2):
+                    raw_send(i, c2, p).start()
+
+            loop(np_, send)
+
+        def pass_on(p):
+            prt_copy(z, p).start()
+
+        loop(np_, pass_on)
+
+    @pl.when(is_mid)
+    def _():
+        for hh in (h_a, h_b, h_c, z):
+            loadown(hh).start()
+        for hh in (h_a, h_b, h_c, z):
+            def pass_on(p):
+                prt_copy(hh, p).start()
+
+            loop(np_, pass_on)
+
+    for blk in range(4):
+        put(ya.at[blk], blk, -1)
+
+    def groups(p, fn):
+        def g(j):
+            fn(pl.ds(p * piece + j * 8, 8))
+
+        loop(piece // 8, g)
+
+    def f32(v):
+        return v.astype(jnp.float32)
+
+    def both(hh, s):
+        return f32(own[hh, s]) + f32(prt[hh, s])
+
+    def onward(i, hh, p, dev_slot, incoming):
+        prt_copy(hh, p).wait_recv()
+
+        def fn(s):
+            fout[i, s] = both(hh, s) + incoming(s)
+
+        groups(p, fn)
+        f_copy(i, dev_slot[1], p, dev_slot[0]).start()
+
+    def finish(p, incoming):
+        prt_copy(z, p).wait_recv()
+
+        def fn(s):
+            yst[s] = (f32(h_ref[s]) + both(z, s) + incoming(s)).astype(jnp.bfloat16)
+
+        groups(p, fn)
+
+        for blk in range(4):
+            for half in range(split):
+                @pl.when(p == blk * split + half)
+                def _():
+                    put(yst.at[rows(p)], blk, half)
+
+    @pl.when(is_mid)
+    def _():
+        loadown(h_a).wait()
+
+        def far(p):
+            raw_recv(0, 0, p).wait_recv()
+            raw_recv(0, 1, p).wait_recv()
+            onward(0, h_a, p, ((r, ep_at(z_oth, c)), 0), lambda s: f32(raw[0, 0, s]) + f32(raw[0, 1, s]))
+
+        loop(np_, far)
+        loadown(h_b).wait()
+        loadown(h_c).wait()
+
+        def near(p):
+            f_copy(2, 0, p, (r, ep_at(z_oth, c))).wait_recv()
+            onward(2, h_c, p, ((r, ep_at(z_end, c)), 0), lambda s: fin[0, s])
+            raw_recv(1, 0, p).wait_recv()
+            raw_recv(1, 1, p).wait_recv()
+            onward(1, h_b, p, ((r, ep_at(z_oth, c)), 1), lambda s: f32(raw[1, 0, s]) + f32(raw[1, 1, s]))
+
+        loop(np_, near)
+        loadown(z).wait()
+
+        def last(p):
+            f_copy(1, 1, p, (r, ep_at(z_oth, c))).wait_recv()
+            raw_recv(2, 0, p).wait_recv()
+            raw_recv(2, 1, p).wait_recv()
+            finish(p, lambda s: fin[1, s] + f32(raw[2, 0, s]) + f32(raw[2, 1, s]))
+
+        loop(np_, last)
+
+    @pl.when(is_end)
+    def _():
+        loadown(z).wait()
+
+        def last(p):
+            f_copy(2, 0, p, (r, ep_at(z_mid, c))).wait_recv()
+            finish(p, lambda s: fin[0, s])
+
+        loop(np_, last)
+
+    @pl.when(is_end)
+    def _():
+        def sent(p):
+            for i in range(3):
+                for c2 in range(2):
+                    raw_send(i, c2, p).wait_send()
+            prt_copy(z, p).wait_send()
+
+        loop(np_, sent)
+
+    @pl.when(is_mid)
+    def _():
+        def sent(p):
+            for hh in (h_a, h_b, h_c, z):
+                prt_copy(hh, p).wait_send()
+            f_copy(0, 0, p, (r, ep_at(z_oth, c))).wait_send()
+            f_copy(1, 1, p, (r, ep_at(z_oth, c))).wait_send()
+            f_copy(2, 0, p, (r, ep_at(z_end, c))).wait_send()
+
+        loop(np_, sent)
+
+    for blk in range(4):
+        for half in range(-1, split):
+            some = ya.at[blk] if half < 0 else yst.at[rows(0)]
+
+            @pl.when(r == blk)
+            def _():
+                y_local(some, half).wait()
+
+            @pl.when(r != blk)
+            def _():
+                y_copy(some, blk, half).wait_send()
+                ref = y_out.at[blk, place(half)]
+                rcopy(ref, ref, y_s.at[blk, half + 1], y_r.at[blk, half + 1], (blk, e)).wait_recv()
+
+
+def back(part, h, ya):
+    _, n, cols, _ = part.shape
+    cut = ya.shape[1]
+    seq = cut + n // 4
+    piece = n // 8
+    vmem = pl.BlockSpec(memory_space=pltpu.VMEM)
+    hbm = pl.BlockSpec(memory_space=pl.ANY)
+    dma = pltpu.SemaphoreType.DMA
+    np_ = n // piece
+
+    def tiles(lead, dtype):
+        return pltpu.VMEM(lead + (cols, LANES), dtype)
+
+    return pl.pallas_call(
+        functools.partial(back_kernel, cut, piece),
+        out_shape=jax.ShapeDtypeStruct((4, seq, cols, LANES), jnp.bfloat16),
+        in_specs=[hbm, vmem, hbm],
+        out_specs=hbm,
+        scratch_shapes=[
+            tiles((4, n), jnp.bfloat16), tiles((4, n), jnp.bfloat16), tiles((3, 2, n), jnp.bfloat16),
+            tiles((2, n), jnp.float32), tiles((3, n), jnp.float32), tiles((n,), jnp.bfloat16),
+            dma((3, 2, np_)), dma((3, 2, np_)), dma((4, np_)), dma((4, np_)), dma((3, np_)), dma((2, np_)),
+            dma((4, 3)), dma((4, 3)), dma((4,)), dma((3,)),
+        ],
+        compiler_params=pltpu.CompilerParams(collective_id=1, has_side_effects=True, vmem_limit_bytes=58 * 1024 * 1024),
+    )(part, h, ya)
+
+
 def block_plan(ids, me, ne):
     nt, k = ids.shape
     le = ids - me * ne
     local = (le >= 0) & (le < ne)
     flat = jnp.arange(nt * k, dtype=jnp.int32).reshape(nt, k)
-    keys = jnp.sort(jnp.where(local, le * (nt * k) + flat, ne * nt * k).reshape(-1))
+    keys = lax.sort(jnp.where(local, le * span(nt * k) + flat, ne * span(nt * k)).reshape(-1), is_stable=False)
     experts = jnp.arange(ne, dtype=jnp.int32)
     counts = jnp.sum((le.reshape(-1)[None, :] == experts[:, None]).astype(jnp.int32), axis=1)
     low = (experts[None, :] < experts[:, None])
@@ -569,11 +830,10 @@
 
 def solution(mesh):
     nd = mesh.shape['ep']
-    nr = mesh.shape['replica']
     tok = P(('replica', 'ep'), None, None)
     rows_ep = P('ep', None)
     by_expert = P('ep', None, None)
-    halves = 2
+    cut = CUT
 
     def local(x, wq, wk, wv, wo, wr, w1, w3, w2, idx):
         b, s, d = x.shape
@@ -583,27 +843,39 @@
         x = lax.all_to_all(x, 'replica', 0, 0, tiled=True)
         idx = lax.all_to_all(idx, 'replica', 0, 0, tiled=True)
         ids = idx.reshape(t, k)
-        th = t // halves
         ids_all = lax.all_gather(ids.T, 'ep', axis=0, tiled=False)
-        plans = []
-        for c in range(halves):
-            ids_c = ids_all[:, :, c * th:(c + 1) * th].transpose(0, 2, 1).reshape(nd * th, k)
-            plans.append(block_plan(ids_c, me, ne))
-
+        x, ids_all = lax.optimization_barrier((x, ids_all))
         h = attention(x.reshape(t, d), s, wq, wk, wv, wo)
         u, g = router(h, wr, ids)
-        u = u.reshape(t, cols, LANES)
-        h = h.reshape(t, cols, LANES)
-        g_all = lax.all_gather(g.reshape(halves, th * k), 'ep', axis=1, tiled=False)
-        ys = []
-        for c in range(halves):
-            u_all = lax.all_gather(u[c * th:(c + 1) * th], 'ep', axis=0, tiled=True)
-            part = moe(*plans[c], g_all[c].reshape(-1), u_all, w1, w3, w2)
-            back = lax.all_to_all(part.reshape(nd, th, cols, LANES), 'ep', 0, 0, tiled=True)
-            total = h[c * th:(c + 1) * th].astype(jnp.float32) + jnp.sum(back.astype(jnp.float32), axis=0)
-            ys.append(total.astype(jnp.bfloat16))
-        y = jnp.concatenate(ys, axis=0).reshape(b, s, d)
-        return lax.all_to_all(y, 'replica', 0, 0, tiled=True)
+        u = u.reshape(b, s, cols, LANES)
+        h = h.reshape(b, s, cols, LANES)
+        g_parts = []
+        for _ in range(3):
+            g_parts.append(lax.reduce_precision(g, 8, 7))
+            g = g - g_parts[-1]
+        gp = jnp.stack(g_parts).astype(jnp.bfloat16).reshape(3, b, s, k)
+
+        def gathered(lo, hi):
+            n = b * (hi - lo)
+            gc = gp[:, :, lo:hi].reshape(3 * n * k // LANES, LANES)
+            gc = jnp.pad(gc, ((0, -gc.shape[0] % cols), (0, 0))).reshape(-1, cols, LANES)
+            both = lax.all_gather(jnp.concatenate([u[:, lo:hi].reshape(n, cols, LANES), gc]), 'ep', axis=0, tiled=False)
+            gall = both[:, n:].reshape(nd, -1)[:, :3 * n * k].reshape(nd, 3, n * k).astype(jnp.float32)
+            return both, gall[:, 0] + gall[:, 1] + gall[:, 2]
+
+        def experts(lo, hi):
+            n = b * (hi - lo)
+            ids_c = ids_all.reshape(nd, k, b, s)[..., lo:hi].transpose(0, 2, 3, 1).reshape(nd * n, k)
+            plan = block_plan(ids_c, me, ne)
+            u_all, gates = gathered(lo, hi)
+            return moe(*plan, gates.reshape(-1), u_all, n, w1, w3, w2).reshape(nd, n, cols, LANES)
+
+        part_a = experts(0, cut)
+        part_a = lax.all_to_all(part_a, 'ep', 0, 0, tiled=True)
+        part_b = experts(cut, s)
+        ya = h[:, :cut].astype(jnp.float32) + jnp.sum(part_a.astype(jnp.float32), axis=0).reshape(b, cut, cols, LANES)
+        y = back(part_b, h[:, cut:].reshape(-1, cols, LANES), ya.astype(jnp.bfloat16))
+        return y.reshape(b, s, d)
 
     return jax.shard_map(local, mesh=mesh,
                          in_specs=(tok, rows_ep, rows_ep, rows_ep, rows_ep, P(None, None),

time: 955 us -> 855 us (0.90)
  waiting for transfers between devices: 265 us -> 83.2 us
  Pallas kernels: 472 us -> 618 us
  blocking collectives: 63.8 us -> 24.3 us
  starting transfers between devices: 57.5 us -> 18.1 us
    all_to_all x3 -> x1, waiting for transfers between devices: 233 us -> 26.7 us  [local(): part_a = lax.all_to_all(part_a, 'ep', 0, 0, tiled=True)]
    pallas_call x0 -> x1, Pallas kernels: none -> 175 us  [back(): pl.pallas_call(functools.partial(back_kernel, cut, piece), out_shape=jax....]
    all_gather x2, waiting for transfers between devices: 7.41 us -> 48.3 us  [gathered(): lax.all_gather(jnp.concatenate([u[:, lo:hi].reshape(n, cols, LANES), gc])...]
    all_to_all x3 -> x1, starting transfers between devices: 52.1 us -> 14.2 us  [local(): part_a = lax.all_to_all(part_a, 'ep', 0, 0, tiled=True)]
    pallas_call x2, Pallas kernels: 197 us -> 171 us  [moe(): pl.pallas_call(functools.partial(moe_kernel, nt, kk), out_shape=jax.Shape...]
    all_to_all x1, blocking collectives: 29.1 us -> 10 us  [local(): idx = lax.all_to_all(idx, 'replica', 0, 0, tiled=True)]
    all_to_all x1, waiting for transfers between devices: 24.5 us -> 8.21 us  [local(): x = lax.all_to_all(x, 'replica', 0, 0, tiled=True)]
    all_gather x1 -> x0, blocking collectives: 15.9 us -> none  [local(): g_all = lax.all_gather(g.reshape(halves, th * k), 'ep', axis=1, tiled=False)]
  transfers between devices with their start and end apart: 6 -> 4, of which waited for: 5 -> 3; matrix products, arithmetic and copies ran while one was open for 6% -> 6% of each run, Pallas kernels for 21% -> 20%
where the time goes in v3:
time: 855 us; the launch traced here: 838 us
  Pallas kernels  618 us (72%)
  waiting for transfers between devices  83.2 us (10%)
  other arithmetic  46.1 us (5%)
  local copies, waits for them, and re-layouts  31.1 us (4%)
  blocking collectives  24.3 us (3%)
  starting transfers between devices  18.1 us (2%)
  between operations  13.9 us (2%)
    pallas_call x1, Pallas kernels, attention(): pl.pallas_call(functools.partial(attn_kernel, seq), out_shape=(jax.ShapeD...  272 us
    pallas_call x1, Pallas kernels, back(): pl.pallas_call(functools.partial(back_kernel, cut, piece), out_shape=jax....  175 us
    pallas_call x2, Pallas kernels, moe(): pl.pallas_call(functools.partial(moe_kernel, nt, kk), out_shape=jax.Shape...  171 us
    all_gather x2, waiting for transfers between devices, gathered(): lax.all_gather(jnp.concatenate([u[:, lo:hi].reshape(n, cols, LANES), gc])...  48.3 us
    all_to_all x1, waiting for transfers between devices, local(): part_a = lax.all_to_all(part_a, 'ep', 0, 0, tiled=True)  26.7 us
  transfers between devices with their start and end apart: 4, of which 3 were waited for; matrix products, arithmetic and copies ran while one was open for 6% of the time, Pallas kernels for 20%

profile of v3, /device:TPU:0, one launch (start us, length us, event | category | flops | bytes accessed | tf_op | source)
XLA Modules:
  0.0 838.3 jit_solution(14293575000065145050)
XLA Ops:
  6.5 10.0 %all_to_all.15 = s32[4,128,8]{1,2,0:T(8,128)S(1)} all-to-all(s32[4,128,8]{1,2,0:T(8,128)} %param.19), channel_id=1, replica_groups=mesh['replica'=4,'ep'=8] {'replica'}, dimensions={0} | all-to-all | bytes 32768 | tf_op jit(solution)/shard_map/all_to_all | solution.py:844
  16.6 3.6 all-to-all-start
  20.3 0.3 fusion.7
  20.5 0.8 pad_maximum_fusion.2
  21.3 0.1 copy.25
  21.4 14.3 %all-gather = s32[64,512]{1,0:T(8,128)S(1)} all-gather(s32[8,512]{1,0:T(8,128)S(1)} %bitcast.100), channel_id=2, replica_groups=mesh['replica'=4,'ep'=8] {'ep'}, dimensions={0}, use_global_device_ids=true | all-gather | bytes 147456 | tf_op jit(solution)/shard_map/all_gather | solution.py:846
  35.7 8.2 all-to-all-done
  43.9 1.6 tile.8
  45.5 1.6 tile.20
  47.1 272.0 %shard_map.100 = (bf16[512,2048]{1,0:T(8,128)(2,1)}, bf16[8,3,2048,512]{3,2,1,0:T(8,128)(2,1)}, bf16[4096,2048]{1,0:T(8,128)(2,1)}) custom-call(bf16[512,2048]{1,0:T(8,128)(2,1)} %bitcast.87, f32[512,128]{1,0:T(8,128)} %bitcast.96, f32[512,128]{1,0:T(8,128)} %bitcast.97, bf16[256,4096]{1,0:T(8,128)(2,1)} %wq_ref.1, bf16[256,4096]{1,0:T(8,128)(2,1)} %wk_ref.1, ...), custom_call_target="tpu_custom_call" | custom-call | flops 42949672960 | bytes 67108864 | tf_op jit(solution)/shard_map/pallas_call | solution.py:401
  319.1 2.2 fusion.2
  321.4 1.8 fusion.3
  323.2 3.5 fusion
  326.6 7.3 select_reduce_fusion
  334.1 0.2 reduce_max.9
  334.2 0.2 exponential_reduce_fusion
  334.5 0.1 copy.29
  334.6 0.2 reshape.342
  334.8 2.2 copy.32
  337.0 1.3 copy-done.3
  338.3 0.1 slice.83
  338.5 1.0 pad_maximum_fusion.1
  339.5 0.2 all-gather.6.cloned.1.call-start
  339.8 2.6 slice.73
  342.4 0.2 copy.27
  342.5 0.3 reshape.330
  342.8 2.5 pad_maximum_fusion
  345.4 0.4 reshape.340
  345.9 1.5 copy.30
  347.4 2.5 subtract_bitcast_fusion
  349.9 1.9 sub.123
  351.7 0.3 copy.31
  352.0 0.9 subtract_bitcast_fusion.1
  353.0 1.5 sub.139
  354.5 0.2 convert_reduce_fusion.2
  354.7 0.3 convert_reduce_fusion.1
  355.0 0.7 fusion.18
  355.7 0.1 select_reduce_fusion.10
  355.8 6.3 sort.15
  362.1 0.6 concatenate.24.key_ref
  362.8 0.1 select_reduce_fusion.8
  363.0 0.6 select_reduce_fusion.5
  363.5 0.6 subtract_clamp_fusion.1
  364.1 48.3 %all-gather.8.cloned.1.call-done = bf16[1560,16,128]{2,1,0:T(8,128)(2,1)} async-done(((bf16[195,16,128]{2,1,0:T(8,128)(2,1)}), bf16[1560,16,128]{2,1,0:T(8,128)(2,1)}) %all-gather.8.cloned.1.call-update) | async-done | bytes 6389776 | tf_op jit(solution)/shard_map/all_gather | solution.py:862
  412.5 0.9 slice.85
  413.5 0.6 add.139.gate_ref
  414.1 77.3 %shard_map.102 = bf16[1536,16,128]{2,1,0:T(8,128)(2,1)} custom-call(s32[1]{0:T(128)} %bitcast.20.nblk_ref, s32[114]{0:T(128)} %get-tuple-element.14.be_ref, s32[114]{0:T(128)} %get-tuple-element.29.bb_ref, s32[114]{0:T(128)} %get-tuple-element.28.bn_ref, s32[12416]{0:T(1024)} %concatenate.24.key_ref, f32[12288]{0:T(1024)} %add.139.gate_ref, ...), custom_call_target="tpu_custom_call" | custom-call | flops 47185920000 | bytes 150994944 | tf_op jit(solution)/shard_map/pallas_call | solution.py:531
  491.4 14.2 %all-to-all-start.2 = ((bf16[8,192,16,128]{3,2,1,0:T(8,128)(2,1)}), bf16[8,192,16,128]{3,2,1,0:T(8,128)(2,1)}, u32[]{:S(2)}, u32[]{:S(2)}) async-start(bf16[8,192,16,128]{3,2,1,0:T(8,128)(2,1)} %bitcast.82), calls=%async_computation.2 | async-start | bytes 12582912 | tf_op jit(solution)/shard_map/all_to_all | solution.py:874
  505.6 1.2 multiply_add_fusion
  506.8 1.9 reshape.326
  508.7 2.0 copy.34
  510.8 8.5 %sort.14 = s32[20480]{0:T(1024)S(1)} sort(s32[20480]{0:T(1024)S(1)} %add_select_fusion), dimensions={0}, to_apply=%region_9.10 | sort | flops 307200 | bytes 163840 | tf_op jit(solution)/shard_map/sort | solution.py:809
  519.3 0.6 concatenate.20.key_ref
  520.0 2.6 slice.80
  522.8 0.7 select_reduce_fusion.1
  523.5 0.5 subtract_clamp_fusion
  524.0 0.9 slice.75
  525.1 0.6 add.133.gate_ref
  525.7 93.9 %shard_map.101 = bf16[2560,16,128]{2,1,0:T(8,128)(2,1)} custom-call(s32[1]{0:T(128)} %bitcast.5.nblk_ref, s32[178]{0:T(256)} %get-tuple-element.18.be_ref, s32[178]{0:T(256)} %get-tuple-element.27.bb_ref, s32[178]{0:T(256)} %get-tuple-element.26.bn_ref, s32[20608]{0:T(1024)} %concatenate.20.key_ref, f32[20480]{0:T(1024)} %add.133.gate_ref, ...), custom_call_target="tpu_custom_call" | custom-call | flops 47185920000 | bytes 150994944 | tf_op jit(solution)/shard_map/pallas_call | solution.py:531
  619.6 26.7 %all-to-all-done.2 = bf16[8,192,16,128]{3,2,1,0:T(8,128)(2,1)} async-done(((bf16[8,192,16,128]{3,2,1,0:T(8,128)(2,1)}), bf16[8,192,16,128]{3,2,1,0:T(8,128)(2,1)}, u32[]{:S(2)}, u32[]{:S(2)}) %all-to-all-start.2) | async-done | bytes 6291488 | tf_op jit(solution)/shard_map/all_to_all | solution.py:874
  646.3 3.8 convert_reduce_fusion
  650.1 2.2 add_convert_fusion.ya
  652.3 174.8 %shard_map.103 = bf16[4,128,16,128]{3,2,1,0:T(8,128)(2,1)} custom-call(bf16[8,320,16,128]{3,2,1,0:T(8,128)(2,1)} %bitcast.77, bf16[320,16,128]{2,1,0:T(8,128)(2,1)} %bitcast.84, bf16[4,48,16,128]{3,2,1,0:T(8,128)(2,1)} %add_convert_fusion.ya), custom_call_target="tpu_custom_call" | custom-call | tf_op jit(solution)/shard_map/pallas_call | solution.py:789
  827.1 4.2 reshape.347
  (39 shorter events, 1.1 us)
Async XLA Ops:
  6.5 316.6 %copy-start = (f32[2048,128]{1,0:T(8,128)S(1)}, f32[2048,128]{1,0:T(8,128)}, u32[]{:S(2)}) copy-start(f32[2048,128]{1,0:T(8,128)} %param.15) | copy-start | bytes 3145732
  16.6 27.3 %all-to-all-start = ((bf16[4,128,2048]{2,1,0:T(8,128)(2,1)}), bf16[4,128,2048]{2,1,0:T(8,128)(2,1)S(1)}, u32[]{:S(2)}, u32[]{:S(2)}) async-start(bf16[4,128,2048]{2,1,0:T(8,128)(2,1)} %param.10), calls=%async_computation | async-start | bytes 4194304 | tf_op jit(solution)/shard_map/all_to_all | solution.py:843
  20.2 392.3 %all-gather.8.cloned.1.call-start = ((), (), s32[]{:S(2)}) async-start(), calls=%async_computation.4 | async-start | bytes 7188480 | tf_op jit(solution)/shard_map/all_gather | solution.py:862
  43.9 3.2 copy-start.4
  319.1 2.2 copy-start.2
  337.0 1.3 copy-start.3
  339.5 184.5 %all-gather.6.cloned.1.call-start = ((), (), s32[]{:S(2)}) async-start(), calls=%async_computation.3 | async-start | bytes 11943936 | tf_op jit(solution)/shard_map/all_gather | solution.py:862
  491.4 154.9 %all-to-all-start.2 = ((bf16[8,192,16,128]{3,2,1,0:T(8,128)(2,1)}), bf16[8,192,16,128]{3,2,1,0:T(8,128)(2,1)}, u32[]{:S(2)}, u32[]{:S(2)}) async-start(bf16[8,192,16,128]{3,2,1,0:T(8,128)(2,1)} %bitcast.82), calls=%async_computation.2 | async-start | bytes 12582912 | tf_op jit(solution)/shard_map/all_to_all | solution.py:874
  652.3 179.0 %copy-start.1 = (f32[2048,128]{1,0:T(8,128)S(1)}, f32[2048,128]{1,0:T(8,128)}, u32[]{:S(2)}) copy-start(f32[2048,128]{1,0:T(8,128)} %param.15) | copy-start | bytes 3145732
Sparse Core Ops, SparseCore 0:
  339.6 72.8 all-gather.7
  414.1 102.0 all-gather.5

commit v4 on v3

v4 whole, which is shorter than its diff:
```python
import functools
import jax
import jax.numpy as jnp
from jax import lax
from jax.experimental import pallas as pl
from jax.experimental.pallas import tpu as pltpu
from jax.sharding import PartitionSpec as P

HEAD = 128
EPS = 1e-6
THETA = 10000.0
BM = 128
PITCH = BM + 1
LANES = 128
CUT = 48
STEPS = 8
SLOT_BITS, TOKEN_BITS = 15, 12


def loop(n, fn):
    def step(i, carry):
        fn(i)
        return carry

    lax.fori_loop(0, n, step, 0)


def ep_at(z, c):
    return 2 * z + c


MESH_ID = pl.DeviceIdType.MESH


def rcopy(src, dst, ssem, rsem, dev):
    return pltpu.make_async_remote_copy(src_ref=src, dst_ref=dst, send_sem=ssem, recv_sem=rsem, device_id=dev,
                                        device_id_type=MESH_ID)


def meet(peers, count):
    barrier = pltpu.get_barrier_semaphore()
    for guard, dev in peers:
        def greet():
            pl.semaphore_signal(barrier, device_id=dev, device_id_type=MESH_ID)

        if guard is None:
            greet()
        else:
            pl.when(guard)(greet)
    pl.semaphore_wait(barrier, count)


def attn_kernel(cut, x_hbm, idt_hbm, cos_ref, sin_ref, wr_ref, wq_ref, wk_ref, wv_ref, wo_ref,
                ua_ref, ub_ref, ha_ref, hb_ref, ids_out, gw, go,
                xg, a_ref, acc, wbuf, obuf, tm, gates, idv, zr, zp, zm, xr, yr, xs, ys, xd, yd, dr, pr, ps,
                x_s, x_r, i_s, i_r, j_s, j_r, lsem, csem):
    r, e = lax.axis_index('replica'), lax.axis_index('ep')
    nz, nq = 4, 4
    z, c = e // 2, e % 2
    e_p = ep_at(z, 1 - c)
    r_x, r_y = (r + 2) % nq, r + 1 - 2 * (r % 2)
    r_d = (r_y + 2) % nq
    nd = ids_out.shape[0]
    rows, wide = wq_ref.shape[0], wq_ref.shape[1] // STEPS
    quarter = rows // nq
    orows = go.shape[0] // STEPS
    nseq, seq, d = x_hbm.shape
    partner, x_dev, y_dev = (r, e_p), (r_x, e), (r_y, e)
    per = STEPS // nd

    def mod(v, m):
        return lax.rem(v, m)

    others = [mod(r + i, nq) for i in range(1, nq)]
    mates = [mod(e + i, nd) for i in range(1, nd)]
    meet([(None, (q, e)) for q in others] + [(None, (r, f)) for f in mates], len(others) + len(mates))

    for i, q in enumerate(others):
        rcopy(idt_hbm.at[q], ids_out.at[e, r], i_s.at[i], i_r.at[r], (q, e)).start()
        rcopy(x_hbm.at[q], xg.at[r], x_s.at[i], x_r.at[r], (q, e)).start()
    keep_ids = pltpu.make_async_copy(idt_hbm.at[r], ids_out.at[e, r], csem.at[0])
    keep_x = pltpu.make_async_copy(x_hbm.at[r], xg.at[r], csem.at[1])
    keep_ids.start()
    keep_x.start()

    def spread_ids():
        keep_ids.wait()
        for i, q in enumerate(others):
            rcopy(idt_hbm.at[q], ids_out.at[e, q], i_s.at[i], i_r.at[q], (q, e)).wait_recv()
        for i, f in enumerate(mates):
            rcopy(ids_out.at[e], ids_out.at[e], j_s.at[i], j_r.at[e], (r, f)).start()

    def prepare():
        keep_x.wait()
        for i, q in enumerate(others):
            rcopy(x_hbm.at[q], xg.at[q], x_s.at[i], x_r.at[q], (q, e)).wait_recv()

        def norm(b):
            x = xg[b].astype(jnp.float32)
            at = pl.ds(b * seq, seq)
            a_ref[at, :] = (x * lax.rsqrt(jnp.mean(x * x, axis=-1, keepdims=True) + EPS)).astype(jnp.bfloat16)
            acc[at, :] = x

        loop(nseq, norm)

    def piece(w, s, f, q):
        if w:
            return go.at[pl.ds(s * orows + q * (orows // nq), orows // nq), :]
        return gw.at[s, :, pl.ds(f * rows + q * quarter, quarter), :]

    def half(w, s, zs, q, i):
        if w:
            n = orows // nq // 2
            return go.at[pl.ds(s * orows + (2 * q + i) * n, n), :]
        n = quarter // 2
        return gw.at[s, :, pl.ds(ep_at(zs, c) * rows + (2 * q + i) * n, n), :]

    def own_wo(s, lo, n):
        return wo_ref.at[pl.ds(mod(s, per) * orows + lo, n), :]

    def z_send(w, s, zs, up):
        ref = piece(w, s, ep_at(zs, c), r)
        return rcopy(ref, ref, (zp if up else zm).at[w, s, zs], zr.at[w, s, zs], (r, e + 2) if up else (r, e - 2))

    def xy_send(w, s, zs, q, ssem, rsem, dev):
        ref = piece(w, s, ep_at(zs, c), q)
        return rcopy(ref, ref, ssem.at[w, s, zs], rsem.at[w, s, zs], dev)

    def xd_send(w, s, zs, q):
        ref = half(w, s, zs, q, 1)
        return rcopy(ref, ref, xd.at[w, s, zs], dr.at[1, w, s, zs], x_dev)

    def yd_send(w, s, zs, q):
        ref = half(w, s, zs, q, 0)
        return rcopy(ref, ref, yd.at[w, s, zs], dr.at[0, w, s, zs], y_dev)

    def p_copy(w, s, zs, j, core):
        ref = piece(w, s, ep_at(zs, core), (r, r_x, r_y, r_d)[j])
        return rcopy(ref, ref, ps.at[w, s, zs, j], pr.at[w, s, zs, j], partner)

    def p_whole(w, s, f):
        ref = go.at[pl.ds(s * orows, orows), :] if w else gw.at[s, :, pl.ds(f * rows, rows), :]
        return rcopy(ref, ref, ps.at[w, s, z, 0], pr.at[w, s, z, 0], partner)

    def own_parts(s):
        return [(w.at[:, pl.ds(s * wide, wide)], m) for m, w in enumerate((wq_ref, wk_ref, wv_ref))]

    def if_wo(s, f, *fns):
        @pl.when(s // per == f)
        def _():
            for fn in fns:
                fn()

    def each_line(fn):
        pl.when(z > 0)(lambda: fn(False))
        pl.when(z < nz - 1)(lambda: fn(True))

    def each_side(k, fn):
        pl.when(z - k - 1 >= 0)(lambda: fn(z - k - 1, True))
        pl.when(z + k + 1 < nz)(lambda: fn(z + k + 1, False))

    def originate(s):
        def line(up):
            sem = zp if up else zm
            dev = (r, e + 2) if up else (r, e - 2)
            for w, m in own_parts(s):
                rcopy(w.at[pl.ds(r * quarter, quarter), :], gw.at[s, m, pl.ds(e * rows + r * quarter, quarter), :],
                      sem.at[0, s, z], zr.at[0, s, z], dev).start()
            if_wo(s, e, lambda: rcopy(own_wo(s, r * (orows // nq), orows // nq), piece(1, s, e, r), sem.at[1, s, z],
                                      zr.at[1, s, z], dev).start())

        each_line(line)
        for w, m in own_parts(s):
            rcopy(w, gw.at[s, m, pl.ds(e * rows, rows), :], ps.at[0, s, z, 0], pr.at[0, s, z, 0], partner).start()
        if_wo(s, e, lambda: rcopy(own_wo(s, 0, orows), go.at[pl.ds(s * orows, orows), :], ps.at[1, s, z, 0],
                                  pr.at[1, s, z, 0], partner).start())

    def for_both(s, f, fn):
        fn(0)
        if_wo(s, f, lambda: fn(1))

    def along_z(s, k):
        def side(zs, up):
            def one(w):
                z_send(w, s, zs, up).wait_recv()
                pl.when(z < nz - 1 if up else z > 0)(lambda: z_send(w, s, zs, up).start())
                xy_send(w, s, zs, r, xs, xr, x_dev).start()
                xy_send(w, s, zs, r, ys, yr, y_dev).start()
                p_copy(w, s, zs, 0, c).start()

            for_both(s, ep_at(zs, c), one)

        each_side(k, side)

    def across(s, k):
        def side(zs, up):
            def one(w):
                xy_send(w, s, zs, r_x, xs, xr, x_dev).wait_recv()
                yd_send(w, s, zs, r_x).start()
                p_copy(w, s, zs, 1, c).start()
                xy_send(w, s, zs, r_y, ys, yr, y_dev).wait_recv()
                xd_send(w, s, zs, r_y).start()
                p_copy(w, s, zs, 2, c).start()

            for_both(s, ep_at(zs, c), one)

        each_side(k, side)

    def diagonal(s, k):
        def side(zs, up):
            def one(w):
                xd_send(w, s, zs, r_d).wait_recv()
                yd_send(w, s, zs, r_d).wait_recv()
                p_copy(w, s, zs, 3, c).start()

            for_both(s, ep_at(zs, c), one)

        each_side(k, side)

    def load(s, f):
        slot = mod(s, 2)
        return pltpu.make_async_copy(gw.at[s, :, pl.ds(f * rows, rows), :], wbuf.at[slot, :, pl.ds(f * rows, rows), :],
                                     lsem.at[slot, f])

    def oload(s, src):
        slot = mod(s, 2)
        return pltpu.make_async_copy(src, obuf.at[slot], lsem.at[slot, nd])

    def collect(s):
        slot = mod(s, 2)
        whole = go.at[pl.ds(s * orows, orows), :]

        def side(zs, up):
            def one(w):
                for j in range(nq):
                    p_copy(w, s, zs, j, 1 - c).wait_recv()

            for_both(s, ep_at(zs, 1 - c), one)

        for k in range(nz - 1):
            each_side(k, side)
        p_whole(0, s, e_p).wait_recv()
        if_wo(s, e_p, lambda: p_whole(1, s, e_p).wait_recv())

        for f in range(nd):
            def near():
                for w, m in own_parts(s):
                    pltpu.make_async_copy(w, wbuf.at[slot, m, pl.ds(f * rows, rows), :], lsem.at[slot, f]).start()

            pl.when(f == e)(near)
            pl.when(f != e)(lambda: load(s, f).start())
        if_wo(s, e, lambda: oload(s, own_wo(s, 0, orows)).start())
        pl.when(s // per != e)(lambda: oload(s, whole).start())

    def wait_loads(s):
        for f in range(nd):
            load(s, f).wait()
        oload(s, go.at[pl.ds(s * orows, orows), :]).wait()

    pair = 2 * HEAD
    npair = wide // pair

    def compute(s, j):
        slot = mod(s, 2)
        a = a_ref[...]
        cols = slice(j * pair, (j + 1) * pair)
        cos, sin = cos_ref[...], sin_ref[...]

        def rot(v):
            return (v * cos + pltpu.roll(v, HEAD // 2, 1) * sin).astype(jnp.bfloat16)

        q, k, v = [jnp.dot(a, wbuf[slot, m, :, cols], preferred_element_type=jnp.float32) for m in range(3)]
        v = v.astype(jnp.bfloat16)
        tri = lax.broadcasted_iota(jnp.int32, (seq, seq), 0) >= lax.broadcasted_iota(jnp.int32, (seq, seq), 1)
        heads = []
        for hh in range(2):
            hc = slice(hh * HEAD, (hh + 1) * HEAD)
            outs = []
            for b in range(nseq):
                rs = slice(b * seq, (b + 1) * seq)
                sc = lax.dot_general(rot(q[rs, hc]), rot(k[rs, hc]), (((1,), (1,)), ((), ())),
                                     preferred_element_type=jnp.float32)
                sc = jnp.where(tri, sc * HEAD ** -0.5, -jnp.inf)
                ex = jnp.exp(sc - jnp.max(sc, axis=-1, keepdims=True))
                p = (ex / jnp.sum(ex, axis=-1, keepdims=True)).astype(jnp.bfloat16)
                outs.append(jnp.dot(p, v[rs, hc], preferred_element_type=jnp.float32).astype(jnp.bfloat16))
            heads.append(jnp.concatenate(outs, axis=0))
        o = jnp.concatenate(heads, axis=1)
        acc[...] += jnp.dot(o, obuf[slot, cols, :], preferred_element_type=jnp.float32)

    def within(s, fn, *args):
        pl.when((s >= 0) & (s < STEPS))(lambda: fn(s, *args))

    originate(0)

    def turn(i):
        within(i + 1, originate)
        within(i - 3, wait_loads)
        for k in range(nz - 1):
            within(i, along_z, k)
            within(i - 1, across, k)
            within(i - 2, diagonal, k)
            if k < npair:
                within(i - 3, compute, k)
        within(i - 2, collect)
        pl.when(i == 1)(spread_ids)
        pl.when(i == 2)(prepare)

    loop(STEPS + 3, turn)

    keep_own = pltpu.make_async_copy(ids_out.at[e], idv, csem.at[0])
    keep_own.start()
    keep_own.wait()
    pitch = d // LANES + 1
    tile = pl.ds(0, d // LANES)

    def spill(v, to_a, to_b, b):
        for k in range(d // LANES):
            tm[pl.ds(k, seq, stride=pitch), :] = v[:, k * LANES:(k + 1) * LANES]

        def rows_to(ref, base, lo):
            def some(g):
                for i in range(8):
                    j = g * 8 + i
                    ref[base + j] = tm[pl.ds((lo + j) * pitch, d // LANES), :].astype(jnp.bfloat16)

            return some

        loop(cut // 8, rows_to(to_a, b * cut, 0))
        loop((seq - cut) // 8, rows_to(to_b, b * (seq - cut), cut))

    def route(b):
        h = acc[pl.ds(b * seq, seq), :].astype(jnp.bfloat16).astype(jnp.float32)
        n = h * lax.rsqrt(jnp.mean(h * h, axis=-1, keepdims=True) + EPS)
        logits = jnp.dot(n, wr_ref[...], precision=lax.Precision.HIGHEST, preferred_element_type=jnp.float32).T
        expert = lax.broadcasted_iota(jnp.int32, logits.shape, 0)
        ids = idv[b]
        picked = jnp.concatenate([jnp.sum(jnp.where(expert == ids[k:k + 1, :], logits, 0.0), axis=0, keepdims=True)
                                  for k in range(ids.shape[0])], axis=0)
        ex = jnp.exp(picked - jnp.max(picked, axis=0, keepdims=True))
        gates[b] = ex / jnp.sum(ex, axis=0, keepdims=True)
        spill(n, ua_ref, ub_ref, b)
        spill(h, ha_ref, hb_ref, b)

    loop(nseq, route)
    left = gates[...].reshape(-1, LANES)
    per_tile = d // LANES
    for term in range(3):
        g = left.astype(jnp.bfloat16)
        left = left - g.astype(jnp.float32)
        for i in range(g.shape[0] // per_tile):
            ua_ref[nseq * cut + term * (g.shape[0] // per_tile) + i] = g[i * per_tile:(i + 1) * per_tile, :]

    for i, f in enumerate(mates):
        rcopy(ids_out.at[e], ids_out.at[f], j_s.at[i], j_r.at[f], (r, f)).wait()
    for i, q in enumerate(others):
        rcopy(idt_hbm.at[q], ids_out.at[e, r], i_s.at[i], i_r.at[r], (q, e)).wait_send()
        rcopy(x_hbm.at[q], xg.at[r], x_s.at[i], x_r.at[r], (q, e)).wait_send()

    def drain(s):
        def side(zs, up):
            def sent(w):
                pl.when(z < nz - 1 if up else z > 0)(lambda: z_send(w, s, zs, up).wait_send())
                for j in range(nq):
                    p_copy(w, s, zs, j, c).wait_send()
                xy_send(w, s, zs, r, xs, xr, x_dev).wait_send()
                xy_send(w, s, zs, r, ys, yr, y_dev).wait_send()
                xd_send(w, s, zs, r_y).wait_send()
                yd_send(w, s, zs, r_x).wait_send()

            for_both(s, ep_at(zs, c), sent)

        for k in range(nz - 1):
            each_side(k, side)

        def own(w):
            each_line(lambda up: z_send(w, s, z, up).wait_send())
            p_whole(w, s, e).wait_send()

        for_both(s, e, own)

    loop(STEPS, drain)


def attention(x, idt, wr, wq, wk, wv, wo, cut):
    nseq, seq, d = x.shape
    rows, hd = wq.shape
    nd, k = d // rows, idt.shape[1]
    cols = d // LANES
    half = HEAD // 2
    freq = THETA ** (-jnp.arange(half, dtype=jnp.float32) / half)
    ang = jnp.arange(seq, dtype=jnp.float32)[:, None] * freq
    cos = jnp.concatenate([jnp.cos(ang)] * 2, axis=1)
    sin = jnp.concatenate([-jnp.sin(ang), jnp.sin(ang)], axis=1)
    vmem = pl.BlockSpec(memory_space=pltpu.VMEM)
    hbm = pl.BlockSpec(memory_space=pl.ANY)
    wide = hd // STEPS
    dma = pltpu.SemaphoreType.DMA
    bf = jnp.bfloat16

    def out(*shape, dtype=bf):
        return jax.ShapeDtypeStruct(shape, dtype)

    na, nb = nseq * cut, nseq * (seq - cut)
    return pl.pallas_call(
        functools.partial(attn_kernel, cut),
        out_shape=(out(na + 3 * nseq * k // cols, cols, LANES), out(nb, cols, LANES), out(na, cols, LANES),
                   out(nb, cols, LANES), out(nd, nseq, k, seq, dtype=jnp.int32), out(STEPS, 3, d, wide), out(hd, d)),
        in_specs=[hbm, hbm] + [vmem] * 3 + [hbm] * 4,
        out_specs=(vmem, vmem, vmem, vmem, hbm, hbm, hbm),
        scratch_shapes=[
            pltpu.VMEM((nseq, seq, d), bf), pltpu.VMEM((nseq * seq, d), bf), pltpu.VMEM((nseq * seq, d), jnp.float32),
            pltpu.VMEM((2, 3, d, wide), bf), pltpu.VMEM((2, hd // STEPS, d), bf),
            pltpu.VMEM((seq * (cols + 1), LANES), jnp.float32), pltpu.VMEM((nseq, k, seq), jnp.float32),
            pltpu.VMEM((nseq, k, seq), jnp.int32),
            *([dma((2, STEPS, 4))] * 9), dma((2, 2, STEPS, 4)), *([dma((2, STEPS, 4, 4))] * 2),
            *([dma((4,))] * 4), *([dma((nd,))] * 2), dma((2, nd + 1)), dma((2,)),
        ],
        compiler_params=pltpu.CompilerParams(collective_id=0, has_side_effects=True, vmem_limit_bytes=58 * 1024 * 1024),
        cost_estimate=pl.CostEstimate(flops=10 * nseq * seq * d * hd, bytes_accessed=8 * d * hd, transcendentals=0),
    )(x, idt, cos, sin, wr, wq, wk, wv, wo)[:5]


def token_of(key):
    return lax.shift_right_logical(key, SLOT_BITS) & ((1 << TOKEN_BITS) - 1)


def moe_kernel(nt, nblk_ref, be_ref, bb_ref, bn_ref, key_ref, gate_ref, u_hbm, w1_hbm, w3_hbm, w2_hbm,
               out_hbm, ub, acc, w1, w3, w2, xs, zs, lhs, usem, wsem, osem):
    cols = ub.shape[1]
    nexp = w1_hbm.shape[0]
    nblk = nblk_ref[0]

    def weights(e, slot):
        return (pltpu.make_async_copy(w1_hbm.at[e], w1.at[slot], wsem.at[slot, 0]),
                pltpu.make_async_copy(w3_hbm.at[e], w3.at[slot], wsem.at[slot, 1]),
                pltpu.make_async_copy(w2_hbm.at[e], w2.at[slot], wsem.at[slot, 2]))

    nd = u_hbm.shape[0]
    n = nt // nd
    for dev in range(nd):
        pltpu.make_async_copy(u_hbm.at[dev, pl.ds(0, n)], ub.at[pl.ds(dev * n, n)], usem).start()

    for c in weights(0, 0):
        c.start()

    def zero(i):
        acc[pl.ds(i * 8, 8)] = jnp.zeros((8,) + acc.shape[1:], jnp.float32)

    loop(acc.shape[0] // 8, zero)
    pltpu.make_async_copy(ub.at[pl.ds(0, nt)], ub.at[pl.ds(0, nt)], usem).wait()

    def gather(b):
        base = bb_ref[b]
        for i in range(BM):
            t = token_of(key_ref[base + i])
            xs[pl.ds(i, cols, stride=PITCH), :] = ub[t].astype(jnp.float32)

    def scatter(base, n, rows):
        new = []
        for i in rows:
            key = key_ref[base + i]
            t = jnp.where(i < n, token_of(key), nt)
            new.append((t, acc[t] + gate_ref[key & ((1 << SLOT_BITS) - 1)] * zs[pl.ds(i, cols, stride=PITCH), :]))
        for t, v in new:
            acc[t] = v

    gather(0)

    def body(b, e_prev):
        e = be_ref[b]
        slot = e % 2

        @pl.when(e != e_prev)
        def _():
            @pl.when(e + 1 < nexp)
            def _():
                for c in weights(e + 1, 1 - slot):
                    c.start()

            for c in weights(e, slot):
                c.wait()

        for k in range(cols):
            lhs[:, k * LANES:(k + 1) * LANES] = xs[k * PITCH:k * PITCH + BM, :].astype(jnp.bfloat16)
        gather(b + 1)
        bp = jnp.maximum(b - 1, 0)
        base, n = bb_ref[bp], jnp.where(b > 0, bn_ref[bp], 0)
        for i in range(0, BM, 8):
            scatter(base, n, range(i, i + 8))
        x = lhs[...]
        a1 = jnp.dot(x, w1[slot], preferred_element_type=jnp.float32)
        a3 = jnp.dot(x, w3[slot], preferred_element_type=jnp.float32)
        act = (jax.nn.silu(a1) * a3).astype(jnp.bfloat16)
        z = jnp.dot(act, w2[slot], preferred_element_type=jnp.float32).astype(jnp.bfloat16).astype(jnp.float32)
        for k in range(cols):
            zs[k * PITCH:k * PITCH + BM, :] = z[:, k * LANES:(k + 1) * LANES]
        return e

    lax.fori_loop(0, nblk, body, -1)
    base, n = bb_ref[nblk - 1], bn_ref[nblk - 1]
    for i in range(0, BM, 8):
        scatter(base, n, range(i, i + 8))

    def pack(i):
        for j in range(8):
            t = i * 8 + j
            ub[t] = acc[t].astype(jnp.bfloat16)

    loop(nt // 8, pack)
    store = pltpu.make_async_copy(ub.at[pl.ds(0, nt)], out_hbm, osem)
    store.start()
    store.wait()


def moe(nblk, be, bb, bn, keys, gates, u, n, w1, w3, w2):
    nd, _, cols, _ = u.shape
    nt = nd * n
    ne, d, f = w1.shape
    smem = pl.BlockSpec(memory_space=pltpu.SMEM)
    hbm = pl.BlockSpec(memory_space=pl.ANY)
    return pl.pallas_call(
        functools.partial(moe_kernel, nt),
        out_shape=jax.ShapeDtypeStruct((nt, cols, LANES), jnp.bfloat16),
        in_specs=[smem] * 6 + [hbm] * 4,
        out_specs=hbm,
        scratch_shapes=[
            pltpu.VMEM((nt + 8, cols, LANES), jnp.bfloat16),
            pltpu.VMEM((nt + 8, cols, LANES), jnp.float32),
            pltpu.VMEM((2, d, f), jnp.bfloat16),
            pltpu.VMEM((2, d, f), jnp.bfloat16),
            pltpu.VMEM((2, f, d), jnp.bfloat16),
            pltpu.VMEM((cols * PITCH, LANES), jnp.float32),
            pltpu.VMEM((cols * PITCH, LANES), jnp.float32),
            pltpu.VMEM((BM, d), jnp.bfloat16),
            pltpu.SemaphoreType.DMA,
            pltpu.SemaphoreType.DMA((2, 3)),
            pltpu.SemaphoreType.DMA,
        ],
        compiler_params=pltpu.CompilerParams(vmem_limit_bytes=60 * 1024 * 1024),
        cost_estimate=pl.CostEstimate(flops=6 * 5000 * d * f, bytes_accessed=ne * 3 * d * f * 2, transcendentals=0),
    )(nblk, be, bb, bn, keys, gates, u, w1, w3, w2)


def back_kernel(cut, piece, part, h_ref, ya, y_out, own, prt, raw, fin, fout, yst, raw_s, raw_r, prt_s, prt_r, f_s, f_r,
                y_s, y_r, osem, lsem):
    r, e = lax.axis_index('replica'), lax.axis_index('ep')
    z, c = e // 2, e % 2
    me_p = e + 1 - 2 * c
    n = h_ref.shape[0]
    np_ = n // piece
    split = n // 4 // piece
    mid = (z + 2) // 3 + (5 - z) // 3 - 1
    is_mid, is_end = mid == 1, mid == 0
    low = z // 2
    z_mid = 1 + low
    z_end = 3 * low
    z_oth = 2 - low
    h_a, h_b, h_c = 3 - 3 * low, 2 - low, 3 * low
    replicas = [(r + i) % 4 for i in range(1, 4)]

    def rows(p):
        return pl.ds(p * piece, piece)

    meet([(None, (q, e)) for q in replicas] + [(None, (r, me_p))] +
         [(is_end, (r, ep_at(z_mid, i))) for i in range(2)] + [(is_mid, (r, ep_at(z_end, i))) for i in range(2)] +
         [(is_mid, (r, ep_at(z_oth, c)))], 6 + mid)

    def raw_send(i, c2, p):
        dest = (3 - i) + low * (2 * i - 3)
        return rcopy(part.at[ep_at(dest, c2), rows(p)], raw.at[i, c, rows(p)], raw_s.at[i, c2, p], raw_r.at[i, c, p],
                     (r, ep_at(z_mid, c2)))

    def raw_recv(i, src, p):
        return rcopy(raw.at[i, src, rows(p)], raw.at[i, src, rows(p)], raw_s.at[i, src, p], raw_r.at[i, src, p],
                     (r, ep_at(z_end, src)))

    def prt_copy(hh, p):
        return rcopy(part.at[ep_at(hh, 1 - c), rows(p)], prt.at[hh, rows(p)], prt_s.at[hh, p], prt_r.at[hh, p], (r, me_p))

    def f_copy(i, slot, p, dev):
        return rcopy(fout.at[i, rows(p)], fin.at[slot, rows(p)], f_s.at[i, p], f_r.at[slot, p], dev)

    def loadown(hh):
        return pltpu.make_async_copy(part.at[ep_at(hh, c)], own.at[hh], osem.at[hh])

    def place(half):
        return pl.ds(0, cut) if half < 0 else pl.ds(cut + half * piece, piece)

    def y_copy(src, blk, half):
        return rcopy(src, y_out.at[r, place(half)], y_s.at[blk, half + 1], y_r.at[r, half + 1], (blk, e))

    def y_local(src, half):
        return pltpu.make_async_copy(src, y_out.at[r, place(half)], lsem.at[half + 1])

    def put(src, blk, half):
        @pl.when(r == blk)
        def _():
            y_local(src, half).start()

        @pl.when(r != blk)
        def _():
            y_copy(src, blk, half).start()

    @pl.when(is_end)
    def _():
        loadown(z).start()
        for i in range(3):
            def send(p):
                for c2 in range(2):
                    raw_send(i, c2, p).start()

            loop(np_, send)

        def pass_on(p):
            prt_copy(z, p).start()

        loop(np_, pass_on)

    @pl.when(is_mid)
    def _():
        for hh in (h_a, h_b, h_c, z):
            loadown(hh).start()
        for hh in (h_a, h_b, h_c, z):
            def pass_on(p):
                prt_copy(hh, p).start()

            loop(np_, pass_on)

    for blk in range(4):
        put(ya.at[blk], blk, -1)

    def groups(p, fn):
        def g(j):
            fn(pl.ds(p * piece + j * 8, 8))

        loop(piece // 8, g)

    def f32(v):
        return v.astype(jnp.float32)

    def both(hh, s):
        return f32(own[hh, s]) + f32(prt[hh, s])

    def onward(i, hh, p, dev_slot, incoming):
        prt_copy(hh, p).wait_recv()

        def fn(s):
            fout[i, s] = both(hh, s) + incoming(s)

        groups(p, fn)
        f_copy(i, dev_slot[1], p, dev_slot[0]).start()

    def finish(p, incoming):
        prt_copy(z, p).wait_recv()

        def fn(s):
            yst[s] = (f32(h_ref[s]) + both(z, s) + incoming(s)).astype(jnp.bfloat16)

        groups(p, fn)

        for blk in range(4):
            for half in range(split):
                @pl.when(p == blk * split + half)
                def _():
                    put(yst.at[rows(p)], blk, half)

    @pl.when(is_mid)
    def _():
        loadown(h_a).wait()

        def far(p):
            raw_recv(0, 0, p).wait_recv()
            raw_recv(0, 1, p).wait_recv()
            onward(0, h_a, p, ((r, ep_at(z_oth, c)), 0), lambda s: f32(raw[0, 0, s]) + f32(raw[0, 1, s]))

        loop(np_, far)
        loadown(h_b).wait()
        loadown(h_c).wait()

        def near(p):
            f_copy(2, 0, p, (r, ep_at(z_oth, c))).wait_recv()
            onward(2, h_c, p, ((r, ep_at(z_end, c)), 0), lambda s: fin[0, s])
            raw_recv(1, 0, p).wait_recv()
            raw_recv(1, 1, p).wait_recv()
            onward(1, h_b, p, ((r, ep_at(z_oth, c)), 1), lambda s: f32(raw[1, 0, s]) + f32(raw[1, 1, s]))

        loop(np_, near)
        loadown(z).wait()

        def last(p):
            f_copy(1, 1, p, (r, ep_at(z_oth, c))).wait_recv()
            raw_recv(2, 0, p).wait_recv()
            raw_recv(2, 1, p).wait_recv()
            finish(p, lambda s: fin[1, s] + f32(raw[2, 0, s]) + f32(raw[2, 1, s]))

        loop(np_, last)

    @pl.when(is_end)
    def _():
        loadown(z).wait()

        def last(p):
            f_copy(2, 0, p, (r, ep_at(z_mid, c))).wait_recv()
            finish(p, lambda s: fin[0, s])

        loop(np_, last)

    @pl.when(is_end)
    def _():
        def sent(p):
            for i in range(3):
                for c2 in range(2):
                    raw_send(i, c2, p).wait_send()
            prt_copy(z, p).wait_send()

        loop(np_, sent)

    @pl.when(is_mid)
    def _():
        def sent(p):
            for hh in (h_a, h_b, h_c, z):
                prt_copy(hh, p).wait_send()
            f_copy(0, 0, p, (r, ep_at(z_oth, c))).wait_send()
            f_copy(1, 1, p, (r, ep_at(z_oth, c))).wait_send()
            f_copy(2, 0, p, (r, ep_at(z_end, c))).wait_send()

        loop(np_, sent)

    for blk in range(4):
        for half in range(-1, split):
            some = ya.at[blk] if half < 0 else yst.at[rows(0)]

            @pl.when(r == blk)
            def _():
                y_local(some, half).wait()

            @pl.when(r != blk)
            def _():
                y_copy(some, blk, half).wait_send()
                ref = y_out.at[blk, place(half)]
                rcopy(ref, ref, y_s.at[blk, half + 1], y_r.at[blk, half + 1], (blk, e)).wait_recv()


def back(part, h, ya):
    _, n, cols, _ = part.shape
    cut = ya.shape[1]
    seq = cut + n // 4
    piece = n // 8
    vmem = pl.BlockSpec(memory_space=pltpu.VMEM)
    hbm = pl.BlockSpec(memory_space=pl.ANY)
    dma = pltpu.SemaphoreType.DMA
    np_ = n // piece

    def tiles(lead, dtype):
        return pltpu.VMEM(lead + (cols, LANES), dtype)

    return pl.pallas_call(
        functools.partial(back_kernel, cut, piece),
        out_shape=jax.ShapeDtypeStruct((4, seq, cols, LANES), jnp.bfloat16),
        in_specs=[hbm, vmem, hbm],
        out_specs=hbm,
        scratch_shapes=[
            tiles((4, n), jnp.bfloat16), tiles((4, n), jnp.bfloat16), tiles((3, 2, n), jnp.bfloat16),
            tiles((2, n), jnp.float32), tiles((3, n), jnp.float32), tiles((n,), jnp.bfloat16),
            dma((3, 2, np_)), dma((3, 2, np_)), dma((4, np_)), dma((4, np_)), dma((3, np_)), dma((2, np_)),
            dma((4, 3)), dma((4, 3)), dma((4,)), dma((3,)),
        ],
        compiler_params=pltpu.CompilerParams(collective_id=1, has_side_effects=True, vmem_limit_bytes=58 * 1024 * 1024),
    )(part, h, ya)


def block_plan(ids, me, ne):
    _, nseq, _, n = ids.shape
    le = ids - me * ne
    local = (le >= 0) & (le < ne)
    total = ids.size
    slot = lax.iota(jnp.int32, total).reshape(ids.shape)
    token = (lax.broadcasted_iota(jnp.int32, ids.shape, 0) * nseq + lax.broadcasted_iota(jnp.int32, ids.shape, 1)) * n
    token = token + lax.broadcasted_iota(jnp.int32, ids.shape, 3)
    key = (le << (SLOT_BITS + TOKEN_BITS)) | (token << SLOT_BITS) | slot
    none = jnp.iinfo(jnp.int32).max
    keys = lax.sort(jnp.where(local, key, none).reshape(-1), is_stable=False)
    experts = jnp.arange(ne, dtype=jnp.int32)
    counts = jnp.sum((le.reshape(-1)[None, :] == experts[:, None]).astype(jnp.int32), axis=1)
    low = (experts[None, :] < experts[:, None])
    first = jnp.sum(jnp.where(low, counts[None, :], 0), axis=1)
    nb = jnp.maximum((counts + BM - 1) // BM, 1)
    bfirst = jnp.sum(jnp.where(low, nb[None, :], 0), axis=1)
    maxb = total // BM + ne + 2
    b = jnp.arange(maxb, dtype=jnp.int32)
    inside = (b[:, None] >= bfirst[None, :]) & (b[:, None] < (bfirst + nb)[None, :])

    def of(v):
        return jnp.sum(jnp.where(inside, v[None, :], 0), axis=1)

    done = (b - of(bfirst)) * BM
    be, bb = of(experts), of(first) + done
    bn = jnp.clip(of(counts) - done, 0, BM)
    bb = jnp.where(jnp.any(inside, axis=1), bb, 0)
    keys = jnp.concatenate([jnp.where(keys == none, 0, keys), jnp.zeros((BM,), jnp.int32)])
    return jnp.sum(nb).reshape(1), be, bb, bn, keys


def solution(mesh):
    nd = mesh.shape['ep']
    tok = P(('replica', 'ep'), None, None)
    rows_ep = P('ep', None)
    by_expert = P('ep', None, None)
    cut = CUT

    def local(x, wq, wk, wv, wo, wr, w1, w3, w2, idx):
        b, s, d = x.shape
        k, ne = idx.shape[-1], w1.shape[0]
        me = lax.axis_index('ep')
        cols = d // LANES
        ua, ub, ha, hb, ids = attention(x, idx.transpose(0, 2, 1), wr, wq, wk, wv, wo, cut)

        def experts(u, gates, lo, hi):
            n = b * (hi - lo)
            plan = block_plan(ids[..., lo:hi], me, ne)
            return moe(*plan, gates[..., lo:hi].reshape(-1), u, n, w1, w3, w2).reshape(nd, n, cols, LANES)

        u_all = lax.all_gather(ua, 'ep', axis=0, tiled=False)
        terms = u_all[:, b * cut:].reshape(nd, 3, b, k, s).astype(jnp.float32)
        gates = terms[:, 0] + terms[:, 1] + terms[:, 2]
        part_a = experts(u_all, gates, 0, cut)
        part_a = lax.all_to_all(part_a, 'ep', 0, 0, tiled=True)
        part_b = experts(lax.all_gather(ub, 'ep', axis=0, tiled=False), gates, cut, s)
        ya = ha.astype(jnp.float32) + jnp.sum(part_a.astype(jnp.float32), axis=0)
        y = back(part_b, hb, ya.astype(jnp.bfloat16).reshape(b, cut, cols, LANES))
        return y.reshape(b, s, d)

    return jax.shard_map(local, mesh=mesh,
                         in_specs=(tok, rows_ep, rows_ep, rows_ep, rows_ep, P(None, None),
                                   by_expert, by_expert, by_expert, tok),
                         out_specs=tok, check_vma=False)
```

time: 855 us -> 788 us (0.922); the launches traced: 838 us -> 782 us
  blocking collectives: 24.3 us -> 0 us
  local copies, waits for them, and re-layouts: 31.1 us -> 8.5 us
  other arithmetic: 46.1 us -> 26.1 us
  waiting for transfers between devices: 83.2 us -> 92.8 us
    all_gather x1 -> x0, blocking collectives: 14.3 us -> none  [local(): ids_all = lax.all_gather(ids.T, 'ep', axis=0, tiled=False)]
    all_gather x2, waiting for transfers between devices: 48.3 us -> 59 us  [the longest x1 59 us: local(): u_all = lax.all_gather(ua, 'ep', axis=0, tiled=False)]
    all_to_all x1 -> x0, blocking collectives: 10 us -> none  [local(): idx = lax.all_to_all(idx, 'replica', 0, 0, tiled=True)]
    reduce_sum x4 -> x1, other arithmetic: 13.6 us -> 3.82 us  [local(): ya = ha.astype(jnp.float32) + jnp.sum(part_a.astype(jnp.float32), axis=0)]
    pallas_call x3, Pallas kernels: 443 us -> 452 us  [the longest x1 280 us: attention(): pl.pallas_call(functools.partial(attn_kernel, cut), out_shape=(out(na + 3...]
  transfers between devices with their start and end apart: 4 -> 3, of which waited for: 3 -> 2; matrix products, arithmetic and copies ran while one was open for 6% -> 3% of each run, Pallas kernels for 20% -> 22%
where the time goes in v4:
time: 788 us; the launch traced here: 782 us
  Pallas kernels  626 us (79%)
  waiting for transfers between devices  92.8 us (12%)
  other arithmetic  26.1 us (3%)
  starting transfers between devices  14.7 us (2%)
  between operations  13.6 us (2%)
  local copies, waits for them, and re-layouts  8.5 us (1%)
    pallas_call x1, Pallas kernels, attention(): pl.pallas_call(functools.partial(attn_kernel, cut), out_shape=(out(na + 3...  280 us
    pallas_call x1, Pallas kernels, back(): pl.pallas_call(functools.partial(back_kernel, cut, piece), out_shape=jax....  174 us
    pallas_call x2, Pallas kernels, moe(): pl.pallas_call(functools.partial(moe_kernel, nt), out_shape=jax.ShapeDtyp...  172 us
    all_gather x1, waiting for transfers between devices, local(): u_all = lax.all_gather(ua, 'ep', axis=0, tiled=False)  59 us
    all_to_all x1, waiting for transfers between devices, local(): part_a = lax.all_to_all(part_a, 'ep', 0, 0, tiled=True)  33.1 us
  transfers between devices with their start and end apart: 3, of which 2 were waited for; matrix products, arithmetic and copies ran while one was open for 3% of the time, Pallas kernels for 22%

profile of v4, /device:TPU:0, one launch (start us, length us, event | category | flops | bytes accessed | tf_op | source)
XLA Modules:
  0.0 781.8 jit_solution(14468658422152318627)
XLA Ops:
  6.5 0.0 all-gather.5.cloned.1.call-start
  6.5 0.3 fusion.3
  6.8 0.7 pad_maximum_fusion.cos_ref
  7.5 0.7 pad_maximum_fusion.1.sin_ref
  8.2 280.2 %shard_map.100 = (bf16[198,16,128]{2,1,0:T(8,128)(2,1)}, bf16[320,16,128]{2,1,0:T(8,128)(2,1)}, bf16[192,16,128]{2,1,0:T(8,128)(2,1)}, bf16[320,16,128]{2,1,0:T(...) custom-call(bf16[4,128,2048]{2,1,0:T(8,128)(2,1)} %x_hbm.1, ...), custom_call_target="tpu_custom_call" | custom-call | flops 42949672960 | bytes 67108864 | tf_op jit(solution)/shard_map/pallas_call | solution.py:405
  288.5 0.0 copy-start.1
  288.5 0.0 all-gather.5.cloned.1.call-update
  288.5 0.0 all-gather.7.cloned.1.call-start
  288.5 0.7 all-gather.7.cloned.1.call-update
  289.3 0.1 copy-done.1
  289.4 0.1 or_select_fusion.1
  289.5 0.1 eq.42
  289.6 0.1 or_select_fusion
  289.7 0.1 eq.48
  289.9 0.2 convert_reduce_fusion.2
  290.1 0.3 convert_reduce_fusion.1
  290.4 0.7 fusion.10
  291.1 0.1 select_reduce_fusion.9
  291.2 0.1 reshape.152
  291.3 6.3 sort.15
  297.6 0.6 concatenate.15.key_ref
  298.2 0.1 select_reduce_fusion.7
  298.4 0.1 fusion.9
  298.5 0.7 select_reduce_fusion.4
  299.1 0.6 subtract_clamp_fusion.1
  299.7 59.0 %all-gather.5.cloned.1.call-done = bf16[1584,16,128]{2,1,0:T(8,128)(2,1)} async-done(((bf16[198,16,128]{2,1,0:T(8,128)(2,1)}), bf16[1584,16,128]{2,1,0:T(8,128)(2,1)}) %all-gather.5.cloned.1.call-update) | async-done | bytes 6488080 | tf_op jit(solution)/shard_map/all_gather | solution.py:824
  358.7 0.9 slice.32
  359.7 0.7 reshape.153.gate_ref
  360.4 77.6 %shard_map.102 = bf16[1536,16,128]{2,1,0:T(8,128)(2,1)} custom-call(s32[1]{0:T(128)} %bitcast.8.nblk_ref, s32[114]{0:T(128)} %get-tuple-element.18.be_ref, s32[114]{0:T(128)} %get-tuple-element.34.bb_ref, s32[114]{0:T(128)} %get-tuple-element.33.bn_ref, s32[12416]{0:T(1024)} %concatenate.15.key_ref, f32[12288]{0:T(1024)} %reshape.153.gate_ref, ...), custom_call_target="tpu_custom_call" | custom-call | flops 47185920000 | bytes 150994944 | tf_op jit(solution)/shard_map/pallas_call | solution.py:522
  438.0 14.7 %all-to-all-start = ((bf16[8,192,16,128]{3,2,1,0:T(8,128)(2,1)}), bf16[8,192,16,128]{3,2,1,0:T(8,128)(2,1)}, u32[]{:S(2)}, u32[]{:S(2)}) async-start(bf16[8,192,16,128]{3,2,1,0:T(8,128)(2,1)} %bitcast.28), calls=%async_computation | async-start | bytes 12582912 | tf_op jit(solution)/shard_map/all_to_all | solution.py:828
  452.7 0.1 select_reduce_fusion.11
  452.8 0.1 reshape.140
  452.9 8.5 %sort.14 = s32[20480]{0:T(1024)S(1)} sort(s32[20480]{0:T(1024)S(1)} %reshape.140), dimensions={0}, to_apply=%region_9.10 | sort | flops 307200 | bytes 163840 | tf_op jit(solution)/shard_map/sort | solution.py:783
  461.5 0.6 concatenate.14.key_ref
  462.1 0.1 select_reduce_fusion.10
  462.3 0.1 fusion.8
  462.3 0.7 select_reduce_fusion
  463.0 0.6 subtract_clamp_fusion
  463.6 0.1 slice.36
  463.7 0.8 reshape.141.gate_ref
  464.4 0.0 all-gather.7.cloned.1.call-done
  464.4 94.1 %shard_map.101 = bf16[2560,16,128]{2,1,0:T(8,128)(2,1)} custom-call(s32[1]{0:T(128)} %bitcast.1.nblk_ref, s32[178]{0:T(256)} %get-tuple-element.22.be_ref, s32[178]{0:T(256)} %get-tuple-element.32.bb_ref, s32[178]{0:T(256)} %get-tuple-element.31.bn_ref, s32[20608]{0:T(1024)} %concatenate.14.key_ref, f32[20480]{0:T(1024)} %reshape.141.gate_ref, ...), custom_call_target="tpu_custom_call" | custom-call | flops 47185920000 | bytes 150994944 | tf_op jit(solution)/shard_map/pallas_call | solution.py:522
  558.6 0.0 copy-start
  558.6 33.1 %all-to-all-done = bf16[8,192,16,128]{3,2,1,0:T(8,128)(2,1)} async-done(((bf16[8,192,16,128]{3,2,1,0:T(8,128)(2,1)}), bf16[8,192,16,128]{3,2,1,0:T(8,128)(2,1)}, u32[]{:S(2)}, u32[]{:S(2)}) %all-to-all-start) | async-done | bytes 6291488 | tf_op jit(solution)/shard_map/all_to_all | solution.py:828
  591.7 3.8 convert_reduce_fusion
  595.5 0.0 copy-done
  595.5 1.1 add_convert_fusion
  596.6 174.3 %shard_map.103 = bf16[4,128,16,128]{3,2,1,0:T(8,128)(2,1)} custom-call(bf16[8,320,16,128]{3,2,1,0:T(8,128)(2,1)} %bitcast.27, bf16[320,16,128]{2,1,0:T(8,128)(2,1)} %get-tuple-element.13.h_ref, bf16[4,48,16,128]{3,2,1,0:T(8,128)(2,1)} %bitcast.29), custom_call_target="tpu_custom_call" | custom-call | tf_op jit(solution)/shard_map/pallas_call | solution.py:758
  770.8 4.2 reshape.156
  (8 shorter events, 0.1 us)
Async XLA Ops:
  6.5 352.2 %all-gather.5.cloned.1.call-start = ((), (), s32[]{:S(2)}) async-start(), calls=%async_computation.1 | async-start | bytes 7299072 | tf_op jit(solution)/shard_map/all_gather | solution.py:824
  288.5 0.9 copy-start.1
  288.5 176.0 %all-gather.7.cloned.1.call-start = ((), (), s32[]{:S(2)}) async-start(), calls=%async_computation.2 | async-start | bytes 11796480 | tf_op jit(solution)/shard_map/all_gather | solution.py:829
  438.0 153.7 %all-to-all-start = ((bf16[8,192,16,128]{3,2,1,0:T(8,128)(2,1)}), bf16[8,192,16,128]{3,2,1,0:T(8,128)(2,1)}, u32[]{:S(2)}, u32[]{:S(2)}) async-start(bf16[8,192,16,128]{3,2,1,0:T(8,128)(2,1)} %bitcast.28), calls=%async_computation | async-start | bytes 12582912 | tf_op jit(solution)/shard_map/all_to_all | solution.py:828
  558.6 36.9 %copy-start = (bf16[192,16,128]{2,1,0:T(8,128)(2,1)S(1)}, bf16[192,16,128]{2,1,0:T(8,128)(2,1)}, u32[]{:S(2)}) copy-start(bf16[192,16,128]{2,1,0:T(8,128)(2,1)} %get-tuple-element.14) | copy-start | bytes 2359300
Sparse Core Ops, SparseCore 0:
  288.6 70.0 all-gather.4
  360.3 98.0 all-gather.6

commit v5 on v4

--- a/solution.py
+++ b/solution.py
@@ -12,7 +12,7 @@
 BM = 128
 PITCH = BM + 1
 LANES = 128
-CUT = 48
+CUT = 40
 STEPS = 8
 SLOT_BITS, TOKEN_BITS = 15, 12
 
@@ -542,204 +542,184 @@
     )(nblk, be, bb, bn, keys, gates, u, w1, w3, w2)
 
 
-def back_kernel(cut, piece, part, h_ref, ya, y_out, own, prt, raw, fin, fout, yst, raw_s, raw_r, prt_s, prt_r, f_s, f_r,
-                y_s, y_r, osem, lsem):
+def back_kernel(cut, piece, part, h_ref, ya, y_out, own, prt, raw, fin, fout, hs, yst, raw_s, raw_r, prt_s, prt_r, f_s, f_r,
+                h_s, h_r, y_s, y_r, osem, lsem):
     r, e = lax.axis_index('replica'), lax.axis_index('ep')
     z, c = e // 2, e % 2
-    me_p = e + 1 - 2 * c
     n = h_ref.shape[0]
-    np_ = n // piece
-    split = n // 4 // piece
+    pieces = n // piece
+    split = pieces // 4
     mid = (z + 2) // 3 + (5 - z) // 3 - 1
-    is_mid, is_end = mid == 1, mid == 0
     low = z // 2
-    z_mid = 1 + low
-    z_end = 3 * low
-    z_oth = 2 - low
-    h_a, h_b, h_c = 3 - 3 * low, 2 - low, 3 * low
-    replicas = [(r + i) % 4 for i in range(1, 4)]
+    on_mid, on_end = pl.when(mid == 1), pl.when(mid == 0)
+    z_mid, z_end = 1 + low, 3 * low
+    partner, across = (r, ep_at(z, 1 - c)), (r, ep_at(2 - low, c))
+    to_end = (r, ep_at(z_end, c))
+    others = [lax.rem(r + i, 4) for i in range(1, 4)]
+
+    def far(i):
+        return 2 + i + low * (-1 - 2 * i)
+
+    def near(i):
+        return 1 - i + low * (1 + 2 * i)
 
     def rows(p):
         return pl.ds(p * piece, piece)
 
-    meet([(None, (q, e)) for q in replicas] + [(None, (r, me_p))] +
-         [(is_end, (r, ep_at(z_mid, i))) for i in range(2)] + [(is_mid, (r, ep_at(z_end, i))) for i in range(2)] +
-         [(is_mid, (r, ep_at(z_oth, c)))], 6 + mid)
-
-    def raw_send(i, c2, p):
-        dest = (3 - i) + low * (2 * i - 3)
-        return rcopy(part.at[ep_at(dest, c2), rows(p)], raw.at[i, c, rows(p)], raw_s.at[i, c2, p], raw_r.at[i, c, p],
-                     (r, ep_at(z_mid, c2)))
-
-    def raw_recv(i, src, p):
-        return rcopy(raw.at[i, src, rows(p)], raw.at[i, src, rows(p)], raw_s.at[i, src, p], raw_r.at[i, src, p],
-                     (r, ep_at(z_end, src)))
-
-    def prt_copy(hh, p):
-        return rcopy(part.at[ep_at(hh, 1 - c), rows(p)], prt.at[hh, rows(p)], prt_s.at[hh, p], prt_r.at[hh, p], (r, me_p))
-
-    def f_copy(i, slot, p, dev):
-        return rcopy(fout.at[i, rows(p)], fin.at[slot, rows(p)], f_s.at[i, p], f_r.at[slot, p], dev)
-
-    def loadown(hh):
-        return pltpu.make_async_copy(part.at[ep_at(hh, c)], own.at[hh], osem.at[hh])
+    end, inner = mid == 0, mid == 1
+    meet([(None, (q, e)) for q in others] + [(None, partner)] +
+         [(end, (q, ep_at(z_mid, c))) for q in range(4)] + [(end, (r, ep_at(z_mid, 1 - c)))] +
+         [(inner, (q, ep_at(z_end, c))) for q in range(4)] + [(inner, (r, ep_at(z_end, 1 - c))), (inner, across)], 9 + mid)
+
+    def raw_send(i, core, p):
+        return rcopy(part.at[ep_at(far(i), core), rows(p)], raw.at[i, c, rows(p)], raw_s.at[i, core, p], raw_r.at[i, c, p],
+                     (r, ep_at(z_mid, core)))
+
+    def raw_recv(i, core, p):
+        ref = raw.at[i, core, rows(p)]
+        return rcopy(ref, ref, raw_s.at[i, core, p], raw_r.at[i, core, p], (r, ep_at(z_end, core)))
+
+    def prt_copy(chip, p):
+        return rcopy(part.at[ep_at(chip, 1 - c), rows(p)], prt.at[chip, rows(p)], prt_s.at[chip, p], prt_r.at[chip, p], partner)
+
+    def f_copy(i, p, onward):
+        return rcopy(fout.at[2 * onward + i, rows(p)], fin.at[i, rows(p)], f_s.at[2 * onward + i, p], f_r.at[i, p],
+                     to_end if onward else across)
+
+    def load(chip):
+        return pltpu.make_async_copy(part.at[ep_at(chip, c)], own.at[chip], osem.at[chip])
+
+    send_h = rcopy(h_ref, hs, h_s, h_r, to_end)
 
     def place(half):
         return pl.ds(0, cut) if half < 0 else pl.ds(cut + half * piece, piece)
 
-    def y_copy(src, blk, half):
-        return rcopy(src, y_out.at[r, place(half)], y_s.at[blk, half + 1], y_r.at[r, half + 1], (blk, e))
+    def y_copy(src, i, blk, half, f):
+        return rcopy(src, y_out.at[r, place(half)], y_s.at[i, blk, half + 1], y_r.at[r, half + 1], (blk, f))
 
     def y_local(src, half):
         return pltpu.make_async_copy(src, y_out.at[r, place(half)], lsem.at[half + 1])
 
     def put(src, blk, half):
-        @pl.when(r == blk)
-        def _():
-            y_local(src, half).start()
-
-        @pl.when(r != blk)
-        def _():
-            y_copy(src, blk, half).start()
-
-    @pl.when(is_end)
+        pl.when(r == blk)(lambda: y_local(src, half).start())
+        pl.when(r != blk)(lambda: y_copy(src, 1, blk, half, e).start())
+
+    def each(fn, count=pieces):
+        loop(count, fn)
+
+    for i in range(2):
+        load(near(i)).start()
+
+    @on_end
     def _():
-        loadown(z).start()
-        for i in range(3):
-            def send(p):
-                for c2 in range(2):
-                    raw_send(i, c2, p).start()
-
-            loop(np_, send)
-
-        def pass_on(p):
-            prt_copy(z, p).start()
-
-        loop(np_, pass_on)
-
-    @pl.when(is_mid)
+        for i in range(2):
+            each(lambda p: [raw_send(i, core, p).start() for core in range(2)])
+            each(lambda p: prt_copy(near(i), p).start())
+
+    @on_mid
     def _():
-        for hh in (h_a, h_b, h_c, z):
-            loadown(hh).start()
-        for hh in (h_a, h_b, h_c, z):
-            def pass_on(p):
-                prt_copy(hh, p).start()
-
-            loop(np_, pass_on)
+        send_h.start()
+        for i in range(2):
+            load(far(i)).start()
+            each(lambda p: [prt_copy(far(i), p).start(), prt_copy(near(i), p).start()])
 
     for blk in range(4):
         put(ya.at[blk], blk, -1)
 
-    def groups(p, fn):
-        def g(j):
-            fn(pl.ds(p * piece + j * 8, 8))
-
-        loop(piece // 8, g)
-
     def f32(v):
         return v.astype(jnp.float32)
 
-    def both(hh, s):
-        return f32(own[hh, s]) + f32(prt[hh, s])
-
-    def onward(i, hh, p, dev_slot, incoming):
-        prt_copy(hh, p).wait_recv()
-
-        def fn(s):
-            fout[i, s] = both(hh, s) + incoming(s)
-
-        groups(p, fn)
-        f_copy(i, dev_slot[1], p, dev_slot[0]).start()
-
-    def finish(p, incoming):
-        prt_copy(z, p).wait_recv()
-
-        def fn(s):
-            yst[s] = (f32(h_ref[s]) + both(z, s) + incoming(s)).astype(jnp.bfloat16)
-
-        groups(p, fn)
-
+    def add(chip, p, incoming, out, finish=f32):
+        prt_copy(chip, p).wait_recv()
+
+        def some(j):
+            s = pl.ds(p * piece + j * 4, 4)
+            out[s] = finish(f32(own[chip, s]) + f32(prt[chip, s]) + incoming(s))
+
+        each(some, piece // 4)
+
+    @on_mid
+    def _():
+        for i in range(2):
+            load(far(i)).wait()
+            load(near(i)).wait()
+
+        def first(q):
+            i, p = q // pieces, lax.rem(q, pieces)
+            for core in range(2):
+                raw_recv(i, core, p).wait_recv()
+            add(far(i), p, lambda s: f32(raw[i, 0, s]) + f32(raw[i, 1, s]), fout.at[i])
+            f_copy(i, p, 0).start()
+
+        def second(q):
+            i, p = q // pieces, lax.rem(q, pieces)
+            f_copy(i, p, 0).wait_recv()
+            add(near(i), p, lambda s: fin[i, s], fout.at[2 + i])
+            f_copy(i, p, 1).start()
+
+        lag = 2
+
+        def step(q):
+            pl.when(q < 2 * pieces)(lambda: first(q))
+            pl.when(q >= lag)(lambda: second(q - lag))
+
+        each(step, 2 * pieces + lag)
+
+    @on_end
+    def _():
+        for i in range(2):
+            load(near(i)).wait()
+            if i == 0:
+                send_h.wait_recv()
+            h = h_ref if i else hs
+
+            def last(p):
+                f_copy(i, p, 1).wait_recv()
+                add(near(i), p, lambda s: fin[i, s] + f32(h[s]), yst.at[i], lambda v: v.astype(jnp.bfloat16))
+                src = yst.at[i, rows(p)]
+                for blk in range(4):
+                    for half in range(split):
+                        @pl.when(p == blk * split + half)
+                        def _():
+                            if i:
+                                put(src, blk, half)
+                            else:
+                                y_copy(src, i, blk, half, ep_at(z_mid, c)).start()
+
+            each(last)
+
+    @on_end
+    def _():
+        for i in range(2):
+            each(lambda p: [raw_send(i, core, p).wait_send() for core in range(2)])
+            each(lambda p: prt_copy(near(i), p).wait_send())
         for blk in range(4):
             for half in range(split):
-                @pl.when(p == blk * split + half)
-                def _():
-                    put(yst.at[rows(p)], blk, half)
-
-    @pl.when(is_mid)
+                y_copy(yst.at[0, rows(0)], 0, blk, half, ep_at(z_mid, c)).wait_send()
+
+    @on_mid
     def _():
-        loadown(h_a).wait()
-
-        def far(p):
-            raw_recv(0, 0, p).wait_recv()
-            raw_recv(0, 1, p).wait_recv()
-            onward(0, h_a, p, ((r, ep_at(z_oth, c)), 0), lambda s: f32(raw[0, 0, s]) + f32(raw[0, 1, s]))
-
-        loop(np_, far)
-        loadown(h_b).wait()
-        loadown(h_c).wait()
-
-        def near(p):
-            f_copy(2, 0, p, (r, ep_at(z_oth, c))).wait_recv()
-            onward(2, h_c, p, ((r, ep_at(z_end, c)), 0), lambda s: fin[0, s])
-            raw_recv(1, 0, p).wait_recv()
-            raw_recv(1, 1, p).wait_recv()
-            onward(1, h_b, p, ((r, ep_at(z_oth, c)), 1), lambda s: f32(raw[1, 0, s]) + f32(raw[1, 1, s]))
-
-        loop(np_, near)
-        loadown(z).wait()
-
-        def last(p):
-            f_copy(1, 1, p, (r, ep_at(z_oth, c))).wait_recv()
-            raw_recv(2, 0, p).wait_recv()
-            raw_recv(2, 1, p).wait_recv()
-            finish(p, lambda s: fin[1, s] + f32(raw[2, 0, s]) + f32(raw[2, 1, s]))
-
-        loop(np_, last)
-
-    @pl.when(is_end)
-    def _():
-        loadown(z).wait()
-
-        def last(p):
-            f_copy(2, 0, p, (r, ep_at(z_mid, c))).wait_recv()
-            finish(p, lambda s: fin[0, s])
-
-        loop(np_, last)
-
-    @pl.when(is_end)
-    def _():
-        def sent(p):
-            for i in range(3):
-                for c2 in range(2):
-                    raw_send(i, c2, p).wait_send()
-            prt_copy(z, p).wait_send()
-
-        loop(np_, sent)
-
-    @pl.when(is_mid)
-    def _():
-        def sent(p):
-            for hh in (h_a, h_b, h_c, z):
-                prt_copy(hh, p).wait_send()
-            f_copy(0, 0, p, (r, ep_at(z_oth, c))).wait_send()
-            f_copy(1, 1, p, (r, ep_at(z_oth, c))).wait_send()
-            f_copy(2, 0, p, (r, ep_at(z_end, c))).wait_send()
-
-        loop(np_, sent)
+        send_h.wait_send()
+        for i in range(2):
+            each(lambda p: [prt_copy(far(i), p).wait_send(), prt_copy(near(i), p).wait_send(),
+                            f_copy(i, p, 0).wait_send(), f_copy(i, p, 1).wait_send()])
 
     for blk in range(4):
         for half in range(-1, split):
-            some = ya.at[blk] if half < 0 else yst.at[rows(0)]
-
-            @pl.when(r == blk)
-            def _():
-                y_local(some, half).wait()
-
-            @pl.when(r != blk)
-            def _():
-                y_copy(some, blk, half).wait_send()
-                ref = y_out.at[blk, place(half)]
-                rcopy(ref, ref, y_s.at[blk, half + 1], y_r.at[blk, half + 1], (blk, e)).wait_recv()
+            src = ya.at[blk] if half < 0 else yst.at[1, rows(0)]
+            ref = y_out.at[blk, place(half)]
+            came = rcopy(ref, ref, y_s.at[1, blk, half + 1], y_r.at[blk, half + 1], (blk, e))
+            sent_here = True if half < 0 else end
+
+            def kept():
+                y_local(src, half).wait()
+
+            def sent():
+                y_copy(src, 1, blk, half, e).wait_send()
+
+            pl.when((r == blk) & sent_here)(kept)
+            pl.when((r != blk) & sent_here)(sent)
+            pl.when((r != blk) | jnp.logical_not(sent_here))(came.wait_recv)
 
 
 def back(part, h, ya):
@@ -750,10 +730,10 @@
     vmem = pl.BlockSpec(memory_space=pltpu.VMEM)
     hbm = pl.BlockSpec(memory_space=pl.ANY)
     dma = pltpu.SemaphoreType.DMA
-    np_ = n // piece
-
-    def tiles(lead, dtype):
-        return pltpu.VMEM(lead + (cols, LANES), dtype)
+    pieces = n // piece
+
+    def tiles(*lead, dtype=jnp.bfloat16):
+        return pltpu.VMEM(lead + (n, cols, LANES), dtype)
 
     return pl.pallas_call(
         functools.partial(back_kernel, cut, piece),
@@ -761,10 +741,9 @@
         in_specs=[hbm, vmem, hbm],
         out_specs=hbm,
         scratch_shapes=[
-            tiles((4, n), jnp.bfloat16), tiles((4, n), jnp.bfloat16), tiles((3, 2, n), jnp.bfloat16),
-            tiles((2, n), jnp.float32), tiles((3, n), jnp.float32), tiles((n,), jnp.bfloat16),
-            dma((3, 2, np_)), dma((3, 2, np_)), dma((4, np_)), dma((4, np_)), dma((3, np_)), dma((2, np_)),
-            dma((4, 3)), dma((4, 3)), dma((4,)), dma((3,)),
+            tiles(4), tiles(4), tiles(2, 2), tiles(2, dtype=jnp.float32), tiles(4, dtype=jnp.float32), tiles(), tiles(2),
+            *([dma((2, 2, pieces))] * 2), *([dma((4, pieces))] * 2), dma((4, pieces)), dma((2, pieces)),
+            dma, dma, dma((2, 4, 3)), dma((4, 3)), dma((4,)), dma((3,)),
         ],
         compiler_params=pltpu.CompilerParams(collective_id=1, has_side_effects=True, vmem_limit_bytes=58 * 1024 * 1024),
     )(part, h, ya)
@@ -816,17 +795,20 @@
         cols = d // LANES
         ua, ub, ha, hb, ids = attention(x, idx.transpose(0, 2, 1), wr, wq, wk, wv, wo, cut)
 
-        def experts(u, gates, lo, hi):
+        def experts(u, gates, plan, lo, hi):
             n = b * (hi - lo)
-            plan = block_plan(ids[..., lo:hi], me, ne)
             return moe(*plan, gates[..., lo:hi].reshape(-1), u, n, w1, w3, w2).reshape(nd, n, cols, LANES)
 
+        plan_a, plan_b = block_plan(ids[..., :cut], me, ne), block_plan(ids[..., cut:], me, ne)
         u_all = lax.all_gather(ua, 'ep', axis=0, tiled=False)
+        u_all, plan_b = lax.optimization_barrier((u_all, plan_b))
         terms = u_all[:, b * cut:].reshape(nd, 3, b, k, s).astype(jnp.float32)
         gates = terms[:, 0] + terms[:, 1] + terms[:, 2]
-        part_a = experts(u_all, gates, 0, cut)
+        part_a = experts(u_all, gates, plan_a, 0, cut)
+        ub_all = lax.all_gather(ub, 'ep', axis=0, tiled=False)
+        part_a, ub_all = lax.optimization_barrier((part_a, ub_all))
         part_a = lax.all_to_all(part_a, 'ep', 0, 0, tiled=True)
-        part_b = experts(lax.all_gather(ub, 'ep', axis=0, tiled=False), gates, cut, s)
+        part_b = experts(ub_all, gates, plan_b, cut, s)
         ya = ha.astype(jnp.float32) + jnp.sum(part_a.astype(jnp.float32), axis=0)
         y = back(part_b, hb, ya.astype(jnp.bfloat16).reshape(b, cut, cols, LANES))
         return y.reshape(b, s, d)

time: 788 us -> 768 us (0.975)
  Pallas kernels: 626 us -> 614 us
  starting transfers between devices: 14.7 us -> 4.89 us
    all_gather x1, waiting for transfers between devices: 0.01 us -> 37.1 us  [local(): ub_all = lax.all_gather(ub, 'ep', axis=0, tiled=False)]
    all_gather x1, waiting for transfers between devices: 59 us -> 38.7 us  [local(): u_all = lax.all_gather(ua, 'ep', axis=0, tiled=False)]
    all_to_all x1, waiting for transfers between devices: 33.1 us -> 20.1 us  [local(): part_a = lax.all_to_all(part_a, 'ep', 0, 0, tiled=True)]
    all_to_all x1, starting transfers between devices: 14.7 us -> 4.85 us  [local(): part_a = lax.all_to_all(part_a, 'ep', 0, 0, tiled=True)]
  transfers between devices with their start and end apart: 3 -> 3, of which waited for: 2 -> 3; matrix products, arithmetic and copies ran while one was open for 3% -> 3% of each run, Pallas kernels for 22% -> 22%
where the time goes in v5:
time: 768 us; the launch traced here: 764 us
  Pallas kernels  614 us (80%)
  waiting for transfers between devices  96.6 us (13%)
  other arithmetic  25.6 us (3%)
  between operations  13.6 us (2%)
  local copies, waits for them, and re-layouts  8.52 us (1%)
    pallas_call x1, Pallas kernels, attention(): pl.pallas_call(functools.partial(attn_kernel, cut), out_shape=(out(na + 3...  280 us
    pallas_call x1, Pallas kernels, back(): pl.pallas_call(functools.partial(back_kernel, cut, piece), out_shape=jax....  169 us
    pallas_call x2, Pallas kernels, moe(): pl.pallas_call(functools.partial(moe_kernel, nt), out_shape=jax.ShapeDtyp...  165 us
    all_gather x1, waiting for transfers between devices, local(): u_all = lax.all_gather(ua, 'ep', axis=0, tiled=False)  38.7 us
    all_gather x1, waiting for transfers between devices, local(): ub_all = lax.all_gather(ub, 'ep', axis=0, tiled=False)  37.1 us
    all_to_all x1, waiting for transfers between devices, local(): part_a = lax.all_to_all(part_a, 'ep', 0, 0, tiled=True)  20.1 us
  transfers between devices with their start and end apart: 3, of which 3 were waited for; matrix products, arithmetic and copies ran while one was open for 3% of the time, Pallas kernels for 22%

profile of v5, /device:TPU:0, one launch (start us, length us, event | category | flops | bytes accessed | tf_op | source)
XLA Modules:
  0.0 763.7 jit_solution(12978127730233635714)
XLA Ops:
  6.5 0.0 all-gather.5.cloned.1.call-start
  6.5 0.3 fusion.3
  6.8 0.7 pad_maximum_fusion
  7.6 280.2 %shard_map.100 = (bf16[166,16,128]{2,1,0:T(8,128)(2,1)}, bf16[352,16,128]{2,1,0:T(8,128)(2,1)}, bf16[160,16,128]{2,1,0:T(8,128)(2,1)}, bf16[352,16,128]{2,1,0:T(...) custom-call(bf16[4,128,2048]{2,1,0:T(8,128)(2,1)} %x_hbm.1, ...), custom_call_target="tpu_custom_call" | custom-call | flops 42949672960 | bytes 67108864 | tf_op jit(solution)/shard_map/pallas_call | solution.py:405
  287.8 0.0 copy-start.1
  287.8 0.0 all-gather.5.cloned.1.call-update
  287.8 0.0 all-gather.7.cloned.1.call-start
  287.9 0.7 all-gather.7.cloned.1.call-update
  288.6 0.1 copy-done.1
  288.7 0.1 or_select_fusion
  288.8 0.1 eq.48
  288.9 0.2 convert_reduce_fusion.2
  289.1 0.7 fusion.10
  289.8 0.1 select_reduce_fusion.9
  290.0 0.1 or_select_fusion.1
  290.1 0.1 eq.42
  290.2 0.3 convert_reduce_fusion.1
  290.5 0.7 fusion.12
  291.2 0.1 select_reduce_fusion.11
  291.3 0.1 reshape.140
  291.5 8.5 %sort.14 = s32[22528]{0:T(1024)S(1)} sort(s32[22528]{0:T(1024)S(1)} %reshape.140), dimensions={0}, to_apply=%region_9.10 | sort | flops 337920 | bytes 180224 | tf_op jit(solution)/shard_map/sort | solution.py:762
  300.0 0.1 reshape.151
  300.1 6.3 sort.15
  306.5 0.6 concatenate.14.key_ref
  307.1 0.6 concatenate.15.key_ref
  307.7 0.1 select_reduce_fusion.7
  307.8 0.1 select_reduce_fusion.10
  308.0 0.1 fusion.9
  308.1 0.1 fusion.8
  308.1 0.6 select_reduce_fusion.4
  308.8 0.7 select_reduce_fusion
  309.4 0.6 subtract_clamp_fusion.1
  310.0 0.6 subtract_clamp_fusion
  310.6 38.7 %all-gather.5.cloned.1.call-done = bf16[1328,16,128]{2,1,0:T(8,128)(2,1)} async-done(((bf16[166,16,128]{2,1,0:T(8,128)(2,1)}), bf16[1328,16,128]{2,1,0:T(8,128)(2,1)}) %all-gather.5.cloned.1.call-update) | async-done | bytes 5439504 | tf_op jit(solution)/shard_map/all_gather | solution.py:803
  349.4 0.9 slice.25
  350.4 0.7 reshape.152.gate_ref
  351.1 69.7 %shard_map.101 = bf16[1280,16,128]{2,1,0:T(8,128)(2,1)} custom-call(s32[1]{0:T(128)} %bitcast.6.nblk_ref, s32[98]{0:T(128)} %get-tuple-element.34.be_ref, s32[98]{0:T(128)} %get-tuple-element.50.bb_ref, s32[98]{0:T(128)} %get-tuple-element.49.bn_ref, s32[10368]{0:T(1024)} %concatenate.15.key_ref, f32[10240]{0:T(1024)} %reshape.152.gate_ref, ...), custom_call_target="tpu_custom_call" | custom-call | flops 47185920000 | bytes 150994944 | tf_op jit(solution)/shard_map/pallas_call | solution.py:522
  420.8 37.1 %all-gather.7.cloned.1.call-done = bf16[2816,16,128]{2,1,0:T(8,128)(2,1)} async-done(((bf16[352,16,128]{2,1,0:T(8,128)(2,1)}), bf16[2816,16,128]{2,1,0:T(8,128)(2,1)}) %all-gather.7.cloned.1.call-update) | async-done | bytes 11534352 | tf_op jit(solution)/shard_map/all_gather | solution.py:808
  457.8 4.8 all-to-all-start
  462.7 0.1 slice.35
  462.8 0.8 reshape.141.gate_ref
  463.5 95.5 %shard_map.102 = bf16[2816,16,128]{2,1,0:T(8,128)(2,1)} custom-call(s32[1]{0:T(128)} %bitcast.2.nblk_ref, s32[194]{0:T(256)} %get-tuple-element.21.be_ref, s32[194]{0:T(256)} %get-tuple-element.22.bb_ref, s32[194]{0:T(256)} %get-tuple-element.23.bn_ref, s32[22656]{0:T(1024)} %concatenate.14.key_ref, f32[22528]{0:T(1024)} %reshape.141.gate_ref, ...), custom_call_target="tpu_custom_call" | custom-call | flops 47185920000 | bytes 150994944 | tf_op jit(solution)/shard_map/pallas_call | solution.py:522
  559.0 0.0 copy-start
  559.0 20.1 %all-to-all-done = bf16[8,160,16,128]{3,2,1,0:T(8,128)(2,1)} async-done(((bf16[8,160,16,128]{3,2,1,0:T(8,128)(2,1)}), bf16[8,160,16,128]{3,2,1,0:T(8,128)(2,1)}, u32[]{:S(2)}, u32[]{:S(2)}) %all-to-all-start) | async-done | bytes 5242912 | tf_op jit(solution)/shard_map/all_to_all | solution.py:810
  579.1 3.3 convert_reduce_fusion
  582.5 0.0 copy-done
  582.5 1.0 add_convert_fusion
  583.5 169.2 %shard_map.103 = bf16[4,128,16,128]{3,2,1,0:T(8,128)(2,1)} custom-call(bf16[8,352,16,128]{3,2,1,0:T(8,128)(2,1)} %bitcast.27, bf16[352,16,128]{2,1,0:T(8,128)(2,1)} %get-tuple-element.28.h_ref, bf16[4,40,16,128]{3,2,1,0:T(8,128)(2,1)} %bitcast.29), custom_call_target="tpu_custom_call" | custom-call | tf_op jit(solution)/shard_map/pallas_call | solution.py:738
  752.7 4.2 reshape.156
  (8 shorter events, 0.1 us)
Async XLA Ops:
  6.5 342.8 %all-gather.5.cloned.1.call-start = ((), (), s32[]{:S(2)}) async-start(), calls=%async_computation.1 | async-start | bytes 6119424 | tf_op jit(solution)/shard_map/all_gather | solution.py:803
  287.8 0.9 copy-start.1
  287.8 170.0 %all-gather.7.cloned.1.call-start = ((), (), s32[]{:S(2)}) async-start(), calls=%async_computation.2 | async-start | bytes 12976128 | tf_op jit(solution)/shard_map/all_gather | solution.py:808
  457.8 121.3 %all-to-all-start = ((bf16[8,160,16,128]{3,2,1,0:T(8,128)(2,1)}), bf16[8,160,16,128]{3,2,1,0:T(8,128)(2,1)}, u32[]{:S(2)}, u32[]{:S(2)}) async-start(bf16[8,160,16,128]{3,2,1,0:T(8,128)(2,1)} %bitcast.28), calls=%async_computation | async-start | bytes 10485760 | tf_op jit(solution)/shard_map/all_to_all | solution.py:810
  559.0 23.5 %copy-start = (bf16[160,16,128]{2,1,0:T(8,128)(2,1)S(1)}, bf16[160,16,128]{2,1,0:T(8,128)(2,1)}, u32[]{:S(2)}) copy-start(bf16[160,16,128]{2,1,0:T(8,128)(2,1)} %get-tuple-element.29) | copy-start | bytes 1966084
Sparse Core Ops, SparseCore 0:
  287.9 61.3 all-gather.4
  351.0 106.7 all-gather.6

commit v6 on v5

--- a/solution.py
+++ b/solution.py
@@ -12,7 +12,10 @@
 BM = 128
 PITCH = BM + 1
 LANES = 128
-CUT = 40
+CORES = 2
+REPLICAS = 4
+CUT = 56
+RET = 32
 STEPS = 8
 SLOT_BITS, TOKEN_BITS = 15, 12
 
@@ -23,6 +26,10 @@
         return carry
 
     lax.fori_loop(0, n, step, 0)
+
+
+def kept(fn, v, axis=-1):
+    return fn(v, axis=axis, keepdims=True)
 
 
 def ep_at(z, c):
@@ -50,7 +57,7 @@
     pl.semaphore_wait(barrier, count)
 
 
-def attn_kernel(cut, x_hbm, idt_hbm, cos_ref, sin_ref, wr_ref, wq_ref, wk_ref, wv_ref, wo_ref,
+def attn_kernel(cut, ret, x_hbm, idt_hbm, cos_ref, sin_ref, wr_ref, wq_ref, wk_ref, wv_ref, wo_ref,
                 ua_ref, ub_ref, ha_ref, hb_ref, ids_out, gw, go,
                 xg, a_ref, acc, wbuf, obuf, tm, gates, idv, zr, zp, zm, xr, yr, xs, ys, xd, yd, dr, pr, ps,
                 x_s, x_r, i_s, i_r, j_s, j_r, lsem, csem):
@@ -58,8 +65,23 @@
     nz, nq = 4, 4
     z, c = e // 2, e % 2
     e_p = ep_at(z, 1 - c)
-    r_x, r_y = (r + 2) % nq, r + 1 - 2 * (r % 2)
-    r_d = (r_y + 2) % nq
+    x, y = r // 2, r % 2
+    r_x, r_y = (r + 2) % nq, r + 1 - 2 * y
+
+    def line_quarter(x, y):
+        return 2 - y + x * (4 * y - 2)
+
+    mine = line_quarter(x, y)
+    q_line = (mine, line_quarter(1 - x, y), line_quarter(x, 1 - y), line_quarter(1 - x, 1 - y))
+    to_x, to_y = 2 + x, y
+    q_pair = (mine, 3 - x, 1 - y, to_x + to_y - mine)
+
+    def pairs(w, k):
+        return w == 0 and k == 0
+
+    def quarters(w, k):
+        return q_pair if pairs(w, k) else q_line
+
     nd = ids_out.shape[0]
     rows, wide = wq_ref.shape[0], wq_ref.shape[1] // STEPS
     quarter = rows // nq
@@ -98,7 +120,7 @@
         def norm(b):
             x = xg[b].astype(jnp.float32)
             at = pl.ds(b * seq, seq)
-            a_ref[at, :] = (x * lax.rsqrt(jnp.mean(x * x, axis=-1, keepdims=True) + EPS)).astype(jnp.bfloat16)
+            a_ref[at, :] = (x * lax.rsqrt(kept(jnp.mean, x * x) + EPS)).astype(jnp.bfloat16)
             acc[at, :] = x
 
         loop(nseq, norm)
@@ -118,9 +140,10 @@
     def own_wo(s, lo, n):
         return wo_ref.at[pl.ds(mod(s, per) * orows + lo, n), :]
 
-    def z_send(w, s, zs, up):
-        ref = piece(w, s, ep_at(zs, c), r)
-        return rcopy(ref, ref, (zp if up else zm).at[w, s, zs], zr.at[w, s, zs], (r, e + 2) if up else (r, e - 2))
+    def z_send(w, s, zs, up, second=0):
+        ref = piece(w, s, ep_at(zs, c), q_pair[3] if second else mine)
+        i = 2 if second else w
+        return rcopy(ref, ref, (zp if up else zm).at[i, s, zs], zr.at[i, s, zs], (r, e + 2) if up else (r, e - 2))
 
     def xy_send(w, s, zs, q, ssem, rsem, dev):
         ref = piece(w, s, ep_at(zs, c), q)
@@ -134,8 +157,8 @@
         ref = half(w, s, zs, q, 0)
         return rcopy(ref, ref, yd.at[w, s, zs], dr.at[0, w, s, zs], y_dev)
 
-    def p_copy(w, s, zs, j, core):
-        ref = piece(w, s, ep_at(zs, core), (r, r_x, r_y, r_d)[j])
+    def p_copy(w, s, zs, k, j, core):
+        ref = piece(w, s, ep_at(zs, core), quarters(w, k)[j])
         return rcopy(ref, ref, ps.at[w, s, zs, j], pr.at[w, s, zs, j], partner)
 
     def p_whole(w, s, f):
@@ -163,10 +186,11 @@
         def line(up):
             sem = zp if up else zm
             dev = (r, e + 2) if up else (r, e - 2)
-            for w, m in own_parts(s):
-                rcopy(w.at[pl.ds(r * quarter, quarter), :], gw.at[s, m, pl.ds(e * rows + r * quarter, quarter), :],
-                      sem.at[0, s, z], zr.at[0, s, z], dev).start()
-            if_wo(s, e, lambda: rcopy(own_wo(s, r * (orows // nq), orows // nq), piece(1, s, e, r), sem.at[1, s, z],
+            for i, q in ((0, mine), (2, q_pair[3])):
+                for w, m in own_parts(s):
+                    rcopy(w.at[pl.ds(q * quarter, quarter), :], gw.at[s, m, pl.ds(e * rows + q * quarter, quarter), :],
+                          sem.at[i, s, z], zr.at[i, s, z], dev).start()
+            if_wo(s, e, lambda: rcopy(own_wo(s, mine * (orows // nq), orows // nq), piece(1, s, e, mine), sem.at[1, s, z],
                                       zr.at[1, s, z], dev).start())
 
         each_line(line)
@@ -184,9 +208,12 @@
             def one(w):
                 z_send(w, s, zs, up).wait_recv()
                 pl.when(z < nz - 1 if up else z > 0)(lambda: z_send(w, s, zs, up).start())
-                xy_send(w, s, zs, r, xs, xr, x_dev).start()
-                xy_send(w, s, zs, r, ys, yr, y_dev).start()
-                p_copy(w, s, zs, 0, c).start()
+                if pairs(w, k):
+                    z_send(w, s, zs, up, 1).wait_recv()
+                    p_copy(w, s, zs, k, 3, c).start()
+                xy_send(w, s, zs, to_x if pairs(w, k) else mine, xs, xr, x_dev).start()
+                xy_send(w, s, zs, to_y if pairs(w, k) else mine, ys, yr, y_dev).start()
+                p_copy(w, s, zs, k, 0, c).start()
 
             for_both(s, ep_at(zs, c), one)
 
@@ -195,12 +222,15 @@
     def across(s, k):
         def side(zs, up):
             def one(w):
-                xy_send(w, s, zs, r_x, xs, xr, x_dev).wait_recv()
-                yd_send(w, s, zs, r_x).start()
-                p_copy(w, s, zs, 1, c).start()
-                xy_send(w, s, zs, r_y, ys, yr, y_dev).wait_recv()
-                xd_send(w, s, zs, r_y).start()
-                p_copy(w, s, zs, 2, c).start()
+                q = quarters(w, k)
+                xy_send(w, s, zs, q[1], xs, xr, x_dev).wait_recv()
+                if not pairs(w, k):
+                    yd_send(w, s, zs, q[1]).start()
+                p_copy(w, s, zs, k, 1, c).start()
+                xy_send(w, s, zs, q[2], ys, yr, y_dev).wait_recv()
+                if not pairs(w, k):
+                    xd_send(w, s, zs, q[2]).start()
+                p_copy(w, s, zs, k, 2, c).start()
 
             for_both(s, ep_at(zs, c), one)
 
@@ -209,9 +239,10 @@
     def diagonal(s, k):
         def side(zs, up):
             def one(w):
-                xd_send(w, s, zs, r_d).wait_recv()
-                yd_send(w, s, zs, r_d).wait_recv()
-                p_copy(w, s, zs, 3, c).start()
+                if not pairs(w, k):
+                    xd_send(w, s, zs, q_line[3]).wait_recv()
+                    yd_send(w, s, zs, q_line[3]).wait_recv()
+                    p_copy(w, s, zs, k, 3, c).start()
 
             for_both(s, ep_at(zs, c), one)
 
@@ -230,15 +261,15 @@
         slot = mod(s, 2)
         whole = go.at[pl.ds(s * orows, orows), :]
 
-        def side(zs, up):
+        def side(k, zs):
             def one(w):
                 for j in range(nq):
-                    p_copy(w, s, zs, j, 1 - c).wait_recv()
+                    p_copy(w, s, zs, k, j, 1 - c).wait_recv()
 
             for_both(s, ep_at(zs, 1 - c), one)
 
         for k in range(nz - 1):
-            each_side(k, side)
+            each_side(k, lambda zs, up: side(k, zs))
         p_whole(0, s, e_p).wait_recv()
         if_wo(s, e_p, lambda: p_whole(1, s, e_p).wait_recv())
 
@@ -273,7 +304,7 @@
         v = v.astype(jnp.bfloat16)
         tri = lax.broadcasted_iota(jnp.int32, (seq, seq), 0) >= lax.broadcasted_iota(jnp.int32, (seq, seq), 1)
         heads = []
-        for hh in range(2):
+        for hh in range(CORES):
             hc = slice(hh * HEAD, (hh + 1) * HEAD)
             outs = []
             for b in range(nseq):
@@ -281,8 +312,8 @@
                 sc = lax.dot_general(rot(q[rs, hc]), rot(k[rs, hc]), (((1,), (1,)), ((), ())),
                                      preferred_element_type=jnp.float32)
                 sc = jnp.where(tri, sc * HEAD ** -0.5, -jnp.inf)
-                ex = jnp.exp(sc - jnp.max(sc, axis=-1, keepdims=True))
-                p = (ex / jnp.sum(ex, axis=-1, keepdims=True)).astype(jnp.bfloat16)
+                ex = jnp.exp(sc - kept(jnp.max, sc))
+                p = (ex / kept(jnp.sum, ex)).astype(jnp.bfloat16)
                 outs.append(jnp.dot(p, v[rs, hc], preferred_element_type=jnp.float32).astype(jnp.bfloat16))
             heads.append(jnp.concatenate(outs, axis=0))
         o = jnp.concatenate(heads, axis=1)
@@ -297,9 +328,9 @@
         within(i + 1, originate)
         within(i - 3, wait_loads)
         for k in range(nz - 1):
+            within(i - 2, diagonal, k)
+            within(i - 1, across, k)
             within(i, along_z, k)
-            within(i - 1, across, k)
-            within(i - 2, diagonal, k)
             if k < npair:
                 within(i - 3, compute, k)
         within(i - 2, collect)
@@ -314,7 +345,7 @@
     pitch = d // LANES + 1
     tile = pl.ds(0, d // LANES)
 
-    def spill(v, to_a, to_b, b):
+    def spill(v, *parts):
         for k in range(d // LANES):
             tm[pl.ds(k, seq, stride=pitch), :] = v[:, k * LANES:(k + 1) * LANES]
 
@@ -326,21 +357,22 @@
 
             return some
 
-        loop(cut // 8, rows_to(to_a, b * cut, 0))
-        loop((seq - cut) // 8, rows_to(to_b, b * (seq - cut), cut))
+        for ref, base, lo, hi in parts:
+            loop((hi - lo) // 8, rows_to(ref, base, lo))
 
     def route(b):
         h = acc[pl.ds(b * seq, seq), :].astype(jnp.bfloat16).astype(jnp.float32)
-        n = h * lax.rsqrt(jnp.mean(h * h, axis=-1, keepdims=True) + EPS)
+        n = h * lax.rsqrt(kept(jnp.mean, h * h) + EPS)
         logits = jnp.dot(n, wr_ref[...], precision=lax.Precision.HIGHEST, preferred_element_type=jnp.float32).T
         expert = lax.broadcasted_iota(jnp.int32, logits.shape, 0)
         ids = idv[b]
         picked = jnp.concatenate([jnp.sum(jnp.where(expert == ids[k:k + 1, :], logits, 0.0), axis=0, keepdims=True)
                                   for k in range(ids.shape[0])], axis=0)
-        ex = jnp.exp(picked - jnp.max(picked, axis=0, keepdims=True))
-        gates[b] = ex / jnp.sum(ex, axis=0, keepdims=True)
-        spill(n, ua_ref, ub_ref, b)
-        spill(h, ha_ref, hb_ref, b)
+        ex = jnp.exp(picked - kept(jnp.max, picked, 0))
+        gates[b] = ex / kept(jnp.sum, ex, 0)
+        rest, tail = seq - cut, cut - ret
+        spill(n, (ua_ref, b * cut, 0, cut), (ub_ref, b * rest, cut, seq))
+        spill(h, (ha_ref, b * ret, 0, ret), (hb_ref, b * tail, ret, cut), (hb_ref, nseq * tail + b * rest, cut, seq))
 
     loop(nseq, route)
     left = gates[...].reshape(-1, LANES)
@@ -358,31 +390,33 @@
         rcopy(x_hbm.at[q], xg.at[r], x_s.at[i], x_r.at[r], (q, e)).wait_send()
 
     def drain(s):
-        def side(zs, up):
+        def side(k, zs, up):
             def sent(w):
                 pl.when(z < nz - 1 if up else z > 0)(lambda: z_send(w, s, zs, up).wait_send())
                 for j in range(nq):
-                    p_copy(w, s, zs, j, c).wait_send()
-                xy_send(w, s, zs, r, xs, xr, x_dev).wait_send()
-                xy_send(w, s, zs, r, ys, yr, y_dev).wait_send()
-                xd_send(w, s, zs, r_y).wait_send()
-                yd_send(w, s, zs, r_x).wait_send()
+                    p_copy(w, s, zs, k, j, c).wait_send()
+                xy_send(w, s, zs, mine, xs, xr, x_dev).wait_send()
+                xy_send(w, s, zs, mine, ys, yr, y_dev).wait_send()
+                if not pairs(w, k):
+                    xd_send(w, s, zs, mine).wait_send()
+                    yd_send(w, s, zs, mine).wait_send()
 
             for_both(s, ep_at(zs, c), sent)
 
         for k in range(nz - 1):
-            each_side(k, side)
+            each_side(k, lambda zs, up: side(k, zs, up))
 
         def own(w):
             each_line(lambda up: z_send(w, s, z, up).wait_send())
             p_whole(w, s, e).wait_send()
 
         for_both(s, e, own)
+        each_line(lambda up: z_send(0, s, z, up, 1).wait_send())
 
     loop(STEPS, drain)
 
 
-def attention(x, idt, wr, wq, wk, wv, wo, cut):
+def attention(x, idt, wr, wq, wk, wv, wo, cut, ret):
     nseq, seq, d = x.shape
     rows, hd = wq.shape
     nd, k = d // rows, idt.shape[1]
@@ -403,9 +437,9 @@
 
     na, nb = nseq * cut, nseq * (seq - cut)
     return pl.pallas_call(
-        functools.partial(attn_kernel, cut),
-        out_shape=(out(na + 3 * nseq * k // cols, cols, LANES), out(nb, cols, LANES), out(na, cols, LANES),
-                   out(nb, cols, LANES), out(nd, nseq, k, seq, dtype=jnp.int32), out(STEPS, 3, d, wide), out(hd, d)),
+        functools.partial(attn_kernel, cut, ret),
+        out_shape=(out(na + 3 * nseq * k // cols, cols, LANES), out(nb, cols, LANES),
+                   out(nseq * ret, cols, LANES), out(nseq * (seq - ret), cols, LANES), out(nd, nseq, k, seq, dtype=jnp.int32), out(STEPS, 3, d, wide), out(hd, d)),
         in_specs=[hbm, hbm] + [vmem] * 3 + [hbm] * 4,
         out_specs=(vmem, vmem, vmem, vmem, hbm, hbm, hbm),
         scratch_shapes=[
@@ -413,7 +447,7 @@
             pltpu.VMEM((2, 3, d, wide), bf), pltpu.VMEM((2, hd // STEPS, d), bf),
             pltpu.VMEM((seq * (cols + 1), LANES), jnp.float32), pltpu.VMEM((nseq, k, seq), jnp.float32),
             pltpu.VMEM((nseq, k, seq), jnp.int32),
-            *([dma((2, STEPS, 4))] * 9), dma((2, 2, STEPS, 4)), *([dma((2, STEPS, 4, 4))] * 2),
+            *([dma((3, STEPS, 4))] * 3), *([dma((2, STEPS, 4))] * 6), dma((2, 2, STEPS, 4)), *([dma((2, STEPS, 4, 4))] * 2),
             *([dma((4,))] * 4), *([dma((nd,))] * 2), dma((2, nd + 1)), dma((2,)),
         ],
         compiler_params=pltpu.CompilerParams(collective_id=0, has_side_effects=True, vmem_limit_bytes=58 * 1024 * 1024),
@@ -425,8 +459,8 @@
     return lax.shift_right_logical(key, SLOT_BITS) & ((1 << TOKEN_BITS) - 1)
 
 
-def moe_kernel(nt, nblk_ref, be_ref, bb_ref, bn_ref, key_ref, gate_ref, u_hbm, w1_hbm, w3_hbm, w2_hbm,
-               out_hbm, ub, acc, w1, w3, w2, xs, zs, lhs, usem, wsem, osem):
+def moe_kernel(nt, stores, given, nblk_ref, be_ref, bb_ref, bn_ref, key_ref, gate_ref, u_hbm, w1_hbm, w3_hbm, w2_hbm, *refs):
+    outs, (ub, acc, w1, w3, w2, xs, zs, lhs, usem, wsem, osem) = refs[given:-11], refs[-11:]
     cols = ub.shape[1]
     nexp = w1_hbm.shape[0]
     nblk = nblk_ref[0]
@@ -498,9 +532,8 @@
         return e
 
     lax.fori_loop(0, nblk, body, -1)
-    base, n = bb_ref[nblk - 1], bn_ref[nblk - 1]
     for i in range(0, BM, 8):
-        scatter(base, n, range(i, i + 8))
+        scatter(bb_ref[nblk - 1], bn_ref[nblk - 1], range(i, i + 8))
 
     def pack(i):
         for j in range(8):
@@ -508,22 +541,29 @@
             ub[t] = acc[t].astype(jnp.bfloat16)
 
     loop(nt // 8, pack)
-    store = pltpu.make_async_copy(ub.at[pl.ds(0, nt)], out_hbm, osem)
-    store.start()
-    store.wait()
-
-
-def moe(nblk, be, bb, bn, keys, gates, u, n, w1, w3, w2):
+
+    def store(i):
+        dev, b = i // 4, lax.rem(i, 4)
+        for out, lo, hi, base in stores:
+            pltpu.make_async_copy(ub.at[pl.ds(i * (n // 4) + lo, hi - lo)],
+                                  outs[out].at[dev, pl.ds(base + b * (hi - lo), hi - lo)], osem).start()
+
+    loop(nd * 4, store)
+    pltpu.make_async_copy(ub.at[pl.ds(0, nt)], ub.at[pl.ds(0, nt)], osem).wait()
+
+
+def moe(nblk, be, bb, bn, keys, gates, u, n, w1, w3, w2, lengths, stores, *into):
     nd, _, cols, _ = u.shape
     nt = nd * n
     ne, d, f = w1.shape
     smem = pl.BlockSpec(memory_space=pltpu.SMEM)
     hbm = pl.BlockSpec(memory_space=pl.ANY)
     return pl.pallas_call(
-        functools.partial(moe_kernel, nt),
-        out_shape=jax.ShapeDtypeStruct((nt, cols, LANES), jnp.bfloat16),
-        in_specs=[smem] * 6 + [hbm] * 4,
-        out_specs=hbm,
+        functools.partial(moe_kernel, nt, stores, len(into)),
+        out_shape=[jax.ShapeDtypeStruct((nd, m, cols, LANES), jnp.bfloat16) for m in lengths],
+        in_specs=[smem] * 6 + [hbm] * (4 + len(into)),
+        out_specs=[hbm] * len(lengths),
+        input_output_aliases={10 + i: i for i in range(len(into))},
         scratch_shapes=[
             pltpu.VMEM((nt + 8, cols, LANES), jnp.bfloat16),
             pltpu.VMEM((nt + 8, cols, LANES), jnp.float32),
@@ -539,16 +579,17 @@
         ],
         compiler_params=pltpu.CompilerParams(vmem_limit_bytes=60 * 1024 * 1024),
         cost_estimate=pl.CostEstimate(flops=6 * 5000 * d * f, bytes_accessed=ne * 3 * d * f * 2, transcendentals=0),
-    )(nblk, be, bb, bn, keys, gates, u, w1, w3, w2)
-
-
-def back_kernel(cut, piece, part, h_ref, ya, y_out, own, prt, raw, fin, fout, hs, yst, raw_s, raw_r, prt_s, prt_r, f_s, f_r,
-                h_s, h_r, y_s, y_r, osem, lsem):
+    )(nblk, be, bb, bn, keys, gates, u, w1, w3, w2, *into)
+
+
+def back_kernel(ret, piece, part, h_ref, h_mid, raw_here, raw_cross, ya, y_out, own, prt, raw, fin, fout, hs, yst, raw_s, raw_r,
+                prt_s, prt_r, f_s, f_r, y_s, y_r, osem, lsem, csem):
     r, e = lax.axis_index('replica'), lax.axis_index('ep')
     z, c = e // 2, e % 2
     n = h_ref.shape[0]
     pieces = n // piece
     split = pieces // 4
+    early = 4
     mid = (z + 2) // 3 + (5 - z) // 3 - 1
     low = z // 2
     on_mid, on_end = pl.when(mid == 1), pl.when(mid == 0)
@@ -568,8 +609,8 @@
 
     end, inner = mid == 0, mid == 1
     meet([(None, (q, e)) for q in others] + [(None, partner)] +
-         [(end, (q, ep_at(z_mid, c))) for q in range(4)] + [(end, (r, ep_at(z_mid, 1 - c)))] +
-         [(inner, (q, ep_at(z_end, c))) for q in range(4)] + [(inner, (r, ep_at(z_end, 1 - c))), (inner, across)], 9 + mid)
+         [(end, (q, ep_at(z_mid, c))) for q in range(REPLICAS)] + [(end, (r, ep_at(z_mid, 1 - c)))] +
+         [(inner, (q, ep_at(z_end, c))) for q in range(REPLICAS)] + [(inner, (r, ep_at(z_end, 1 - c))), (inner, across)], 9 + mid)
 
     def raw_send(i, core, p):
         return rcopy(part.at[ep_at(far(i), core), rows(p)], raw.at[i, c, rows(p)], raw_s.at[i, core, p], raw_r.at[i, c, p],
@@ -589,10 +630,16 @@
     def load(chip):
         return pltpu.make_async_copy(part.at[ep_at(chip, c)], own.at[chip], osem.at[chip])
 
-    send_h = rcopy(h_ref, hs, h_s, h_r, to_end)
+    def landed(i):
+        j = i + low * (1 - 2 * i)
+        rest = pl.ds(0, early * piece)
+        return (pltpu.make_async_copy(raw_here.at[j], raw.at[i, c, rest], csem.at[i, 0]),
+                pltpu.make_async_copy(raw_cross.at[j], raw.at[i, 1 - c, rest], csem.at[i, 1]))
+
+    keep_h = pltpu.make_async_copy(h_mid, hs, csem.at[0, 0])
 
     def place(half):
-        return pl.ds(0, cut) if half < 0 else pl.ds(cut + half * piece, piece)
+        return pl.ds(0, ret) if half < 0 else pl.ds(ret + half * piece, piece)
 
     def y_copy(src, i, blk, half, f):
         return rcopy(src, y_out.at[r, place(half)], y_s.at[i, blk, half + 1], y_r.at[r, half + 1], (blk, f))
@@ -607,23 +654,25 @@
     def each(fn, count=pieces):
         loop(count, fn)
 
-    for i in range(2):
+    for i in range(CORES):
         load(near(i)).start()
 
     @on_end
     def _():
-        for i in range(2):
-            each(lambda p: [raw_send(i, core, p).start() for core in range(2)])
+        keep_h.start()
+        for i in range(CORES):
+            each(lambda p: [raw_send(i, core, p + early).start() for core in range(CORES)], pieces - early)
             each(lambda p: prt_copy(near(i), p).start())
 
     @on_mid
     def _():
-        send_h.start()
-        for i in range(2):
+        for i in range(CORES):
+            for copy in landed(i):
+                copy.start()
             load(far(i)).start()
             each(lambda p: [prt_copy(far(i), p).start(), prt_copy(near(i), p).start()])
 
-    for blk in range(4):
+    for blk in range(REPLICAS):
         put(ya.at[blk], blk, -1)
 
     def f32(v):
@@ -640,14 +689,15 @@
 
     @on_mid
     def _():
-        for i in range(2):
+        for i in range(CORES):
             load(far(i)).wait()
             load(near(i)).wait()
+            for copy in landed(i):
+                copy.wait()
 
         def first(q):
             i, p = q // pieces, lax.rem(q, pieces)
-            for core in range(2):
-                raw_recv(i, core, p).wait_recv()
+            pl.when(p >= early)(lambda: [raw_recv(i, core, p).wait_recv() for core in range(CORES)][0])
             add(far(i), p, lambda s: f32(raw[i, 0, s]) + f32(raw[i, 1, s]), fout.at[i])
             f_copy(i, p, 0).start()
 
@@ -667,19 +717,19 @@
 
     @on_end
     def _():
-        for i in range(2):
+        for i in range(CORES):
             load(near(i)).wait()
             if i == 0:
-                send_h.wait_recv()
+                keep_h.wait()
             h = h_ref if i else hs
 
             def last(p):
                 f_copy(i, p, 1).wait_recv()
                 add(near(i), p, lambda s: fin[i, s] + f32(h[s]), yst.at[i], lambda v: v.astype(jnp.bfloat16))
                 src = yst.at[i, rows(p)]
-                for blk in range(4):
+                for blk in range(REPLICAS):
                     for half in range(split):
-                        @pl.when(p == blk * split + half)
+                        @pl.when(p == (early + blk * (split - 1) + half - 1 if half else blk))
                         def _():
                             if i:
                                 put(src, blk, half)
@@ -690,63 +740,63 @@
 
     @on_end
     def _():
-        for i in range(2):
-            each(lambda p: [raw_send(i, core, p).wait_send() for core in range(2)])
+        for i in range(CORES):
+            each(lambda p: [raw_send(i, core, p + early).wait_send() for core in range(CORES)], pieces - early)
             each(lambda p: prt_copy(near(i), p).wait_send())
-        for blk in range(4):
+        for blk in range(REPLICAS):
             for half in range(split):
                 y_copy(yst.at[0, rows(0)], 0, blk, half, ep_at(z_mid, c)).wait_send()
 
     @on_mid
     def _():
-        send_h.wait_send()
-        for i in range(2):
+        for i in range(CORES):
             each(lambda p: [prt_copy(far(i), p).wait_send(), prt_copy(near(i), p).wait_send(),
                             f_copy(i, p, 0).wait_send(), f_copy(i, p, 1).wait_send()])
 
-    for blk in range(4):
+    for blk in range(REPLICAS):
         for half in range(-1, split):
             src = ya.at[blk] if half < 0 else yst.at[1, rows(0)]
             ref = y_out.at[blk, place(half)]
             came = rcopy(ref, ref, y_s.at[1, blk, half + 1], y_r.at[blk, half + 1], (blk, e))
             sent_here = True if half < 0 else end
 
-            def kept():
+            def stayed():
                 y_local(src, half).wait()
 
             def sent():
                 y_copy(src, 1, blk, half, e).wait_send()
 
-            pl.when((r == blk) & sent_here)(kept)
+            pl.when((r == blk) & sent_here)(stayed)
             pl.when((r != blk) & sent_here)(sent)
             pl.when((r != blk) | jnp.logical_not(sent_here))(came.wait_recv)
 
 
-def back(part, h, ya):
+def back(part, h, h_mid, raw_here, raw_cross, ya):
     _, n, cols, _ = part.shape
-    cut = ya.shape[1]
-    seq = cut + n // 4
-    piece = n // 8
+    ret = ya.shape[1]
+    seq = ret + n // 4
+    piece = raw_here.shape[1] // 4
     vmem = pl.BlockSpec(memory_space=pltpu.VMEM)
     hbm = pl.BlockSpec(memory_space=pl.ANY)
     dma = pltpu.SemaphoreType.DMA
     pieces = n // piece
+    split = pieces // 4
 
     def tiles(*lead, dtype=jnp.bfloat16):
         return pltpu.VMEM(lead + (n, cols, LANES), dtype)
 
     return pl.pallas_call(
-        functools.partial(back_kernel, cut, piece),
+        functools.partial(back_kernel, ret, piece),
         out_shape=jax.ShapeDtypeStruct((4, seq, cols, LANES), jnp.bfloat16),
-        in_specs=[hbm, vmem, hbm],
+        in_specs=[hbm, vmem] + [hbm] * 4,
         out_specs=hbm,
         scratch_shapes=[
             tiles(4), tiles(4), tiles(2, 2), tiles(2, dtype=jnp.float32), tiles(4, dtype=jnp.float32), tiles(), tiles(2),
             *([dma((2, 2, pieces))] * 2), *([dma((4, pieces))] * 2), dma((4, pieces)), dma((2, pieces)),
-            dma, dma, dma((2, 4, 3)), dma((4, 3)), dma((4,)), dma((3,)),
+            dma((2, 4, split + 1)), dma((4, split + 1)), dma((4,)), dma((split + 1,)), dma((2, 2)),
         ],
         compiler_params=pltpu.CompilerParams(collective_id=1, has_side_effects=True, vmem_limit_bytes=58 * 1024 * 1024),
-    )(part, h, ya)
+    )(part, h, h_mid, raw_here, raw_cross, ya)
 
 
 def block_plan(ids, me, ne):
@@ -786,31 +836,37 @@
     tok = P(('replica', 'ep'), None, None)
     rows_ep = P('ep', None)
     by_expert = P('ep', None, None)
-    cut = CUT
+    cut, ret = CUT, RET
 
     def local(x, wq, wk, wv, wo, wr, w1, w3, w2, idx):
         b, s, d = x.shape
         k, ne = idx.shape[-1], w1.shape[0]
         me = lax.axis_index('ep')
+        low, c = me // 4, me % 2
         cols = d // LANES
-        ua, ub, ha, hb, ids = attention(x, idx.transpose(0, 2, 1), wr, wq, wk, wv, wo, cut)
-
-        def experts(u, gates, plan, lo, hi):
-            n = b * (hi - lo)
-            return moe(*plan, gates[..., lo:hi].reshape(-1), u, n, w1, w3, w2).reshape(nd, n, cols, LANES)
-
+        tail, rest = cut - ret, s - cut
+        ua, ub, ha, hb, ids = attention(x, idx.transpose(0, 2, 1), wr, wq, wk, wv, wo, cut, ret)
         plan_a, plan_b = block_plan(ids[..., :cut], me, ne), block_plan(ids[..., cut:], me, ne)
-        u_all = lax.all_gather(ua, 'ep', axis=0, tiled=False)
+        u_all = lax.all_gather(ua, 'ep')
         u_all, plan_b = lax.optimization_barrier((u_all, plan_b))
         terms = u_all[:, b * cut:].reshape(nd, 3, b, k, s).astype(jnp.float32)
         gates = terms[:, 0] + terms[:, 1] + terms[:, 2]
-        part_a = experts(u_all, gates, plan_a, 0, cut)
-        ub_all = lax.all_gather(ub, 'ep', axis=0, tiled=False)
-        part_a, ub_all = lax.optimization_barrier((part_a, ub_all))
+        lengths = (b * ret, b * (tail + rest))
+        part_a, part_b = moe(*plan_a, gates[..., :cut].reshape(-1), u_all, b * cut, w1, w3, w2, lengths,
+                             ((0, 0, ret, 0), (1, ret, cut, 0)))
+        ub_all = lax.all_gather(ub, 'ep')
+        part_a, part_b, ub_all = lax.optimization_barrier((part_a, part_b, ub_all))
+        far = lax.dynamic_index_in_dim(part_b.reshape(-1, nd // 4, CORES, b * (tail + rest), cols, LANES)[:, :, :, :b * tail], 1 - low, 0, False)
+        here, cross = [lax.dynamic_index_in_dim(far, i, 1, False) for i in (c, 1 - c)]
+        inward = [(0, 2), (1, 3), (6, 4), (7, 5)]
+        here = lax.ppermute(here, 'ep', inward)
+        cross = lax.ppermute(cross, 'ep', [(i, j ^ 1) for i, j in inward])
+        h_mid = lax.ppermute(hb, 'ep', [(j, i) for i, j in inward])
         part_a = lax.all_to_all(part_a, 'ep', 0, 0, tiled=True)
-        part_b = experts(ub_all, gates, plan_b, cut, s)
+        part_b, = moe(*plan_b, gates[..., cut:].reshape(-1), ub_all, b * rest, w1, w3, w2, lengths[1:],
+                      ((0, 0, rest, b * tail),), part_b)
         ya = ha.astype(jnp.float32) + jnp.sum(part_a.astype(jnp.float32), axis=0)
-        y = back(part_b, hb, ya.astype(jnp.bfloat16).reshape(b, cut, cols, LANES))
+        y = back(part_b, hb, h_mid, here, cross, ya.astype(jnp.bfloat16).reshape(b, ret, cols, LANES))
         return y.reshape(b, s, d)
 
     return jax.shard_map(local, mesh=mesh,

time: 768 us -> 748 us (0.974)
  waiting for transfers between devices: 96.6 us -> 63.4 us
  starting transfers between devices: 4.89 us -> 14 us
    all_to_all x1, waiting for transfers between devices: 20.1 us -> 0.01 us  [local(): part_a = lax.all_to_all(part_a, 'ep', 0, 0, tiled=True)]
    all_gather x2, waiting for transfers between devices: 75.8 us -> 62.6 us  [the longest x1 51.8 us: local(): u_all = lax.all_gather(ua, 'ep')]
    ppermute x0 -> x3, starting transfers between devices: none -> 9.24 us  [the longest x1 5.52 us: local(): here = lax.ppermute(here, 'ep', inward)]
  transfers between devices with their start and end apart: 3 -> 6, of which waited for: 3 -> 3; matrix products, arithmetic and copies ran while one was open for 3% -> 4% of each run, Pallas kernels for 22% -> 22%
where the time goes in v6:
time: 748 us; the launch traced here: 746 us
  Pallas kernels  616 us (82%)
  waiting for transfers between devices  63.4 us (8%)
  other arithmetic  26 us (3%)
  starting transfers between devices  14 us (2%)
  between operations  13.6 us (2%)
  local copies, waits for them, and re-layouts  13.4 us (2%)
    pallas_call x1, Pallas kernels, attention(): pl.pallas_call(functools.partial(attn_kernel, cut, ret), out_shape=(out(n...  275 us
    pallas_call x1, Pallas kernels, back(): pl.pallas_call(functools.partial(back_kernel, ret, piece), out_shape=jax....  175 us
    pallas_call x2, Pallas kernels, moe(): pl.pallas_call(functools.partial(moe_kernel, nt, stores, len(into)), out_...  165 us
    all_gather x1, waiting for transfers between devices, local(): u_all = lax.all_gather(ua, 'ep')  51.8 us
    sort x2, other arithmetic, block_plan(): keys = lax.sort(jnp.where(local, key, none).reshape(-1), is_stable=False)  15 us
  transfers between devices with their start and end apart: 6, of which 3 were waited for; matrix products, arithmetic and copies ran while one was open for 4% of the time, Pallas kernels for 22%

profile of v6, /device:TPU:0, one launch (start us, length us, event | category | flops | bytes accessed | tf_op | source)
XLA Modules:
  0.0 746.1 jit_solution(13333764270494552928)
XLA Ops:
  6.5 0.0 all-gather.5.cloned.1.call-start
  6.5 0.3 fusion.3
  6.8 0.7 pad_maximum_fusion
  7.6 275.5 %shard_map.100 = (bf16[230,16,128]{2,1,0:T(8,128)(2,1)}, bf16[288,16,128]{2,1,0:T(8,128)(2,1)}, bf16[128,16,128]{2,1,0:T(8,128)(2,1)}, bf16[384,16,128]{2,1,0:T(...) custom-call(bf16[4,128,2048]{2,1,0:T(8,128)(2,1)} %x_hbm.1, ...), custom_call_target="tpu_custom_call" | custom-call | flops 42949672960 | bytes 67108864 | tf_op jit(solution)/shard_map/pallas_call | solution.py:439
  283.0 0.0 copy-start.2
  283.0 0.0 all-gather.5.cloned.1.call-update
  283.1 0.0 all-gather.7.cloned.1.call-start
  283.1 0.7 all-gather.7.cloned.1.call-update
  283.8 1.0 or_select_fusion.1
  284.9 0.1 eq.44
  285.0 0.3 convert_reduce_fusion.1
  285.3 0.7 fusion.12
  285.9 0.1 select_reduce_fusion.11
  286.0 0.1 reshape.141
  286.2 8.8 %sort.14 = s32[18432]{0:T(1024)S(1)} sort(s32[18432]{0:T(1024)S(1)} %reshape.141), dimensions={0}, to_apply=%region_9.10 | sort | flops 276480 | bytes 147456 | tf_op jit(solution)/shard_map/sort | solution.py:812
  294.9 0.0 copy-done.2
  294.9 0.1 or_select_fusion
  295.0 0.1 eq.50
  295.2 0.2 convert_reduce_fusion.2
  295.4 0.6 fusion.10
  296.0 0.1 select_reduce_fusion.9
  296.1 0.1 reshape.152
  296.3 6.3 sort.15
  302.6 0.6 concatenate.14.key_ref
  303.2 0.6 concatenate.15.key_ref
  303.8 0.1 select_reduce_fusion.10
  304.0 0.1 select_reduce_fusion.8
  304.1 0.1 fusion.9
  304.2 0.1 fusion.8
  304.2 0.7 select_reduce_fusion.4
  304.9 0.7 select_reduce_fusion
  305.6 0.6 subtract_clamp_fusion.1
  306.2 0.5 subtract_clamp_fusion
  306.8 51.8 %all-gather.5.cloned.1.call-done = bf16[1840,16,128]{2,1,0:T(8,128)(2,1)} async-done(((bf16[230,16,128]{2,1,0:T(8,128)(2,1)}), bf16[1840,16,128]{2,1,0:T(8,128)(2,1)}) %all-gather.5.cloned.1.call-update) | async-done | bytes 7536656 | tf_op jit(solution)/shard_map/all_gather | solution.py:850
  358.5 0.9 slice.28
  359.5 0.7 reshape.153.gate_ref
  360.3 78.7 %shard_map.101 = (bf16[8,128,16,128]{3,2,1,0:T(8,128)(2,1)}, bf16[8,384,16,128]{3,2,1,0:T(8,128)(2,1)}) custom-call(s32[1]{0:T(128)} %bitcast.6.nblk_ref, s32[130]{0:T(256)} %get-tuple-element.40.be_ref, s32[130]{0:T(256)} %get-tuple-element.56.bb_ref, s32[130]{0:T(256)} %get-tuple-element.55.bn_ref, s32[14464]{0:T(1024)} %concatenate.15.key_ref, ...), custom_call_target="tpu_custom_call" | custom-call | flops 47185920000 | bytes 150994944 | tf_op jit(solution)/shard_map/pallas_call | solution.py:561
  439.0 10.8 %all-gather.7.cloned.1.call-done = bf16[2304,16,128]{2,1,0:T(8,128)(2,1)} async-done(((bf16[288,16,128]{2,1,0:T(8,128)(2,1)}), bf16[2304,16,128]{2,1,0:T(8,128)(2,1)}) %all-gather.7.cloned.1.call-update) | async-done | bytes 9437200 | tf_op jit(solution)/shard_map/all_gather | solution.py:857
  449.8 0.0 copy-start
  449.8 4.7 all-to-all-start
  454.5 0.0 copy-done
  454.5 1.5 collective-permute-start
  456.0 0.1 slice.39
  456.1 0.8 reshape.142.gate_ref
  456.9 2.4 slice.41
  459.3 1.4 dynamic-slice_bitcast_fusion
  460.8 5.5 collective-permute-start.1
  466.3 2.2 collective-permute-start.2
  468.5 86.2 %shard_map.102.part = bf16[8,384,16,128]{3,2,1,0:T(8,128)(2,1)} custom-call(s32[1]{0:T(128)} %bitcast.2.nblk_ref, s32[162]{0:T(256)} %get-tuple-element.24.be_ref, s32[162]{0:T(256)} %get-tuple-element.25.bb_ref, s32[162]{0:T(256)} %get-tuple-element.26.bn_ref, s32[18560]{0:T(1024)} %concatenate.14.key_ref, ...), custom_call_target="tpu_custom_call", output_to_operand_aliasing={{}: (10, {})} | custom-call | flops 47185920000 | bytes 150994944 | tf_op jit(solution)/shard_map/pallas_call | solution.py:561
  554.7 0.0 all-to-all-done
  554.7 0.0 copy-start.3
  554.7 2.9 convert_reduce_fusion
  557.6 0.0 copy-done.3
  557.6 0.9 add_convert_fusion
  558.5 0.2 collective-permute-done.h_mid
  558.7 0.0 copy-start.1
  558.7 0.0 collective-permute-done.1.raw_here
  558.7 0.0 collective-permute-done.2.raw_cross
  558.7 1.1 copy-done.1
  559.8 175.3 %shard_map.103 = bf16[4,128,16,128]{3,2,1,0:T(8,128)(2,1)} custom-call(bf16[8,384,16,128]{3,2,1,0:T(8,128)(2,1)} %shard_map.102.part, bf16[384,16,128]{2,1,0:T(8,128)(2,1)} %get-tuple-element.34.h_ref, bf16[384,16,128]{2,1,0:T(8,128)(2,1)} %copy-done.1, bf16[2,96,16,128]{3,2,1,0:T(8,128)(2,1)} %collective-permute-done.1.raw_here, ...), custom_call_target="tpu_custom_call" | custom-call | tf_op jit(solution)/shard_map/pallas_call | solution.py:788
  735.1 4.2 reshape.156
  (8 shorter events, 0.1 us)
Async XLA Ops:
  6.5 352.0 %all-gather.5.cloned.1.call-start = ((), (), s32[]{:S(2)}) async-start(), calls=%async_computation.1 | async-start | bytes 8478720 | tf_op jit(solution)/shard_map/all_gather | solution.py:850
  283.0 11.9 %copy-start.2 = (s32[8,4,8,128]{3,2,1,0:T(8,128)S(1)}, s32[8,4,8,128]{3,2,1,0:T(8,128)}, u32[]{:S(2)}) copy-start(s32[8,4,8,128]{3,2,1,0:T(8,128)} %get-tuple-element.22) | copy-start | bytes 393220
  283.1 166.7 %all-gather.7.cloned.1.call-start = ((), (), s32[]{:S(2)}) async-start(), calls=%async_computation.2 | async-start | bytes 10616832 | tf_op jit(solution)/shard_map/all_gather | solution.py:857
  449.8 4.7 copy-start
  449.8 104.9 %all-to-all-start = ((bf16[8,128,16,128]{3,2,1,0:T(8,128)(2,1)}), bf16[8,128,16,128]{3,2,1,0:T(8,128)(2,1)}, u32[]{:S(2)}, u32[]{:S(2)}) async-start(bf16[8,128,16,128]{3,2,1,0:T(8,128)(2,1)} %get-tuple-element.36), calls=%async_computation | async-start | bytes 8388608 | tf_op jit(solution)/shard_map/all_to_all | solution.py:865
  454.5 104.2 %collective-permute-start = (bf16[384,16,128]{2,1,0:T(8,128)(2,1)S(1)}, bf16[384,16,128]{2,1,0:T(8,128)(2,1)S(1)}, u32[]{:S(2)}, u32[]{:S(2)}) collective-permute-start(bf16[384,16,128]{2,1,0:T(8,128)(2,1)S(1)} %copy-done), channel_id=1, source_target_pairs={{2,0},{3,1},{4,6},{5,7},{10,8},{11,9},{12,14},{13,15},{18,16},{19,... | collective-permute-start | bytes 4718600 | tf_op jit(solution)/shard_map/ppermute | solution.py:864
  460.8 97.9 %collective-permute-start.1 = (bf16[2,96,16,128]{3,2,1,0:T(8,128)(2,1)}, bf16[2,96,16,128]{3,2,1,0:T(8,128)(2,1)}, u32[]{:S(2)}, u32[]{:S(2)}) collective-permute-start(bf16[2,96,16,128]{3,2,1,0:T(8,128)(2,1)} %get-tuple-element.54), channel_id=1, source_target_pairs={{0,2},{1,3},{6,4},{7,5},{8,10},{9,11},{14,12},{15,13},{16,18},{17,... | collective-permute-start | bytes 2359304 | tf_op jit(solution)/shard_map/ppermute | solution.py:862
  466.3 92.4 %collective-permute-start.2 = (bf16[2,96,16,128]{3,2,1,0:T(8,128)(2,1)}, bf16[2,96,16,128]{3,2,1,0:T(8,128)(2,1)}, u32[]{:S(2)}, u32[]{:S(2)}) collective-permute-start(bf16[2,96,16,128]{3,2,1,0:T(8,128)(2,1)} %get-tuple-element.53), channel_id=1, source_target_pairs={{0,3},{1,2},{6,5},{7,4},{8,11},{9,10},{14,13},{15,12},{16,19},{17,... | collective-permute-start | bytes 2359304 | tf_op jit(solution)/shard_map/ppermute | solution.py:863
  554.7 2.9 copy-start.3
  558.7 1.1 copy-start.1
Sparse Core Ops, SparseCore 0:
  283.2 75.2 all-gather.4
  360.2 89.5 all-gather.6

commit v7 on v6

--- a/solution.py
+++ b/solution.py
@@ -12,6 +12,7 @@
 BM = 128
 PITCH = BM + 1
 LANES = 128
+VMEM = 60 * 1024 * 1024
 CORES = 2
 REPLICAS = 4
 CUT = 56
@@ -26,6 +27,10 @@
         return carry
 
     lax.fori_loop(0, n, step, 0)
+
+
+def cost(flops, moved):
+    return pl.CostEstimate(flops=flops, bytes_accessed=moved, transcendentals=0)
 
 
 def kept(fn, v, axis=-1):
@@ -294,7 +299,7 @@
     def compute(s, j):
         slot = mod(s, 2)
         a = a_ref[...]
-        cols = slice(j * pair, (j + 1) * pair)
+        cols = pl.ds(pl.multiple_of(j * pair, pair), pair)
         cos, sin = cos_ref[...], sin_ref[...]
 
         def rot(v):
@@ -327,13 +332,25 @@
     def turn(i):
         within(i + 1, originate)
         within(i - 3, wait_loads)
-        for k in range(nz - 1):
-            within(i - 2, diagonal, k)
+
+        def serve(k):
             within(i - 1, across, k)
             within(i, along_z, k)
-            if k < npair:
-                within(i - 3, compute, k)
-        within(i - 2, collect)
+
+        def work(j):
+            within(i - 3, compute, j)
+
+            @pl.when(j == 0)
+            def _():
+                within(i - 2, diagonal, 1)
+                serve(1)
+                within(i - 2, diagonal, 2)
+                within(i - 2, collect)
+
+        within(i - 2, diagonal, 0)
+        serve(0)
+        loop(npair, work)
+        serve(2)
         pl.when(i == 1)(spread_ids)
         pl.when(i == 2)(prepare)
 
@@ -450,8 +467,8 @@
             *([dma((3, STEPS, 4))] * 3), *([dma((2, STEPS, 4))] * 6), dma((2, 2, STEPS, 4)), *([dma((2, STEPS, 4, 4))] * 2),
             *([dma((4,))] * 4), *([dma((nd,))] * 2), dma((2, nd + 1)), dma((2,)),
         ],
-        compiler_params=pltpu.CompilerParams(collective_id=0, has_side_effects=True, vmem_limit_bytes=58 * 1024 * 1024),
-        cost_estimate=pl.CostEstimate(flops=10 * nseq * seq * d * hd, bytes_accessed=8 * d * hd, transcendentals=0),
+        compiler_params=pltpu.CompilerParams(collective_id=0, has_side_effects=True, vmem_limit_bytes=VMEM),
+        cost_estimate=cost(10 * nseq * seq * d * hd, 8 * d * hd),
     )(x, idt, cos, sin, wr, wq, wk, wv, wo)[:5]
 
 
@@ -472,21 +489,20 @@
 
     nd = u_hbm.shape[0]
     n = nt // nd
+    for c in weights(0, 0):
+        c.start()
     for dev in range(nd):
         pltpu.make_async_copy(u_hbm.at[dev, pl.ds(0, n)], ub.at[pl.ds(dev * n, n)], usem).start()
 
-    for c in weights(0, 0):
-        c.start()
-
     def zero(i):
         acc[pl.ds(i * 8, 8)] = jnp.zeros((8,) + acc.shape[1:], jnp.float32)
 
     loop(acc.shape[0] // 8, zero)
     pltpu.make_async_copy(ub.at[pl.ds(0, nt)], ub.at[pl.ds(0, nt)], usem).wait()
 
-    def gather(b):
+    def gather(b, some):
         base = bb_ref[b]
-        for i in range(BM):
+        for i in some:
             t = token_of(key_ref[base + i])
             xs[pl.ds(i, cols, stride=PITCH), :] = ub[t].astype(jnp.float32)
 
@@ -499,7 +515,10 @@
         for t, v in new:
             acc[t] = v
 
-    gather(0)
+    def eight(g):
+        return [g * 8 + i for i in range(8)]
+
+    loop(BM // 8, lambda g: gather(0, eight(g)))
 
     def body(b, e_prev):
         e = be_ref[b]
@@ -517,11 +536,11 @@
 
         for k in range(cols):
             lhs[:, k * LANES:(k + 1) * LANES] = xs[k * PITCH:k * PITCH + BM, :].astype(jnp.bfloat16)
-        gather(b + 1)
+        gather(b + 1, range(BM))
         bp = jnp.maximum(b - 1, 0)
-        base, n = bb_ref[bp], jnp.where(b > 0, bn_ref[bp], 0)
-        for i in range(0, BM, 8):
-            scatter(base, n, range(i, i + 8))
+        base, valid = bb_ref[bp], jnp.where(b > 0, bn_ref[bp], 0)
+        for g in range(BM // 8):
+            scatter(base, valid, eight(g))
         x = lhs[...]
         a1 = jnp.dot(x, w1[slot], preferred_element_type=jnp.float32)
         a3 = jnp.dot(x, w3[slot], preferred_element_type=jnp.float32)
@@ -532,21 +551,20 @@
         return e
 
     lax.fori_loop(0, nblk, body, -1)
-    for i in range(0, BM, 8):
-        scatter(bb_ref[nblk - 1], bn_ref[nblk - 1], range(i, i + 8))
-
-    def pack(i):
-        for j in range(8):
-            t = i * 8 + j
-            ub[t] = acc[t].astype(jnp.bfloat16)
-
-    loop(nt // 8, pack)
+    loop(BM // 8, lambda g: scatter(bb_ref[nblk - 1], bn_ref[nblk - 1], eight(g)))
 
     def store(i):
+        m = n // 4
+
+        def pack(g):
+            for j in eight(g):
+                ub[i * m + j] = acc[i * m + j].astype(jnp.bfloat16)
+
+        loop(m // 8, pack)
         dev, b = i // 4, lax.rem(i, 4)
         for out, lo, hi, base in stores:
-            pltpu.make_async_copy(ub.at[pl.ds(i * (n // 4) + lo, hi - lo)],
-                                  outs[out].at[dev, pl.ds(base + b * (hi - lo), hi - lo)], osem).start()
+            pltpu.make_async_copy(ub.at[pl.ds(i * m + lo, hi - lo)], outs[out].at[dev, pl.ds(base + b * (hi - lo), hi - lo)],
+                                  osem).start()
 
     loop(nd * 4, store)
     pltpu.make_async_copy(ub.at[pl.ds(0, nt)], ub.at[pl.ds(0, nt)], osem).wait()
@@ -577,12 +595,12 @@
             pltpu.SemaphoreType.DMA((2, 3)),
             pltpu.SemaphoreType.DMA,
         ],
-        compiler_params=pltpu.CompilerParams(vmem_limit_bytes=60 * 1024 * 1024),
-        cost_estimate=pl.CostEstimate(flops=6 * 5000 * d * f, bytes_accessed=ne * 3 * d * f * 2, transcendentals=0),
+        compiler_params=pltpu.CompilerParams(vmem_limit_bytes=VMEM),
+        cost_estimate=cost(30000 * d * f, 6 * ne * d * f),
     )(nblk, be, bb, bn, keys, gates, u, w1, w3, w2, *into)
 
 
-def back_kernel(ret, piece, part, h_ref, h_mid, raw_here, raw_cross, ya, y_out, own, prt, raw, fin, fout, hs, yst, raw_s, raw_r,
+def back_kernel(ret, piece, part, h_ref, h_mid, raw_here, raw_cross, first_hbm, ha_ref, y_out, own, prt, raw, fin, fout, hs, yst, yfirst, firsts, tm, raw_s, raw_r,
                 prt_s, prt_r, f_s, f_r, y_s, y_r, osem, lsem, csem):
     r, e = lax.axis_index('replica'), lax.axis_index('ep')
     z, c = e // 2, e % 2
@@ -642,10 +660,10 @@
         return pl.ds(0, ret) if half < 0 else pl.ds(ret + half * piece, piece)
 
     def y_copy(src, i, blk, half, f):
-        return rcopy(src, y_out.at[r, place(half)], y_s.at[i, blk, half + 1], y_r.at[r, half + 1], (blk, f))
+        return rcopy(src, y_out.at[r, place(half), :], y_s.at[i, blk, half + 1], y_r.at[r, half + 1], (blk, f))
 
     def y_local(src, half):
-        return pltpu.make_async_copy(src, y_out.at[r, place(half)], lsem.at[half + 1])
+        return pltpu.make_async_copy(src, y_out.at[r, place(half), :], lsem.at[half + 1])
 
     def put(src, blk, half):
         pl.when(r == blk)(lambda: y_local(src, half).start())
@@ -672,20 +690,51 @@
             load(far(i)).start()
             each(lambda p: [prt_copy(far(i), p).start(), prt_copy(near(i), p).start()])
 
-    for blk in range(REPLICAS):
-        put(ya.at[blk], blk, -1)
+    keep_first = pltpu.make_async_copy(first_hbm, firsts, csem.at[2, 0])
+    keep_first.start()
 
     def f32(v):
         return v.astype(jnp.float32)
 
-    def add(chip, p, incoming, out, finish=f32):
+    def add(chip, p, incoming, put_sum):
         prt_copy(chip, p).wait_recv()
 
         def some(j):
             s = pl.ds(p * piece + j * 4, 4)
-            out[s] = finish(f32(own[chip, s]) + f32(prt[chip, s]) + incoming(s))
+            put_sum(j, s, f32(own[chip, s]) + f32(prt[chip, s]) + incoming(s))
 
         each(some, piece // 4)
+
+    cols = h_ref.shape[1]
+    pitch = cols + 1
+
+    def to(out):
+        def put_sum(j, s, v):
+            out[s] = v
+
+        return put_sum
+
+    def to_tiles(j, s, v):
+        for i in range(v.shape[0]):
+            tm[pl.ds((j * v.shape[0] + i) * pitch, cols), :] = v[i]
+
+    def to_rows(out, count):
+        for k in range(cols):
+            out[:, k * LANES:(k + 1) * LANES] = tm[pl.ds(k, count, stride=pitch), :].astype(jnp.bfloat16)
+
+    def finish_first():
+        keep_first.wait()
+        for blk in range(REPLICAS):
+            def some(j):
+                s = pl.ds(blk * ret + j * 4, 4)
+                v = f32(ha_ref[s])
+                for dev in range(firsts.shape[0]):
+                    v = v + f32(firsts[dev, s])
+                to_tiles(j, s, v)
+
+            each(some, ret // 4)
+            to_rows(yfirst.at[blk], ret)
+            put(yfirst.at[blk], blk, -1)
 
     @on_mid
     def _():
@@ -698,13 +747,13 @@
         def first(q):
             i, p = q // pieces, lax.rem(q, pieces)
             pl.when(p >= early)(lambda: [raw_recv(i, core, p).wait_recv() for core in range(CORES)][0])
-            add(far(i), p, lambda s: f32(raw[i, 0, s]) + f32(raw[i, 1, s]), fout.at[i])
+            add(far(i), p, lambda s: f32(raw[i, 0, s]) + f32(raw[i, 1, s]), to(fout.at[i]))
             f_copy(i, p, 0).start()
 
         def second(q):
             i, p = q // pieces, lax.rem(q, pieces)
             f_copy(i, p, 0).wait_recv()
-            add(near(i), p, lambda s: fin[i, s], fout.at[2 + i])
+            add(near(i), p, lambda s: fin[i, s], to(fout.at[2 + i]))
             f_copy(i, p, 1).start()
 
         lag = 2
@@ -714,9 +763,11 @@
             pl.when(q >= lag)(lambda: second(q - lag))
 
         each(step, 2 * pieces + lag)
+        finish_first()
 
     @on_end
     def _():
+        finish_first()
         for i in range(CORES):
             load(near(i)).wait()
             if i == 0:
@@ -725,8 +776,9 @@
 
             def last(p):
                 f_copy(i, p, 1).wait_recv()
-                add(near(i), p, lambda s: fin[i, s] + f32(h[s]), yst.at[i], lambda v: v.astype(jnp.bfloat16))
-                src = yst.at[i, rows(p)]
+                add(near(i), p, lambda s: fin[i, s] + f32(h[s]), to_tiles)
+                src = yst.at[i, p]
+                to_rows(src, piece)
                 for blk in range(REPLICAS):
                     for half in range(split):
                         @pl.when(p == (early + blk * (split - 1) + half - 1 if half else blk))
@@ -745,7 +797,7 @@
             each(lambda p: prt_copy(near(i), p).wait_send())
         for blk in range(REPLICAS):
             for half in range(split):
-                y_copy(yst.at[0, rows(0)], 0, blk, half, ep_at(z_mid, c)).wait_send()
+                y_copy(yst.at[0, 0], 0, blk, half, ep_at(z_mid, c)).wait_send()
 
     @on_mid
     def _():
@@ -755,8 +807,8 @@
 
     for blk in range(REPLICAS):
         for half in range(-1, split):
-            src = ya.at[blk] if half < 0 else yst.at[1, rows(0)]
-            ref = y_out.at[blk, place(half)]
+            src = yfirst.at[blk] if half < 0 else yst.at[1, 0]
+            ref = y_out.at[blk, place(half), :]
             came = rcopy(ref, ref, y_s.at[1, blk, half + 1], y_r.at[blk, half + 1], (blk, e))
             sent_here = True if half < 0 else end
 
@@ -771,9 +823,9 @@
             pl.when((r != blk) | jnp.logical_not(sent_here))(came.wait_recv)
 
 
-def back(part, h, h_mid, raw_here, raw_cross, ya):
+def back(part, h, h_mid, raw_here, raw_cross, first, ha):
     _, n, cols, _ = part.shape
-    ret = ya.shape[1]
+    ret = ha.shape[0] // 4
     seq = ret + n // 4
     piece = raw_here.shape[1] // 4
     vmem = pl.BlockSpec(memory_space=pltpu.VMEM)
@@ -787,16 +839,18 @@
 
     return pl.pallas_call(
         functools.partial(back_kernel, ret, piece),
-        out_shape=jax.ShapeDtypeStruct((4, seq, cols, LANES), jnp.bfloat16),
-        in_specs=[hbm, vmem] + [hbm] * 4,
+        out_shape=jax.ShapeDtypeStruct((4, seq, cols * LANES), jnp.bfloat16),
+        in_specs=[hbm, vmem] + [hbm] * 4 + [vmem],
         out_specs=hbm,
         scratch_shapes=[
-            tiles(4), tiles(4), tiles(2, 2), tiles(2, dtype=jnp.float32), tiles(4, dtype=jnp.float32), tiles(), tiles(2),
+            tiles(4), tiles(4), tiles(2, 2), tiles(2, dtype=jnp.float32), tiles(4, dtype=jnp.float32), tiles(),
+            pltpu.VMEM((2, pieces, piece, cols * LANES), jnp.bfloat16), pltpu.VMEM((4, ret, cols * LANES), jnp.bfloat16),
+            pltpu.VMEM(first.shape, jnp.bfloat16), pltpu.VMEM((ret * (cols + 1), LANES), jnp.float32),
             *([dma((2, 2, pieces))] * 2), *([dma((4, pieces))] * 2), dma((4, pieces)), dma((2, pieces)),
-            dma((2, 4, split + 1)), dma((4, split + 1)), dma((4,)), dma((split + 1,)), dma((2, 2)),
+            dma((2, 4, split + 1)), dma((4, split + 1)), dma((4,)), dma((split + 1,)), dma((3, 2)),
         ],
-        compiler_params=pltpu.CompilerParams(collective_id=1, has_side_effects=True, vmem_limit_bytes=58 * 1024 * 1024),
-    )(part, h, h_mid, raw_here, raw_cross, ya)
+        compiler_params=pltpu.CompilerParams(collective_id=1, has_side_effects=True, vmem_limit_bytes=VMEM),
+    )(part, h, h_mid, raw_here, raw_cross, first, ha)
 
 
 def block_plan(ids, me, ne):
@@ -854,10 +908,11 @@
         lengths = (b * ret, b * (tail + rest))
         part_a, part_b = moe(*plan_a, gates[..., :cut].reshape(-1), u_all, b * cut, w1, w3, w2, lengths,
                              ((0, 0, ret, 0), (1, ret, cut, 0)))
+        early = part_b.reshape(-1, nd // 4, CORES, b * (tail + rest), cols, LANES)[:, :, :, :b * tail]
+        far = lax.dynamic_index_in_dim(early, 1 - low, 0, False)
+        here, cross = [lax.dynamic_index_in_dim(far, i, 1, False) for i in (c, 1 - c)]
         ub_all = lax.all_gather(ub, 'ep')
-        part_a, part_b, ub_all = lax.optimization_barrier((part_a, part_b, ub_all))
-        far = lax.dynamic_index_in_dim(part_b.reshape(-1, nd // 4, CORES, b * (tail + rest), cols, LANES)[:, :, :, :b * tail], 1 - low, 0, False)
-        here, cross = [lax.dynamic_index_in_dim(far, i, 1, False) for i in (c, 1 - c)]
+        part_a, part_b, here, cross, ub_all = lax.optimization_barrier((part_a, part_b, here, cross, ub_all))
         inward = [(0, 2), (1, 3), (6, 4), (7, 5)]
         here = lax.ppermute(here, 'ep', inward)
         cross = lax.ppermute(cross, 'ep', [(i, j ^ 1) for i, j in inward])
@@ -865,9 +920,7 @@
         part_a = lax.all_to_all(part_a, 'ep', 0, 0, tiled=True)
         part_b, = moe(*plan_b, gates[..., cut:].reshape(-1), ub_all, b * rest, w1, w3, w2, lengths[1:],
                       ((0, 0, rest, b * tail),), part_b)
-        ya = ha.astype(jnp.float32) + jnp.sum(part_a.astype(jnp.float32), axis=0)
-        y = back(part_b, hb, h_mid, here, cross, ya.astype(jnp.bfloat16).reshape(b, ret, cols, LANES))
-        return y.reshape(b, s, d)
+        return back(part_b, hb, h_mid, here, cross, part_a, ha)
 
     return jax.shard_map(local, mesh=mesh,
                          in_specs=(tok, rows_ep, rows_ep, rows_ep, rows_ep, P(None, None),

time: 748 us -> 735 us (0.983)
  Pallas kernels: 616 us -> 602 us
    pallas_call x1, Pallas kernels: 175 us -> 166 us  [back(): pl.pallas_call(functools.partial(back_kernel, ret, piece), out_shape=jax....]
    ppermute x1, waiting for transfers between devices: 0.16 us -> 9.14 us  [local(): h_mid = lax.ppermute(hb, 'ep', [(j, i) for i, j in inward])]
where the time goes in v7:
time: 735 us; the launch traced here: 733 us
  Pallas kernels  602 us (82%)
  waiting for transfers between devices  66.5 us (9%)
  other arithmetic  23.1 us (3%)
  starting transfers between devices  15.6 us (2%)
  between operations  13.6 us (2%)
  local copies, waits for them, and re-layouts  12.4 us (2%)
    pallas_call x1, Pallas kernels, attention(): pl.pallas_call(functools.partial(attn_kernel, cut, ret), out_shape=(out(n...  272 us
    pallas_call x1, Pallas kernels, back(): pl.pallas_call(functools.partial(back_kernel, ret, piece), out_shape=jax....  166 us
    pallas_call x2, Pallas kernels, moe(): pl.pallas_call(functools.partial(moe_kernel, nt, stores, len(into)), out_...  164 us
    all_gather x1, waiting for transfers between devices, local(): u_all = lax.all_gather(ua, 'ep')  50 us
    sort x2, other arithmetic, block_plan(): keys = lax.sort(jnp.where(local, key, none).reshape(-1), is_stable=False)  15 us
  transfers between devices with their start and end apart: 6, of which 3 were waited for; matrix products, arithmetic and copies ran while one was open for 4% of the time, Pallas kernels for 22%

profile of v7, /device:TPU:0, one launch (start us, length us, event | category | flops | bytes accessed | tf_op | source)
XLA Modules:
  0.0 732.8 jit_solution(2927090621064477978)
XLA Ops:
  6.5 0.0 all-gather.5.cloned.1.call-start
  6.5 0.3 fusion.3
  6.8 0.7 pad_maximum_fusion
  7.6 271.6 %shard_map.100 = (bf16[230,16,128]{2,1,0:T(8,128)(2,1)}, bf16[288,16,128]{2,1,0:T(8,128)(2,1)}, bf16[128,16,128]{2,1,0:T(8,128)(2,1)}, bf16[384,16,128]{2,1,0:T(...) custom-call(bf16[4,128,2048]{2,1,0:T(8,128)(2,1)} %x_hbm.1, ...), custom_call_target="tpu_custom_call" | custom-call | flops 42949672960 | bytes 67108864 | tf_op jit(solution)/shard_map/pallas_call | solution.py:456
  279.2 0.0 all-gather.5.cloned.1.call-update
  279.2 0.2 all-gather.7.cloned.1.call-start
  279.4 0.5 all-gather.7.cloned.1.call-update
  280.0 1.0 or_select_fusion
  281.0 0.1 eq.50
  281.2 0.2 convert_reduce_fusion.1
  281.4 0.6 fusion.10
  282.0 0.1 select_reduce_fusion.9
  282.1 1.0 or_select_fusion.1
  283.2 0.1 eq.44
  283.3 0.3 convert_reduce_fusion
  283.5 0.7 fusion.12
  284.2 0.1 select_reduce_fusion.11
  284.3 0.1 reshape.135
  284.5 8.8 %sort.14 = s32[18432]{0:T(1024)S(1)} sort(s32[18432]{0:T(1024)S(1)} %reshape.135), dimensions={0}, to_apply=%region_9.10 | sort | flops 276480 | bytes 147456 | tf_op jit(solution)/shard_map/sort | solution.py:866
  293.2 0.6 concatenate.14.key_ref
  293.9 0.1 reshape.146
  294.0 6.3 sort.15
  300.3 0.6 concatenate.15.key_ref
  300.9 0.1 select_reduce_fusion.8
  301.0 0.1 select_reduce_fusion.10
  301.1 0.1 fusion.8
  301.2 0.1 fusion.9
  301.3 0.7 select_reduce_fusion
  302.0 0.7 select_reduce_fusion.4
  302.7 0.5 subtract_clamp_fusion
  303.2 0.6 subtract_clamp_fusion.1
  303.8 50.0 %all-gather.5.cloned.1.call-done = bf16[1840,16,128]{2,1,0:T(8,128)(2,1)} async-done(((bf16[230,16,128]{2,1,0:T(8,128)(2,1)}), bf16[1840,16,128]{2,1,0:T(8,128)(2,1)}) %all-gather.5.cloned.1.call-update) | async-done | bytes 7536656 | tf_op jit(solution)/shard_map/all_gather | solution.py:904
  353.8 0.9 slice.28
  354.9 0.7 reshape.147.gate_ref
  355.6 78.7 %shard_map.101 = (bf16[8,128,16,128]{3,2,1,0:T(8,128)(2,1)}, bf16[8,384,16,128]{3,2,1,0:T(8,128)(2,1)}) custom-call(s32[1]{0:T(128)} %bitcast.6.nblk_ref, s32[130]{0:T(256)} %get-tuple-element.44.be_ref, s32[130]{0:T(256)} %get-tuple-element.60.bb_ref, s32[130]{0:T(256)} %get-tuple-element.59.bn_ref, s32[14464]{0:T(1024)} %concatenate.15.key_ref, ...), custom_call_target="tpu_custom_call" | custom-call | flops 47185920000 | bytes 150994944 | tf_op jit(solution)/shard_map/pallas_call | solution.py:579
  434.3 2.4 slice.41
  436.8 1.4 dynamic-slice_bitcast_fusion
  438.2 6.8 all-gather.7.cloned.1.call-done
  445.0 0.0 copy-start
  445.0 6.3 all-to-all-start
  451.3 0.0 copy-done
  451.3 1.3 collective-permute-start
  452.6 0.1 slice.39
  452.7 0.8 reshape.136.gate_ref
  453.5 5.5 collective-permute-start.1
  459.0 2.2 collective-permute-start.2
  461.2 85.3 %shard_map.102.part = bf16[8,384,16,128]{3,2,1,0:T(8,128)(2,1)} custom-call(s32[1]{0:T(128)} %bitcast.2.nblk_ref, s32[162]{0:T(256)} %get-tuple-element.26.be_ref, s32[162]{0:T(256)} %get-tuple-element.27.bb_ref, s32[162]{0:T(256)} %get-tuple-element.28.bn_ref, s32[18560]{0:T(1024)} %concatenate.14.key_ref, ...), custom_call_target="tpu_custom_call", output_to_operand_aliasing={{}: (10, {})} | custom-call | flops 47185920000 | bytes 150994944 | tf_op jit(solution)/shard_map/pallas_call | solution.py:579
  546.5 9.1 %collective-permute-done.h_mid = bf16[384,16,128]{2,1,0:T(8,128)(2,1)S(1)} collective-permute-done((bf16[384,16,128]{2,1,0:T(8,128)(2,1)S(1)}, bf16[384,16,128]{2,1,0:T(8,128)(2,1)S(1)}, u32[]{:S(2)}, u32[]{:S(2)}) %collective-permute-start) | collective-permute-done | bytes 1572896 | tf_op jit(solution)/shard_map/ppermute | solution.py:919
  555.6 0.0 copy-start.1
  555.6 0.0 collective-permute-done.1.raw_here
  555.6 0.0 collective-permute-done.2.raw_cross
  555.6 0.0 all-to-all-done.first_hbm
  555.7 1.1 copy-done.1
  556.8 166.0 %shard_map.103 = bf16[4,128,2048]{2,1,0:T(8,128)(2,1)} custom-call(bf16[8,384,16,128]{3,2,1,0:T(8,128)(2,1)} %shard_map.102.part, bf16[384,16,128]{2,1,0:T(8,128)(2,1)} %get-tuple-element.36.h_ref, bf16[384,16,128]{2,1,0:T(8,128)(2,1)} %copy-done.1, bf16[2,96,16,128]{3,2,1,0:T(8,128)(2,1)} %collective-permute-done.1.raw_here, ...), custom_call_target="tpu_custom_call" | custom-call | tf_op jit(solution)/shard_map/pallas_call | solution.py:840
  722.8 3.2 copy.20
  (8 shorter events, 0.1 us)
Async XLA Ops:
  6.5 347.3 %all-gather.5.cloned.1.call-start = ((), (), s32[]{:S(2)}) async-start(), calls=%async_computation.1 | async-start | bytes 8478720 | tf_op jit(solution)/shard_map/all_gather | solution.py:904
  279.2 165.8 %all-gather.7.cloned.1.call-start = ((), (), s32[]{:S(2)}) async-start(), calls=%async_computation.2 | async-start | bytes 10616832 | tf_op jit(solution)/shard_map/all_gather | solution.py:914
  445.0 6.3 copy-start
  445.0 110.6 %all-to-all-start = ((bf16[8,128,16,128]{3,2,1,0:T(8,128)(2,1)}), bf16[8,128,16,128]{3,2,1,0:T(8,128)(2,1)}, u32[]{:S(2)}, u32[]{:S(2)}) async-start(bf16[8,128,16,128]{3,2,1,0:T(8,128)(2,1)} %get-tuple-element.39), calls=%async_computation | async-start | bytes 8388608 | tf_op jit(solution)/shard_map/all_to_all | solution.py:920
  451.3 104.3 %collective-permute-start = (bf16[384,16,128]{2,1,0:T(8,128)(2,1)S(1)}, bf16[384,16,128]{2,1,0:T(8,128)(2,1)S(1)}, u32[]{:S(2)}, u32[]{:S(2)}) collective-permute-start(bf16[384,16,128]{2,1,0:T(8,128)(2,1)S(1)} %copy-done), channel_id=1, source_target_pairs={{2,0},{3,1},{4,6},{5,7},{10,8},{11,9},{12,14},{13,15},{18,16},{19,... | collective-permute-start | bytes 4718600 | tf_op jit(solution)/shard_map/ppermute | solution.py:919
  453.5 102.1 %collective-permute-start.1 = (bf16[2,96,16,128]{3,2,1,0:T(8,128)(2,1)}, bf16[2,96,16,128]{3,2,1,0:T(8,128)(2,1)}, u32[]{:S(2)}, u32[]{:S(2)}) collective-permute-start(bf16[2,96,16,128]{3,2,1,0:T(8,128)(2,1)} %get-tuple-element.37), channel_id=1, source_target_pairs={{0,2},{1,3},{6,4},{7,5},{8,10},{9,11},{14,12},{15,13},{16,18},{17,... | collective-permute-start | bytes 2359304 | tf_op jit(solution)/shard_map/ppermute | solution.py:917
  459.0 96.6 %collective-permute-start.2 = (bf16[2,96,16,128]{3,2,1,0:T(8,128)(2,1)}, bf16[2,96,16,128]{3,2,1,0:T(8,128)(2,1)}, u32[]{:S(2)}, u32[]{:S(2)}) collective-permute-start(bf16[2,96,16,128]{3,2,1,0:T(8,128)(2,1)} %get-tuple-element.38), channel_id=1, source_target_pairs={{0,3},{1,2},{6,5},{7,4},{8,11},{9,10},{14,13},{15,12},{16,19},{17,... | collective-permute-start | bytes 2359304 | tf_op jit(solution)/shard_map/ppermute | solution.py:918
  555.6 1.1 copy-start.1
Sparse Core Ops, SparseCore 0:
  279.3 74.4 all-gather.4
  355.5 89.4 all-gather.6

commit v8 on v7

--- a/solution.py
+++ b/solution.py
@@ -37,6 +37,10 @@
     return fn(v, axis=axis, keepdims=True)
 
 
+def odd(v):
+    return lax.rem(v, 2)
+
+
 def ep_at(z, c):
     return 2 * z + c
 
@@ -93,7 +97,7 @@
     orows = go.shape[0] // STEPS
     nseq, seq, d = x_hbm.shape
     partner, x_dev, y_dev = (r, e_p), (r_x, e), (r_y, e)
-    per = STEPS // nd
+    srows = orows // nz
 
     def mod(v, m):
         return lax.rem(v, m)
@@ -132,18 +136,18 @@
 
     def piece(w, s, f, q):
         if w:
-            return go.at[pl.ds(s * orows + q * (orows // nq), orows // nq), :]
+            return go.at[pl.ds(s * orows + f // 2 * srows + q * (srows // nq), srows // nq), :]
         return gw.at[s, :, pl.ds(f * rows + q * quarter, quarter), :]
 
     def half(w, s, zs, q, i):
         if w:
-            n = orows // nq // 2
-            return go.at[pl.ds(s * orows + (2 * q + i) * n, n), :]
+            n = srows // nq // 2
+            return go.at[pl.ds(s * orows + zs * srows + (2 * q + i) * n, n), :]
         n = quarter // 2
         return gw.at[s, :, pl.ds(ep_at(zs, c) * rows + (2 * q + i) * n, n), :]
 
     def own_wo(s, lo, n):
-        return wo_ref.at[pl.ds(mod(s, per) * orows + lo, n), :]
+        return wo_ref.at[pl.ds(s // 2 * srows + lo, n), :]
 
     def z_send(w, s, zs, up, second=0):
         ref = piece(w, s, ep_at(zs, c), q_pair[3] if second else mine)
@@ -167,14 +171,19 @@
         return rcopy(ref, ref, ps.at[w, s, zs, j], pr.at[w, s, zs, j], partner)
 
     def p_whole(w, s, f):
-        ref = go.at[pl.ds(s * orows, orows), :] if w else gw.at[s, :, pl.ds(f * rows, rows), :]
+        ref = go.at[pl.ds(s * orows + z * srows, srows), :] if w else gw.at[s, :, pl.ds(f * rows, rows), :]
         return rcopy(ref, ref, ps.at[w, s, z, 0], pr.at[w, s, z, 0], partner)
 
     def own_parts(s):
-        return [(w.at[:, pl.ds(s * wide, wide)], m) for m, w in enumerate((wq_ref, wk_ref, wv_ref))]
-
-    def if_wo(s, f, *fns):
-        @pl.when(s // per == f)
+        out = []
+        for t in range(nz):
+            head = ep_at(t, odd(t + s)) * (STEPS // 2) + s // 2
+            for m, w in enumerate((wq_ref, wk_ref, wv_ref)):
+                out.append((w.at[:, pl.ds(head * HEAD, HEAD)], m, pl.ds(t * HEAD, HEAD)))
+        return out
+
+    def if_wo(s, zs, core, *fns):
+        @pl.when(odd(zs + s + core) == 0)
         def _():
             for fn in fns:
                 fn()
@@ -192,21 +201,21 @@
             sem = zp if up else zm
             dev = (r, e + 2) if up else (r, e - 2)
             for i, q in ((0, mine), (2, q_pair[3])):
-                for w, m in own_parts(s):
-                    rcopy(w.at[pl.ds(q * quarter, quarter), :], gw.at[s, m, pl.ds(e * rows + q * quarter, quarter), :],
+                for w, m, t in own_parts(s):
+                    rcopy(w.at[pl.ds(q * quarter, quarter), :], gw.at[s, m, pl.ds(e * rows + q * quarter, quarter), t],
                           sem.at[i, s, z], zr.at[i, s, z], dev).start()
-            if_wo(s, e, lambda: rcopy(own_wo(s, mine * (orows // nq), orows // nq), piece(1, s, e, mine), sem.at[1, s, z],
+            if_wo(s, z, c, lambda: rcopy(own_wo(s, mine * (srows // nq), srows // nq), piece(1, s, e, mine), sem.at[1, s, z],
                                       zr.at[1, s, z], dev).start())
 
         each_line(line)
-        for w, m in own_parts(s):
-            rcopy(w, gw.at[s, m, pl.ds(e * rows, rows), :], ps.at[0, s, z, 0], pr.at[0, s, z, 0], partner).start()
-        if_wo(s, e, lambda: rcopy(own_wo(s, 0, orows), go.at[pl.ds(s * orows, orows), :], ps.at[1, s, z, 0],
-                                  pr.at[1, s, z, 0], partner).start())
-
-    def for_both(s, f, fn):
+        for w, m, t in own_parts(s):
+            rcopy(w, gw.at[s, m, pl.ds(e * rows, rows), t], ps.at[0, s, z, 0], pr.at[0, s, z, 0], partner).start()
+        if_wo(s, z, c, lambda: rcopy(own_wo(s, 0, srows), go.at[pl.ds(s * orows + z * srows, srows), :], ps.at[1, s, z, 0],
+                                     pr.at[1, s, z, 0], partner).start())
+
+    def for_both(s, zs, core, fn):
         fn(0)
-        if_wo(s, f, lambda: fn(1))
+        if_wo(s, zs, core, lambda: fn(1))
 
     def along_z(s, k):
         def side(zs, up):
@@ -220,7 +229,7 @@
                 xy_send(w, s, zs, to_y if pairs(w, k) else mine, ys, yr, y_dev).start()
                 p_copy(w, s, zs, k, 0, c).start()
 
-            for_both(s, ep_at(zs, c), one)
+            for_both(s, zs, c, one)
 
         each_side(k, side)
 
@@ -237,7 +246,7 @@
                     xd_send(w, s, zs, q[2]).start()
                 p_copy(w, s, zs, k, 2, c).start()
 
-            for_both(s, ep_at(zs, c), one)
+            for_both(s, zs, c, one)
 
         each_side(k, side)
 
@@ -249,55 +258,57 @@
                     yd_send(w, s, zs, q_line[3]).wait_recv()
                     p_copy(w, s, zs, k, 3, c).start()
 
-            for_both(s, ep_at(zs, c), one)
+            for_both(s, zs, c, one)
 
         each_side(k, side)
 
     def load(s, f):
-        slot = mod(s, 2)
+        slot = odd(s)
         return pltpu.make_async_copy(gw.at[s, :, pl.ds(f * rows, rows), :], wbuf.at[slot, :, pl.ds(f * rows, rows), :],
                                      lsem.at[slot, f])
 
-    def oload(s, src):
-        slot = mod(s, 2)
-        return pltpu.make_async_copy(src, obuf.at[slot], lsem.at[slot, nd])
+    def oload(s, src, t, n):
+        slot = odd(s)
+        return pltpu.make_async_copy(src, obuf.at[slot, pl.ds(t * srows, n), :], lsem.at[slot, nd])
 
     def collect(s):
-        slot = mod(s, 2)
-        whole = go.at[pl.ds(s * orows, orows), :]
+        slot = odd(s)
 
         def side(k, zs):
             def one(w):
                 for j in range(nq):
                     p_copy(w, s, zs, k, j, 1 - c).wait_recv()
 
-            for_both(s, ep_at(zs, 1 - c), one)
+            for_both(s, zs, 1 - c, one)
 
         for k in range(nz - 1):
             each_side(k, lambda zs, up: side(k, zs))
         p_whole(0, s, e_p).wait_recv()
-        if_wo(s, e_p, lambda: p_whole(1, s, e_p).wait_recv())
+        if_wo(s, z, 1 - c, lambda: p_whole(1, s, e_p).wait_recv())
 
         for f in range(nd):
             def near():
-                for w, m in own_parts(s):
-                    pltpu.make_async_copy(w, wbuf.at[slot, m, pl.ds(f * rows, rows), :], lsem.at[slot, f]).start()
+                for w, m, t in own_parts(s):
+                    pltpu.make_async_copy(w, wbuf.at[slot, m, pl.ds(f * rows, rows), t], lsem.at[slot, f]).start()
 
             pl.when(f == e)(near)
             pl.when(f != e)(lambda: load(s, f).start())
-        if_wo(s, e, lambda: oload(s, own_wo(s, 0, orows)).start())
-        pl.when(s // per != e)(lambda: oload(s, whole).start())
+        for t in range(nz):
+            here = (t == z) & (odd(t + s + c) == 0)
+            pl.when(here)(lambda: oload(s, own_wo(s, 0, srows), t, srows).start())
+            pl.when(jnp.logical_not(here))(
+                lambda: oload(s, go.at[pl.ds(s * orows + t * srows, srows), :], t, srows).start())
 
     def wait_loads(s):
         for f in range(nd):
             load(s, f).wait()
-        oload(s, go.at[pl.ds(s * orows, orows), :]).wait()
+        oload(s, go.at[pl.ds(s * orows, orows), :], 0, orows).wait()
 
     pair = 2 * HEAD
     npair = wide // pair
 
     def compute(s, j):
-        slot = mod(s, 2)
+        slot = odd(s)
         a = a_ref[...]
         cols = pl.ds(pl.multiple_of(j * pair, pair), pair)
         cos, sin = cos_ref[...], sin_ref[...]
@@ -418,7 +429,7 @@
                     xd_send(w, s, zs, mine).wait_send()
                     yd_send(w, s, zs, mine).wait_send()
 
-            for_both(s, ep_at(zs, c), sent)
+            for_both(s, zs, c, sent)
 
         for k in range(nz - 1):
             each_side(k, lambda zs, up: side(k, zs, up))
@@ -427,7 +438,7 @@
             each_line(lambda up: z_send(w, s, z, up).wait_send())
             p_whole(w, s, e).wait_send()
 
-        for_both(s, e, own)
+        for_both(s, z, c, own)
         each_line(lambda up: z_send(0, s, z, up, 1).wait_send())
 
     loop(STEPS, drain)
@@ -464,8 +475,8 @@
             pltpu.VMEM((2, 3, d, wide), bf), pltpu.VMEM((2, hd // STEPS, d), bf),
             pltpu.VMEM((seq * (cols + 1), LANES), jnp.float32), pltpu.VMEM((nseq, k, seq), jnp.float32),
             pltpu.VMEM((nseq, k, seq), jnp.int32),
-            *([dma((3, STEPS, 4))] * 3), *([dma((2, STEPS, 4))] * 6), dma((2, 2, STEPS, 4)), *([dma((2, STEPS, 4, 4))] * 2),
-            *([dma((4,))] * 4), *([dma((nd,))] * 2), dma((2, nd + 1)), dma((2,)),
+            *([dma((3, STEPS, REPLICAS))] * 3), *([dma((2, STEPS, REPLICAS))] * 6), dma((2, 2, STEPS, REPLICAS)), *([dma((2, STEPS, REPLICAS, REPLICAS))] * 2),
+            *([dma((REPLICAS,))] * 4), *([dma((nd,))] * 2), dma((2, nd + 1)), dma((2,)),
         ],
         compiler_params=pltpu.CompilerParams(collective_id=0, has_side_effects=True, vmem_limit_bytes=VMEM),
         cost_estimate=cost(10 * nseq * seq * d * hd, 8 * d * hd),
@@ -825,14 +836,14 @@
 
 def back(part, h, h_mid, raw_here, raw_cross, first, ha):
     _, n, cols, _ = part.shape
-    ret = ha.shape[0] // 4
-    seq = ret + n // 4
-    piece = raw_here.shape[1] // 4
+    ret = ha.shape[0] // REPLICAS
+    seq = ret + n // REPLICAS
+    piece = raw_here.shape[1] // REPLICAS
     vmem = pl.BlockSpec(memory_space=pltpu.VMEM)
     hbm = pl.BlockSpec(memory_space=pl.ANY)
     dma = pltpu.SemaphoreType.DMA
     pieces = n // piece
-    split = pieces // 4
+    split = pieces // REPLICAS
 
     def tiles(*lead, dtype=jnp.bfloat16):
         return pltpu.VMEM(lead + (n, cols, LANES), dtype)
@@ -843,11 +854,11 @@
         in_specs=[hbm, vmem] + [hbm] * 4 + [vmem],
         out_specs=hbm,
         scratch_shapes=[
-            tiles(4), tiles(4), tiles(2, 2), tiles(2, dtype=jnp.float32), tiles(4, dtype=jnp.float32), tiles(),
-            pltpu.VMEM((2, pieces, piece, cols * LANES), jnp.bfloat16), pltpu.VMEM((4, ret, cols * LANES), jnp.bfloat16),
+            tiles(REPLICAS), tiles(REPLICAS), tiles(2, 2), tiles(2, dtype=jnp.float32), tiles(REPLICAS, dtype=jnp.float32), tiles(),
+            pltpu.VMEM((2, pieces, piece, cols * LANES), jnp.bfloat16), pltpu.VMEM((REPLICAS, ret, cols * LANES), jnp.bfloat16),
             pltpu.VMEM(first.shape, jnp.bfloat16), pltpu.VMEM((ret * (cols + 1), LANES), jnp.float32),
-            *([dma((2, 2, pieces))] * 2), *([dma((4, pieces))] * 2), dma((4, pieces)), dma((2, pieces)),
-            dma((2, 4, split + 1)), dma((4, split + 1)), dma((4,)), dma((split + 1,)), dma((3, 2)),
+            *([dma((2, 2, pieces))] * 2), *([dma((REPLICAS, pieces))] * 2), dma((REPLICAS, pieces)), dma((2, pieces)),
+            dma((2, 4, split + 1)), dma((REPLICAS, split + 1)), dma((REPLICAS,)), dma((split + 1,)), dma((3, 2)),
         ],
         compiler_params=pltpu.CompilerParams(collective_id=1, has_side_effects=True, vmem_limit_bytes=VMEM),
     )(part, h, h_mid, raw_here, raw_cross, first, ha)

time: 735 us -> 727 us (0.989)
  Pallas kernels: 602 us -> 589 us
    pallas_call x1, Pallas kernels: 272 us -> 260 us  [attention(): pl.pallas_call(functools.partial(attn_kernel, cut, ret), out_shape=(out(n...]
  transfers between devices with their start and end apart: 6 -> 6, of which waited for: 3 -> 3; matrix products, arithmetic and copies ran while one was open for 4% -> 4% of each run, Pallas kernels for 22% -> 23%
where the time goes in v8:
time: 727 us; the launch traced here: 725 us
  Pallas kernels  589 us (81%)
  waiting for transfers between devices  70.2 us (10%)
  other arithmetic  23.1 us (3%)
  starting transfers between devices  15.9 us (2%)
  between operations  13.6 us (2%)
  local copies, waits for them, and re-layouts  12.4 us (2%)
    pallas_call x1, Pallas kernels, attention(): pl.pallas_call(functools.partial(attn_kernel, cut, ret), out_shape=(out(n...  260 us
    pallas_call x1, Pallas kernels, back(): pl.pallas_call(functools.partial(back_kernel, ret, piece), out_shape=jax....  166 us
    pallas_call x2, Pallas kernels, moe(): pl.pallas_call(functools.partial(moe_kernel, nt, stores, len(into)), out_...  164 us
    all_gather x1, waiting for transfers between devices, local(): u_all = lax.all_gather(ua, 'ep')  53.6 us
    sort x2, other arithmetic, block_plan(): keys = lax.sort(jnp.where(local, key, none).reshape(-1), is_stable=False)  15 us
  transfers between devices with their start and end apart: 6, of which 3 were waited for; matrix products, arithmetic and copies ran while one was open for 4% of the time, Pallas kernels for 23%

profile of v8, /device:TPU:0, one launch (start us, length us, event | category | flops | bytes accessed | tf_op | source)
XLA Modules:
  0.0 724.5 jit_solution(2253229184650637973)
XLA Ops:
  6.5 0.0 all-gather.5.cloned.1.call-start
  6.5 0.3 fusion.3
  6.8 0.7 pad_maximum_fusion
  7.6 259.6 %shard_map.100 = (bf16[230,16,128]{2,1,0:T(8,128)(2,1)}, bf16[288,16,128]{2,1,0:T(8,128)(2,1)}, bf16[128,16,128]{2,1,0:T(8,128)(2,1)}, bf16[384,16,128]{2,1,0:T(...) custom-call(bf16[4,128,2048]{2,1,0:T(8,128)(2,1)} %x_hbm.1, ...), custom_call_target="tpu_custom_call" | custom-call | flops 42949672960 | bytes 67108864 | tf_op jit(solution)/shard_map/pallas_call | solution.py:467
  267.2 0.0 all-gather.5.cloned.1.call-update
  267.2 0.2 all-gather.7.cloned.1.call-start
  267.4 0.5 all-gather.7.cloned.1.call-update
  268.0 1.0 or_select_fusion
  269.0 0.1 eq.50
  269.1 0.2 convert_reduce_fusion.1
  269.4 0.6 fusion.10
  270.0 0.1 select_reduce_fusion.9
  270.1 1.0 or_select_fusion.1
  271.1 0.1 eq.44
  271.3 0.3 convert_reduce_fusion
  271.5 0.7 fusion.12
  272.2 0.1 select_reduce_fusion.11
  272.3 0.1 reshape.135
  272.4 8.8 %sort.14 = s32[18432]{0:T(1024)S(1)} sort(s32[18432]{0:T(1024)S(1)} %reshape.135), dimensions={0}, to_apply=%region_9.10 | sort | flops 276480 | bytes 147456 | tf_op jit(solution)/shard_map/sort | solution.py:877
  281.2 0.6 concatenate.14.key_ref
  281.8 0.1 reshape.146
  282.0 6.3 sort.15
  288.3 0.6 concatenate.15.key_ref
  288.9 0.1 select_reduce_fusion.8
  289.0 0.1 select_reduce_fusion.10
  289.1 0.1 fusion.8
  289.2 0.1 fusion.9
  289.3 0.7 select_reduce_fusion
  290.0 0.7 select_reduce_fusion.4
  290.7 0.5 subtract_clamp_fusion
  291.2 0.6 subtract_clamp_fusion.1
  291.8 53.6 %all-gather.5.cloned.1.call-done = bf16[1840,16,128]{2,1,0:T(8,128)(2,1)} async-done(((bf16[230,16,128]{2,1,0:T(8,128)(2,1)}), bf16[1840,16,128]{2,1,0:T(8,128)(2,1)}) %all-gather.5.cloned.1.call-update) | async-done | bytes 7536656 | tf_op jit(solution)/shard_map/all_gather | solution.py:915
  345.4 0.9 slice.28
  346.4 0.7 reshape.147.gate_ref
  347.2 78.7 %shard_map.101 = (bf16[8,128,16,128]{3,2,1,0:T(8,128)(2,1)}, bf16[8,384,16,128]{3,2,1,0:T(8,128)(2,1)}) custom-call(s32[1]{0:T(128)} %bitcast.6.nblk_ref, s32[130]{0:T(256)} %get-tuple-element.44.be_ref, s32[130]{0:T(256)} %get-tuple-element.60.bb_ref, s32[130]{0:T(256)} %get-tuple-element.59.bn_ref, s32[14464]{0:T(1024)} %concatenate.15.key_ref, ...), custom_call_target="tpu_custom_call" | custom-call | flops 47185920000 | bytes 150994944 | tf_op jit(solution)/shard_map/pallas_call | solution.py:590
  425.9 2.4 slice.41
  428.3 1.4 dynamic-slice_bitcast_fusion
  429.8 6.9 all-gather.7.cloned.1.call-done
  436.7 0.0 copy-start
  436.7 6.7 all-to-all-start
  443.3 0.0 copy-done
  443.4 1.3 collective-permute-start
  444.7 0.1 slice.39
  444.7 0.8 reshape.136.gate_ref
  445.5 5.5 collective-permute-start.1
  451.0 2.2 collective-permute-start.2
  453.2 85.3 %shard_map.102.part = bf16[8,384,16,128]{3,2,1,0:T(8,128)(2,1)} custom-call(s32[1]{0:T(128)} %bitcast.2.nblk_ref, s32[162]{0:T(256)} %get-tuple-element.26.be_ref, s32[162]{0:T(256)} %get-tuple-element.27.bb_ref, s32[162]{0:T(256)} %get-tuple-element.28.bn_ref, s32[18560]{0:T(1024)} %concatenate.14.key_ref, ...), custom_call_target="tpu_custom_call", output_to_operand_aliasing={{}: (10, {})} | custom-call | flops 47185920000 | bytes 150994944 | tf_op jit(solution)/shard_map/pallas_call | solution.py:590
  538.5 9.1 %collective-permute-done.h_mid = bf16[384,16,128]{2,1,0:T(8,128)(2,1)S(1)} collective-permute-done((bf16[384,16,128]{2,1,0:T(8,128)(2,1)S(1)}, bf16[384,16,128]{2,1,0:T(8,128)(2,1)S(1)}, u32[]{:S(2)}, u32[]{:S(2)}) %collective-permute-start) | collective-permute-done | bytes 1572896 | tf_op jit(solution)/shard_map/ppermute | solution.py:930
  547.7 0.0 copy-start.1
  547.7 0.0 collective-permute-done.1.raw_here
  547.7 0.0 collective-permute-done.2.raw_cross
  547.7 0.0 all-to-all-done.first_hbm
  547.7 1.1 copy-done.1
  548.8 165.7 %shard_map.103 = bf16[4,128,2048]{2,1,0:T(8,128)(2,1)} custom-call(bf16[8,384,16,128]{3,2,1,0:T(8,128)(2,1)} %shard_map.102.part, bf16[384,16,128]{2,1,0:T(8,128)(2,1)} %get-tuple-element.36.h_ref, bf16[384,16,128]{2,1,0:T(8,128)(2,1)} %copy-done.1, bf16[2,96,16,128]{3,2,1,0:T(8,128)(2,1)} %collective-permute-done.1.raw_here, ...), custom_call_target="tpu_custom_call" | custom-call | tf_op jit(solution)/shard_map/pallas_call | solution.py:851
  714.5 3.2 copy.20
  (8 shorter events, 0.1 us)
Async XLA Ops:
  6.5 338.9 %all-gather.5.cloned.1.call-start = ((), (), s32[]{:S(2)}) async-start(), calls=%async_computation.1 | async-start | bytes 8478720 | tf_op jit(solution)/shard_map/all_gather | solution.py:915
  267.2 169.5 %all-gather.7.cloned.1.call-start = ((), (), s32[]{:S(2)}) async-start(), calls=%async_computation.2 | async-start | bytes 10616832 | tf_op jit(solution)/shard_map/all_gather | solution.py:925
  436.7 6.7 copy-start
  436.7 111.0 %all-to-all-start = ((bf16[8,128,16,128]{3,2,1,0:T(8,128)(2,1)}), bf16[8,128,16,128]{3,2,1,0:T(8,128)(2,1)}, u32[]{:S(2)}, u32[]{:S(2)}) async-start(bf16[8,128,16,128]{3,2,1,0:T(8,128)(2,1)} %get-tuple-element.39), calls=%async_computation | async-start | bytes 8388608 | tf_op jit(solution)/shard_map/all_to_all | solution.py:931
  443.4 104.3 %collective-permute-start = (bf16[384,16,128]{2,1,0:T(8,128)(2,1)S(1)}, bf16[384,16,128]{2,1,0:T(8,128)(2,1)S(1)}, u32[]{:S(2)}, u32[]{:S(2)}) collective-permute-start(bf16[384,16,128]{2,1,0:T(8,128)(2,1)S(1)} %copy-done), channel_id=1, source_target_pairs={{2,0},{3,1},{4,6},{5,7},{10,8},{11,9},{12,14},{13,15},{18,16},{19,... | collective-permute-start | bytes 4718600 | tf_op jit(solution)/shard_map/ppermute | solution.py:930
  445.5 102.1 %collective-permute-start.1 = (bf16[2,96,16,128]{3,2,1,0:T(8,128)(2,1)}, bf16[2,96,16,128]{3,2,1,0:T(8,128)(2,1)}, u32[]{:S(2)}, u32[]{:S(2)}) collective-permute-start(bf16[2,96,16,128]{3,2,1,0:T(8,128)(2,1)} %get-tuple-element.37), channel_id=1, source_target_pairs={{0,2},{1,3},{6,4},{7,5},{8,10},{9,11},{14,12},{15,13},{16,18},{17,... | collective-permute-start | bytes 2359304 | tf_op jit(solution)/shard_map/ppermute | solution.py:928
  451.0 96.6 %collective-permute-start.2 = (bf16[2,96,16,128]{3,2,1,0:T(8,128)(2,1)}, bf16[2,96,16,128]{3,2,1,0:T(8,128)(2,1)}, u32[]{:S(2)}, u32[]{:S(2)}) collective-permute-start(bf16[2,96,16,128]{3,2,1,0:T(8,128)(2,1)} %get-tuple-element.38), channel_id=1, source_target_pairs={{0,3},{1,2},{6,5},{7,4},{8,11},{9,10},{14,13},{15,12},{16,19},{17,... | collective-permute-start | bytes 2359304 | tf_op jit(solution)/shard_map/ppermute | solution.py:929
  547.7 1.1 copy-start.1
Sparse Core Ops, SparseCore 0:
  267.3 78.0 all-gather.4
  347.0 89.5 all-gather.6
